TPU v7x, 512 devices: a whole 4x4x16 slice. The times are simulated.
512 devices in a mesh: bead: 16 (over z_lo, core), slab: 32 (over z_hi, x, y).
Axes of the slice: x: 4, y: 4, z: 16 (z_hi: 2, z_lo: 8; z = z_hi * 8 + z_lo), core: 2. Of those that a mesh axis runs over, the one named last changes fastest.
Arguments:
- positions: float32 [64, 3, 32768], P('bead', None, 'slab'), may hold values from -0.4 to 64.4, as said below
- velocities: float32 [64, 3, 32768], P('bead', None, 'slab'), may hold values from -5 to 5
- masses: float32 [32768], P('slab'), may hold values from 1 to 16
- amplitudes: float32 [32768], P('slab'), may hold values from 0.15 to 0.6
- charges: float32 [32768], P('slab'), may hold values from -1.2 to 1.2
Outputs:
- moved: float32 [64, 3, 32768], P('bead', None, 'slab')
- final_velocities: float32 [64, 3, 32768], P('bead', None, 'slab')
Inputs may be any that keep to these rules, and one draw needn't show every extreme that they name: `positions`: atom n's beads lie within 0.4 of its cell: plane n // 512 spans first coordinates from its index to its index plus one, and cell (n % 512) // 128 = 2 a + e of that plane spans second coordinates a to a + 1 and third coordinates e to e + 1.
All inputs are finite; a program needn't handle non-finite values.
Results may differ from a plain program's by a relative error of at most 0.0003.
Values sent between devices are 32-bit elements; how exact they have to be, the bound alone decides.
No kernel may reach another device: no remote copies, remote signals or barrier semaphores. Data moves between devices by JAX's collectives and lax.ppermute only.
A program may use at most 64 MiB of HBM per device.

v0:
```python
import math

import jax
import jax.numpy as jnp
import numpy as np
from jax import lax
from jax.experimental import pallas as pl
from jax.experimental.pallas import tpu as pltpu
from jax.sharding import Mesh, PartitionSpec as P


TIME_STEP = 0.05
OUTER_STEP = 0.1
SPRING = 25.0
NEAR = 4.0
FAR = 2.0
BEADS = 64
CBEADS = 16
SLABS = 32
MINE = BEADS // CBEADS
STEP = 256
WIDTH = 256
AHEAD = 4

X_ROWS = 0
V_ROWS = 96
M_ROW = 192
A_ROW = 200
Q_ROW = 208
PACKED = 216
WIDE = 72

AXES = ("z2", "z1", "z0", "core", "zh", "x1", "x0", "y1", "y0")
TEAM = ("x0", "y1", "y0", "core")
f32 = jnp.float32
bf16 = jnp.bfloat16


def _place():
    ring = [(0, z) for z in range(16)] + [(1, z) for z in range(15, -1, -1)]
    cycle = [(0, 0), (0, 1), (0, 2), (0, 3), (1, 3), (1, 2), (1, 1), (1, 0)]
    device = np.zeros((CBEADS, SLABS), np.int64)
    role = np.zeros((512, 2), np.int64)
    member = np.zeros((2, 16), np.int64)
    half_of = np.zeros(SLABS, np.int64)
    for s in range(SLABS):
        half, z = ring[(s - 8) % SLABS]
        half_of[s] = half
        for b in range(CBEADS):
            q, core = divmod(b, 2)
            xx, y = cycle[q]
            x = xx if half == 0 else 3 - xx
            d = ((z % 8) * 2 + core) * 32 + (z // 8) * 16 + x * 4 + y
            device[b, s] = d
            role[d] = (b, s)
            member[half, (x % 2) * 8 + y * 2 + core] = b
    return device, role, member, half_of


DEVICE, ROLE, MEMBER, HALF = _place()


def _table():
    b = np.arange(BEADS)[None, :] / BEADS
    c = np.arange(CBEADS)[:, None] / CBEADS
    t = 2.0 * np.pi * (b - c)
    total = 1.0 + np.cos(0.5 * CBEADS * t)
    for k in range(1, CBEADS // 2):
        total = total + 2.0 * np.cos(k * t)
    return (total / BEADS).astype(np.float32)


def _settings():
    table = _table()
    out = np.zeros((CBEADS * SLABS, 128), np.float32)
    for d in range(CBEADS * SLABS):
        b, s = ROLE[d]
        out[d, : 16 * MINE] = table[MEMBER[HALF[s]]][:, b * MINE : (b + 1) * MINE].reshape(-1)
        out[d, SLAB_AT] = s
        out[d, CORE_AT] = b % 2
    return out


SLAB_AT = 16 * MINE
CORE_AT = SLAB_AT + 1
SETTINGS = _settings()


def _moves(f):
    return [
        (int(DEVICE[b, s]), int(DEVICE[f(b, s)]))
        for b in range(CBEADS)
        for s in range(SLABS)
    ]


SLAB_UP = _moves(lambda b, s: (b, (s + 1) % SLABS))
SLAB_DOWN = _moves(lambda b, s: (b, (s - 1) % SLABS))
BEAD_SWAP = _moves(lambda b, s: ((b + (1 if b % 2 else -1)) % CBEADS, s))
MOVE_IN = [(b * SLABS + s, int(DEVICE[b, s])) for b in range(CBEADS) for s in range(SLABS)]
MOVE_OUT = [(d, h) for h, d in MOVE_IN]


def pieces(v):
    high = v.astype(bf16).astype(f32)
    rest = v - high
    mid = rest.astype(bf16).astype(f32)
    return high, mid, rest - mid


def halves(lower, upper):
    return jnp.concatenate([lower, upper], axis=0)


def put(ref, row, value):
    ref[pl.ds(row, 8, stride=8), :] = value


def wide(ref):
    return jnp.concatenate([ref[8 * k : 8 * k + 8, :] for k in range(8)], axis=1)


def init_rows(src, tgt):
    ones = jnp.ones((8, 128), f32)
    zeros = jnp.zeros((8, 128), f32)
    put(src, 4, ones)
    put(tgt, 3, ones)
    for k in range(5, 8):
        put(src, k, zeros)
        put(tgt, k, zeros)


def scaled(coords, scale):
    alpha = math.sqrt(scale * math.log2(math.e))
    a = [alpha * y for y in coords]
    return a, -0.5 * (a[0] * a[0] + a[1] * a[1] + a[2] * a[2])


def put_sources(src, qs, lhs, coords, share, scale):
    a, norm = scaled(coords, scale)
    for k, v in enumerate(a + [norm]):
        put(src, k, v)
    for k, v in enumerate([share] + [share * y for y in coords]):
        put(qs, k, v)
        put(qs, 4 + k, v)
    high, mid, low = pieces(wide(src))
    rows = jnp.concatenate([high, high, mid, mid, high, low], axis=0)
    for block in range(8):
        part = slice(128 * block, 128 * block + 128)
        lhs[part, :] = rows[:, part].T.astype(bf16)
    high, mid, low = pieces(wide(qs))
    upper = lax.broadcasted_iota(jnp.int32, (8, 1024), 0) < 4
    return jnp.concatenate([jnp.where(upper, high, mid), jnp.where(upper, low, 0.0)], axis=0).astype(bf16)


def put_targets(tgt, coords, scale):
    a, norm = scaled(coords, scale)
    for k, v in enumerate(a):
        put(tgt, k, v)
    put(tgt, 4, norm)
    high, mid, low = pieces(wide(tgt))
    return jnp.concatenate([high, mid, high, mid, low, high], axis=0).astype(bf16)


def stream(tasks, ahead=AHEAD):
    totals = {}
    ready = []
    for t in range(len(tasks) + ahead):
        if t < len(tasks):
            lhs, first, rhs, q, key = tasks[t]
            ready.append(jnp.dot(lhs[first : first + STEP, :], rhs, preferred_element_type=f32))
        if t < ahead:
            continue
        lhs, first, rhs, q, key = tasks[t - ahead]
        weight = jnp.exp2(ready[t - ahead])
        high = weight.astype(bf16)
        low = (weight - high.astype(f32)).astype(bf16)
        mine = q[:, first : first + STEP]
        part = jnp.dot(mine, high, preferred_element_type=f32)
        part = part + jnp.dot(mine, low, preferred_element_type=f32)
        totals[key] = totals[key] + part if key in totals else part
    return totals


def chunks(lhs, first, last, rhs, start, stop, q, key):
    return [
        (lhs, j, rhs[:, i : i + WIDTH], q, (key, i))
        for j in range(first, last, STEP)
        for i in range(start, stop, WIDTH)
    ]


def joined(totals, key):
    return jnp.concatenate([totals[key, i] for i in range(0, 1024, WIDTH)], axis=1)


def sums_of(total, rows):
    r = total[0:8]
    r = r + jnp.concatenate([r[4:8], r[0:4]], axis=0) + total[8:16]
    for block in range(8):
        rows[8 * block : 8 * block + 8, :] = r[:, 128 * block : 128 * block + 128]
    return [rows[pl.ds(k, 8, stride=8), :] for k in range(4)]


def field(coords, sums, share, scale):
    return [share * scale * (coords[k] * sums[0] - sums[1 + k]) for k in range(3)]


def slot(scr, i):
    return scr[5 * i : 5 * i + 5]


SCRATCH = 2 * [
    pltpu.VMEM((64, 128), f32),
    pltpu.VMEM((64, 128), f32),
    pltpu.VMEM((64, 128), f32),
    pltpu.VMEM((1024, 48), bf16),
    pltpu.VMEM((64, 128), f32),
]


def bead_at(ref, b):
    return [ref[pl.ds(24 * b + 8 * k, 8), :] for k in range(3)]


def near_own_kernel(y_ref, p_ref, out_ref, *scr):
    share = p_ref[A_ROW : A_ROW + 8, :]
    for i in range(2):
        init_rows(*slot(scr, i)[:2])

    def two(i, carry):
        tasks = []
        for j in range(2):
            src, tgt, qs, lhs, _ = slot(scr, j)
            coords = bead_at(y_ref, 2 * i + j)
            q = put_sources(src, qs, lhs, coords, share, NEAR)
            rhs = put_targets(tgt, coords, NEAR)
            tasks += chunks(lhs, 0, 1024, rhs, 0, 1024, q, j)
        totals = stream(tasks)
        for j in range(2):
            for k, r in enumerate(sums_of(joined(totals, j), slot(scr, j)[4])):
                out_ref[pl.ds(64 * i + 32 * j + 8 * k, 8), :] = r
        return carry

    lax.fori_loop(0, MINE // 2, two, 0)


def emit(y_refs, up_ref, down_ref, inner_ref, outer_ref, core):
    for i in range(12):
        y = y_refs[8 * i : 8 * i + 8, :]
        down_ref[4 * i : 4 * i + 4, :] = y[0:4]
        up_ref[4 * i : 4 * i + 4, :] = y[4:8]
    first = y_refs[0:24, :]
    last = y_refs[72:96, :]
    odd = core > 0.5
    inner_ref[...] = jnp.where(odd, first, last)
    outer_ref[...] = jnp.where(odd, last, first)


def emit_partial(y_refs, cols_ref, part_ref):
    y = [y_refs[24 * b : 24 * b + 24, :] for b in range(MINE)]
    for r in range(16):
        total = cols_ref[0, MINE * r] * y[0]
        for b in range(1, MINE):
            total = total + cols_ref[0, MINE * r + b] * y[b]
        part_ref[24 * r : 24 * r + 24, :] = total


def pack_kernel(x_ref, v_ref, m_ref, a_ref, q_ref, out_ref):
    for base, ref in ((X_ROWS, x_ref), (V_ROWS, v_ref)):
        for k in range(3):
            for block in range(8):
                row = base + 8 * k + block
                out_ref[pl.ds(row, 4, stride=24), :] = ref[k, :, 128 * block : 128 * block + 128]
    out_ref[M_ROW : M_ROW + 8, :] = m_ref[...]
    out_ref[A_ROW : A_ROW + 8, :] = a_ref[...]
    out_ref[Q_ROW : Q_ROW + 8, :] = q_ref[...]


def unpack(value_ref, out_ref):
    for k in range(3):
        for block in range(8):
            out_ref[k, :, 128 * block : 128 * block + 128] = value_ref[pl.ds(8 * k + block, 4, stride=24), :]


def start_kernel(cols_ref, p_ref, y_ref, up_ref, down_ref, inner_ref, outer_ref, part_ref):
    centre = 2.0 * cols_ref[0, SLAB_AT] + 1.0
    for b in range(MINE):
        for k in range(3):
            i = 8 * (3 * b + k)
            y_ref[i : i + 8, :] = p_ref[i : i + 8, :] - (centre if k == 0 else 1.0)
    emit(y_ref, up_ref, down_ref, inner_ref, outer_ref, cols_ref[0, CORE_AT])
    emit_partial(y_ref, cols_ref, part_ref)


def near_halo_body(rate, cols_ref, p_ref, y_ref, v_ref, r_ref, left, right, wide_l, wide_r, inner, outer, store, scr):
    chain = scr[10]
    for i in range(2):
        init_rows(*slot(scr, i)[:2])
    own = p_ref[A_ROW : A_ROW + 8, :]
    mass = p_ref[M_ROW : M_ROW + 8, :]
    inverse = 1.0 / mass
    share = halves(wide_l[WIDE + 4 : WIDE + 8, :], wide_r[WIDE : WIDE + 4, :])
    odd = cols_ref[0, CORE_AT] > 0.5
    from_pair = jnp.where(odd, inner[0:24, :], inner[24:48, :])
    chain[0:24, :] = jnp.where(odd, from_pair, outer[...])
    chain[24:120, :] = y_ref[...]
    chain[120:144, :] = jnp.where(odd, outer[...], from_pair)
    shift = jnp.where(lax.broadcasted_iota(jnp.int32, (8, 128), 0) < 4, -2.0, 2.0).astype(f32)

    def two(i, carry):
        at = pl.multiple_of(48 * i, 8)
        lows = left[pl.ds(pl.multiple_of(24 * i, 8), 24), :]
        highs = right[pl.ds(pl.multiple_of(24 * i, 8), 24), :]
        tasks = []
        places = []
        for j in range(2):
            src, tgt, qs, lhs, _ = slot(scr, j)
            coords = [y_ref[pl.ds(at + 24 * j + 8 * k, 8), :] for k in range(3)]
            far = []
            for k in range(3):
                h = 12 * j + 4 * k
                far.append(halves(lows[h : h + 4], highs[h : h + 4]))
            far[0] = far[0] + shift
            q = put_sources(src, qs, lhs, far, share, NEAR)
            rhs = put_targets(tgt, coords, NEAR)
            tasks += chunks(lhs, 0, 512, rhs, 0, 512, q, j)
            tasks += chunks(lhs, 512, 1024, rhs, 512, 1024, q, j)
            places.append(coords)
        totals = stream(tasks)
        for j in range(2):
            coords = places[j]
            sums = sums_of(joined(totals, j), slot(scr, j)[4])
            mine = pl.multiple_of(64 * i, 8) + 32 * j
            sums = [s + r_ref[pl.ds(mine + 8 * k, 8), :] for k, s in enumerate(sums)]
            force = field(coords, sums, own, NEAR)
            for k in range(3):
                r = at + 24 * j + 8 * k
                spring = 2.0 * coords[k] - chain[pl.ds(r, 8), :] - chain[pl.ds(r + 48, 8), :]
                total = force[k] - SPRING * mass * spring
                store(r, coords[k], v_ref[pl.ds(V_AT(v_ref) + r, 8), :] + rate * total * inverse)
        return carry

    lax.fori_loop(0, MINE // 2, two, 0)


def V_AT(ref):
    return V_ROWS if ref.shape[0] == PACKED else 0


def near_slow_kernel(rate, cols_ref, p_ref, y_ref, v_ref, r_ref, left, right, wide_l, wide_r, inner, outer, vo_ref, *scr):
    def store(r, y, v):
        vo_ref[pl.ds(r, 8), :] = v

    near_halo_body(rate, cols_ref, p_ref, y_ref, v_ref, r_ref, left, right, wide_l, wide_r, inner, outer, store, scr)


def near_fast_kernel(last, cols_ref, p_ref, y_ref, v_ref, r_ref, left, right, wide_l, wide_r, inner, outer, *rest):
    if last:
        first_ref, vo_ref, yo_ref, up_ref, down_ref, in_ref, ou_ref, part_ref, moved_ref = rest[:9]
        scr = rest[9:]
    else:
        vo_ref, yo_ref, up_ref, down_ref, in_ref, ou_ref, part_ref = rest[:7]
        scr = rest[7:]

    def store(r, y, v):
        vo_ref[pl.ds(r, 8), :] = v
        yo_ref[pl.ds(r, 8), :] = y + TIME_STEP * v

    near_halo_body(TIME_STEP, cols_ref, p_ref, y_ref, v_ref, r_ref, left, right, wide_l, wide_r, inner, outer, store, scr)
    emit(yo_ref, up_ref, down_ref, in_ref, ou_ref, cols_ref[0, CORE_AT])
    emit_partial(yo_ref, cols_ref, part_ref)
    if last:
        rows = scr[-1]
        rows[...] = yo_ref[...] - first_ref[...]
        unpack(rows, moved_ref)


def gather_kernel(wide, recv_ref, up_ref, down_ref, p_ref, yc_ref, up_out, down_out):
    total = recv_ref[0:24, :]
    for r in range(1, 16):
        total = total + recv_ref[24 * r : 24 * r + 24, :]
    yc_ref[...] = total
    for out, ref in ((up_out, up_ref), (down_out, down_ref)):
        out[0:48, :] = ref[...]
        out[48:72, :] = total
        if wide:
            out[WIDE : WIDE + 16, :] = p_ref[A_ROW : A_ROW + 16, :]


def far_own_kernel(yc_ref, p_ref, out_ref, src, tgt, qs, lhs, rows):
    init_rows(src, tgt)
    coords = bead_at(yc_ref, 0)
    q = put_sources(src, qs, lhs, coords, p_ref[Q_ROW : Q_ROW + 8, :], FAR)
    rhs = put_targets(tgt, coords, FAR)
    total = joined(stream(chunks(lhs, 0, 1024, rhs, 0, 1024, q, 0)), 0)
    for k, r in enumerate(sums_of(total, rows)):
        out_ref[8 * k : 8 * k + 8, :] = r


def far_halo_kernel(yc_ref, p_ref, r_ref, left, right, wide_l, wide_r, out_ref, *scr):
    coords = bead_at(yc_ref, 0)
    tasks = []
    for i, (block, rows) in enumerate(((left, wide_l), (right, wide_r))):
        src, tgt, qs, lhs, _ = slot(scr, i)
        init_rows(src, tgt)
        if i == 0:
            rhs = put_targets(tgt, coords, FAR)
        there = [block[48 + 8 * k : 56 + 8 * k, :] for k in range(3)]
        there[0] = there[0] + (2.0 if i else -2.0)
        q = put_sources(src, qs, lhs, there, rows[WIDE + 8 : WIDE + 16, :], FAR)
        if i == 0:
            tasks += chunks(lhs, 0, 512, rhs, 0, 512, q, 0)
            tasks += chunks(lhs, 512, 1024, rhs, 0, 1024, q, 0)
        else:
            tasks += chunks(lhs, 0, 512, rhs, 0, 1024, q, 0)
            tasks += chunks(lhs, 512, 1024, rhs, 512, 1024, q, 0)
    totals = stream(tasks)
    total = joined(totals, 0)
    sums = [s + r_ref[8 * k : 8 * k + 8, :] for k, s in enumerate(sums_of(total, slot(scr, 0)[4]))]
    force = field(coords, sums, p_ref[Q_ROW : Q_ROW + 8, :], FAR)
    for r in range(16):
        for k in range(3):
            out_ref[24 * r + 8 * k : 24 * r + 8 * k + 8, :] = force[k]


def kick(rate, cols_ref, p_ref, v_ref, far_ref):
    inverse = (rate * BEADS / CBEADS) / p_ref[M_ROW : M_ROW + 8, :]
    inverse = jnp.concatenate([inverse] * 3, axis=0)
    out = []
    far = [far_ref[24 * r : 24 * r + 24, :] for r in range(16)]
    for b in range(MINE):
        total = cols_ref[0, b] * far[0]
        for r in range(1, 16):
            total = total + cols_ref[0, MINE * r + b] * far[r]
        out.append(v_ref[24 * b : 24 * b + 24, :] + inverse * total)
    return out


def update_kernel(rate, cols_ref, p_ref, y_ref, v_ref, far_ref, vo_ref, yo_ref, up_ref, down_ref, in_ref, ou_ref):
    for b, v in enumerate(kick(rate, cols_ref, p_ref, v_ref, far_ref)):
        vo_ref[24 * b : 24 * b + 24, :] = v
        yo_ref[24 * b : 24 * b + 24, :] = y_ref[24 * b : 24 * b + 24, :] + TIME_STEP * v
    emit(yo_ref, up_ref, down_ref, in_ref, ou_ref, cols_ref[0, CORE_AT])


def final_kernel(rate, cols_ref, p_ref, v_ref, far_ref, out_ref, rows):
    for b, v in enumerate(kick(rate, cols_ref, p_ref, v_ref, far_ref)):
        rows[24 * b : 24 * b + 24, :] = v
    unpack(rows, out_ref)


def call(kernel, outs, cols, args, scratch=(), flops=1000, order=(), passed=()):
    specs = [] if cols is None else [pl.BlockSpec(memory_space=pltpu.SMEM)]
    specs += [pl.BlockSpec(memory_space=pltpu.VMEM)] * len(args)
    used = len(specs)
    specs += [pl.BlockSpec(memory_space=pl.ANY)] * (len(order) + len(passed))
    given = ([] if cols is None else [cols]) + list(args) + list(order) + list(passed)
    base = used + len(order)

    def body(*refs):
        kernel(*refs[:used], *refs[len(given) : len(given) + len(outs)], *refs[len(given) + len(outs) + len(passed) :])

    shapes = [jax.ShapeDtypeStruct(s, f32) for s in outs] + [jax.ShapeDtypeStruct(x.shape, f32) for x in passed]
    return pl.pallas_call(
        body,
        out_shape=shapes,
        in_specs=specs,
        out_specs=[pl.BlockSpec(memory_space=pltpu.VMEM)] * len(outs) + [pl.BlockSpec(memory_space=pl.ANY)] * len(passed),
        scratch_shapes=list(scratch),
        input_output_aliases={base + i: len(outs) + i for i in range(len(passed))},
        cost_estimate=pl.CostEstimate(flops=flops, bytes_accessed=400000, transcendentals=0),
        compiler_params=pltpu.CompilerParams(vmem_limit_bytes=12 * 1024 * 1024),
    )(*given)


HALO = (48, 128)
BEAD = (24, 128)
STATE = (96, 128)
TEAM_ROWS = (16, 24, 128)
PLAIN = (3, 4, 1024)


def exchange_team(x):
    x = lax.all_to_all(x.reshape(TEAM_ROWS), TEAM, split_axis=0, concat_axis=0, tiled=True)
    return x.reshape(384, 128)


def send(x, moves):
    return lax.ppermute(x, AXES, moves)


def pair(x):
    return lax.all_gather(x, "core", axis=0, tiled=True)


CHAIN = pltpu.VMEM((144, 128), f32)


def shards(positions, velocities, masses, amplitudes, charges):
    (packed,) = call(
        pack_kernel,
        [(PACKED, 128)],
        None,
        [
            jnp.transpose(positions, (1, 0, 2)),
            jnp.transpose(velocities, (1, 0, 2)),
            masses.reshape(8, 128),
            amplitudes.reshape(8, 128),
            charges.reshape(8, 128),
        ],
    )
    p = lax.ppermute(packed, AXES, MOVE_IN)
    cols = lax.dynamic_slice_in_dim(jnp.asarray(SETTINGS), lax.axis_index(AXES), 1, 0)

    y, up, down, inner, outer, part = call(start_kernel, [STATE, HALO, HALO, BEAD, BEAD, (384, 128)], cols, [p])
    first = y
    v = p
    wide_l = wide_r = None
    big = 400_000_000
    for stage in range(5):
        slow = stage % 2 == 0
        if not slow:
            left = send(up, SLAB_UP)
            right = send(down, SLAB_DOWN)
            outer = send(outer, BEAD_SWAP)
            inner = pair(inner)
            (sums,) = call(near_own_kernel, [(128, 128)], None, [y, p], SCRATCH, big)
            last = stage == 3

            def near_fast(*refs, last=last):
                near_fast_kernel(last, *refs)

            result = call(
                near_fast,
                [STATE, STATE, HALO, HALO, BEAD, BEAD, (384, 128)] + [PLAIN] * last,
                cols,
                [p, y, v, sums, left, right, wide_l, wide_r, inner, outer] + [first] * last,
                SCRATCH + [CHAIN] + [pltpu.VMEM(STATE, f32)] * last,
                big // 2,
            )
            v, y, up, down, inner, outer, part = result[:7]
            if last:
                moved = result[7]
            continue
        edge = stage in (0, 4)
        got = exchange_team(part)
        inner = pair(inner)
        (sums,) = call(near_own_kernel, [(128, 128)], None, [y, p], SCRATCH, big)

        def gather(*refs, wide=stage == 0):
            gather_kernel(wide, *refs)

        size = (WIDE + 16 * (stage == 0), 128)
        yc, up, down, outer = call(gather, [BEAD, size, size], None, [got, up, down, p], order=[sums], passed=[outer])
        left = send(up, SLAB_UP)
        right = send(down, SLAB_DOWN)
        outer = send(outer, BEAD_SWAP)
        if stage == 0:
            wide_l, wide_r = left, right
        (far_sums,) = call(far_own_kernel, [(32, 128)], None, [yc, p], SCRATCH[:5], big // 4)
        (copies,) = call(
            far_halo_kernel, [(384, 128)], None, [yc, p, far_sums, left, right, wide_l, wide_r], SCRATCH, big // 4
        )
        far = exchange_team(copies)
        rate = TIME_STEP * (0.5 if edge else 1.0)

        def near_slow(*refs, rate=rate):
            near_slow_kernel(rate, *refs)

        (v,) = call(
            near_slow,
            [STATE],
            cols,
            [p, y, v, sums, left, right, wide_l, wide_r, inner, outer],
            SCRATCH + [CHAIN],
            big // 2,
        )
        rate = OUTER_STEP * (0.5 if edge else 1.0)
        if stage == 4:

            def final(*refs, rate=rate):
                final_kernel(rate, *refs)

            (v,) = call(final, [PLAIN], cols, [p, v, far], [pltpu.VMEM(STATE, f32)])
        else:

            def update(*refs, rate=rate):
                update_kernel(rate, *refs)

            v, y, up, down, inner, outer = call(update, [STATE, STATE, HALO, HALO, BEAD, BEAD], cols, [p, y, v, far])
    moved = lax.ppermute(moved, AXES, MOVE_OUT)
    speeds = lax.ppermute(v, AXES, MOVE_OUT)
    return jnp.transpose(moved, (1, 0, 2)), jnp.transpose(speeds, (1, 0, 2))


def solution(mesh):
    fine = Mesh(mesh.devices.reshape((2,) * 9), AXES)
    bead = ("z2", "z1", "z0", "core")
    slab = ("zh", "x1", "x0", "y1", "y0")
    wide = P(bead, None, slab)
    flat = P(slab)
    return jax.shard_map(
        shards,
        mesh=fine,
        in_specs=(wide, wide, flat, flat, flat),
        out_specs=(wide, wide),
        check_vma=False,
    )
```

profile of v0, /device:TPU:30, one launch (start us, length us, event | category | flops | bytes accessed | tf_op | source)
XLA Modules:
  0.0 206.6 jit_solution(4292299768941705187)
XLA Ops:
  0.7 0.7 copy-done.3
  1.3 0.0 copy-done.2
  1.3 0.8 copy-done
  2.1 0.8 copy-done.1
  2.9 0.7 copy-done.4
  3.6 12.7 %collective-permute-start = (f32[216,128]{1,0:T(8,128)S(1)}, f32[216,128]{1,0:T(8,128)S(1)}, u32[]{:S(2)}, u32[]{:S(2)}) collective-permute-start(f32[216,128]{1,0:T(8,128)S(1)} %shard_map.77), channel_id=1, source_target_pairs={{0,460},{1,396},{2,332},{3,268},{4,204},{5,140},{6,76},{7,12},{8,0... | collective-permute-start | bytes 331784 | tf_op jit(solution)/shard_map/ppermute | solution.py:513
  16.4 0.7 constant_dynamic-slice_fusion.refs_0_
  17.1 7.2 %collective-permute-done.refs_1_.refs_3_ = f32[216,128]{1,0:T(8,128)S(1)} collective-permute-done((f32[216,128]{1,0:T(8,128)S(1)}, f32[216,128]{1,0:T(8,128)S(1)}, u32[]{:S(2)}, u32[]{:S(2)}) %collective-permute-start) | collective-permute-done | bytes 110624 | tf_op jit(solution)/shard_map/ppermute | solution.py:513
  24.3 1.3 shard_map.78
  25.6 9.1 %all-to-all-start = ((f32[16,24,128]{2,1,0:T(8,128)}), f32[16,24,128]{2,1,0:T(8,128)S(1)}, u32[]{:S(2)}, u32[]{:S(2)}) async-start(f32[16,24,128]{2,1,0:T(8,128)} %bitcast.5), calls=%async_computation | async-start | bytes 393216 | tf_op jit(solution)/shard_map/all_to_all | solution.py:485
  34.7 4.3 %shard_map.79.refs_4_ = f32[128,128]{1,0:T(8,128)S(1)} custom-call(f32[96,128]{1,0:T(8,128)S(1)} %get-tuple-element.47.refs_0_.refs_2_.refs_11_, f32[216,128]{1,0:T(8,128)S(1)} %collective-permute-done.refs_1_.refs_3_), custom_call_target="tpu_custom_call" | custom-call | flops 400000000 | bytes 400000 | tf_op jit(solution)/shard_map/pallas_call | solution.py:465
  39.0 2.4 %collective-permute-start.1 = (f32[88,128]{1,0:T(8,128)S(1)}, f32[88,128]{1,0:T(8,128)S(1)}, u32[]{:S(2)}, u32[]{:S(2)}) collective-permute-start(f32[88,128]{1,0:T(8,128)S(1)} %get-tuple-element.52), channel_id=1, source_target_pairs={{460,396},{396,332},{332,268},{268,204},{204,140},{140,76},{76,12}... | collective-permute-start | bytes 135176 | tf_op jit(solution)/shard_map/ppermute | solution.py:490
  41.4 3.4 %collective-permute-start.2 = (f32[88,128]{1,0:T(8,128)S(1)}, f32[88,128]{1,0:T(8,128)S(1)}, u32[]{:S(2)}, u32[]{:S(2)}) collective-permute-start(f32[88,128]{1,0:T(8,128)S(1)} %get-tuple-element.53), channel_id=1, source_target_pairs={{460,28},{396,460},{332,396},{268,332},{204,268},{140,204},{76,140... | collective-permute-start | bytes 135176 | tf_op jit(solution)/shard_map/ppermute | solution.py:490
  44.8 1.2 shard_map.82.refs_2_
  46.1 2.5 %collective-permute-done.2.refs_6_.refs_8_.refs_4_ = f32[88,128]{1,0:T(8,128)S(1)} collective-permute-done((f32[88,128]{1,0:T(8,128)S(1)}, f32[88,128]{1,0:T(8,128)S(1)}, u32[]{:S(2)}, u32[]{:S(2)}) %collective-permute-start.2) | collective-permute-done | bytes 45088 | tf_op jit(solution)/shard_map/ppermute | solution.py:490
  48.6 2.4 %shard_map.83 = f32[384,128]{1,0:T(8,128)} custom-call(f32[24,128]{1,0:T(8,128)S(1)} %get-tuple-element.56.refs_0_, f32[216,128]{1,0:T(8,128)S(1)} %collective-permute-done.refs_1_.refs_3_, f32[32,128]{1,0:T(8,128)S(1)} %shard_map.82.refs_2_, f32[88,128]{1,0:T(8,128)S(1)} %collective-permute-done.1.refs_5_.refs_7_.refs_3_, ...), custom_call_target="tpu_custom_call" | custom-call | flops 100000000 | bytes 400000 | tf_op jit(solution)/shard_map/pallas_call | solution.py:465
  51.0 5.4 %all-to-all-start.1 = ((f32[16,24,128]{2,1,0:T(8,128)}), f32[16,24,128]{2,1,0:T(8,128)S(1)}, u32[]{:S(2)}, u32[]{:S(2)}) async-start(f32[16,24,128]{2,1,0:T(8,128)} %bitcast.7), calls=%async_computation.1 | async-start | bytes 393216 | tf_op jit(solution)/shard_map/all_to_all | solution.py:485
  56.4 2.5 %collective-permute-start.3 = (f32[24,128]{1,0:T(8,128)S(1)}, f32[24,128]{1,0:T(8,128)S(1)}, u32[]{:S(2)}, u32[]{:S(2)}) collective-permute-start(f32[24,128]{1,0:T(8,128)S(1)} %get-tuple-element.55), channel_id=1, source_target_pairs={{460,488},{396,424},{332,360},{268,296},{204,232},{140,168},{76,10... | collective-permute-start | bytes 36872 | tf_op jit(solution)/shard_map/ppermute | solution.py:490
  58.9 1.8 all_gather.15.refs_9_
  60.7 0.7 collective-permute-done.3.refs_10_
  61.4 3.1 %shard_map.81.refs_3_ = f32[96,128]{1,0:T(8,128)S(1)} custom-call(f32[1,128]{1,0:T(1,128)S(1)} %constant_dynamic-slice_fusion.refs_0_, f32[216,128]{1,0:T(8,128)S(1)} %collective-permute-done.refs_1_.refs_3_, f32[96,128]{1,0:T(8,128)S(1)} %get-tuple-element.47.refs_0_.refs_2_.refs_11_, f32[216,128]{1,0:T(8,128)S(1)} %collective-permute-done.refs_1_.refs_3_, ...), custom_call_target="tpu_custom_call" | custom-call | flops 200000000 | bytes 400000 | tf_op jit(solution)/shard_map/pallas_call | solution.py:465
  64.5 0.6 shard_map.84
  65.1 2.5 %collective-permute-start.6 = (f32[24,128]{1,0:T(8,128)S(1)}, f32[24,128]{1,0:T(8,128)S(1)}, u32[]{:S(2)}, u32[]{:S(2)}) collective-permute-start(f32[24,128]{1,0:T(8,128)S(1)} %get-tuple-element.62), channel_id=1, source_target_pairs={{460,488},{396,424},{332,360},{268,296},{204,232},{140,168},{76,10... | collective-permute-start | bytes 36872 | tf_op jit(solution)/shard_map/ppermute | solution.py:490
  67.6 1.9 collective-permute-start.4
  69.6 3.9 %collective-permute-start.5 = (f32[48,128]{1,0:T(8,128)S(1)}, f32[48,128]{1,0:T(8,128)S(1)}, u32[]{:S(2)}, u32[]{:S(2)}) collective-permute-start(f32[48,128]{1,0:T(8,128)S(1)} %get-tuple-element.60), channel_id=1, source_target_pairs={{460,28},{396,460},{332,396},{268,332},{204,268},{140,204},{76,140... | collective-permute-start | bytes 73736 | tf_op jit(solution)/shard_map/ppermute | solution.py:490
  73.5 4.3 %shard_map.85.refs_4_ = f32[128,128]{1,0:T(8,128)S(1)} custom-call(f32[96,128]{1,0:T(8,128)S(1)} %get-tuple-element.57.refs_0_.refs_2_, f32[216,128]{1,0:T(8,128)S(1)} %collective-permute-done.refs_1_.refs_3_), custom_call_target="tpu_custom_call" | custom-call | flops 400000000 | bytes 400000 | tf_op jit(solution)/shard_map/pallas_call | solution.py:465
  77.8 1.8 all_gather.16.refs_9_
  79.6 3.9 %shard_map.86 = (f32[96,128]{1,0:T(8,128)S(1)}, f32[96,128]{1,0:T(8,128)S(1)}, f32[48,128]{1,0:T(8,128)S(1)}, f32[48,128]{1,0:T(8,128)S(1)}, f32[24,128]{1,0:T(8...) custom-call(f32[1,128]{1,0:T(1,128)S(1)} %constant_dynamic-slice_fusion.refs_0_, ...), custom_call_target="tpu_custom_call" | custom-call | flops 200000000 | bytes 400000 | tf_op jit(solution)/shard_map/pallas_call | solution.py:465
  83.5 5.6 %all-to-all-start.2 = ((f32[16,24,128]{2,1,0:T(8,128)}), f32[16,24,128]{2,1,0:T(8,128)S(1)}, u32[]{:S(2)}, u32[]{:S(2)}) async-start(f32[16,24,128]{2,1,0:T(8,128)} %bitcast.9), calls=%async_computation.2 | async-start | bytes 393216 | tf_op jit(solution)/shard_map/all_to_all | solution.py:485
  89.1 4.2 %shard_map.87.refs_4_ = f32[128,128]{1,0:T(8,128)S(1)} custom-call(f32[96,128]{1,0:T(8,128)S(1)} %get-tuple-element.63.refs_0_.refs_2_, f32[216,128]{1,0:T(8,128)S(1)} %collective-permute-done.refs_1_.refs_3_), custom_call_target="tpu_custom_call" | custom-call | flops 400000000 | bytes 400000 | tf_op jit(solution)/shard_map/pallas_call | solution.py:465
  93.4 3.2 %collective-permute-start.7 = (f32[72,128]{1,0:T(8,128)S(1)}, f32[72,128]{1,0:T(8,128)S(1)}, u32[]{:S(2)}, u32[]{:S(2)}) collective-permute-start(f32[72,128]{1,0:T(8,128)S(1)} %get-tuple-element.69), channel_id=1, source_target_pairs={{460,396},{396,332},{332,268},{268,204},{204,140},{140,76},{76,12}... | collective-permute-start | bytes 110600 | tf_op jit(solution)/shard_map/ppermute | solution.py:490
  96.6 2.6 %collective-permute-start.8 = (f32[72,128]{1,0:T(8,128)S(1)}, f32[72,128]{1,0:T(8,128)S(1)}, u32[]{:S(2)}, u32[]{:S(2)}) collective-permute-start(f32[72,128]{1,0:T(8,128)S(1)} %get-tuple-element.70), channel_id=1, source_target_pairs={{460,28},{396,460},{332,396},{268,332},{204,268},{140,204},{76,140... | collective-permute-start | bytes 110600 | tf_op jit(solution)/shard_map/ppermute | solution.py:490
  99.2 1.2 shard_map.90.refs_2_
  100.5 3.2 %collective-permute-done.8.refs_6_.refs_4_ = f32[72,128]{1,0:T(8,128)S(1)} collective-permute-done((f32[72,128]{1,0:T(8,128)S(1)}, f32[72,128]{1,0:T(8,128)S(1)}, u32[]{:S(2)}, u32[]{:S(2)}) %collective-permute-start.8) | collective-permute-done | bytes 36896 | tf_op jit(solution)/shard_map/ppermute | solution.py:490
  103.7 2.4 %shard_map.91 = f32[384,128]{1,0:T(8,128)} custom-call(f32[24,128]{1,0:T(8,128)S(1)} %get-tuple-element.73.refs_0_, f32[216,128]{1,0:T(8,128)S(1)} %collective-permute-done.refs_1_.refs_3_, f32[32,128]{1,0:T(8,128)S(1)} %shard_map.90.refs_2_, f32[72,128]{1,0:T(8,128)S(1)} %collective-permute-done.7.refs_5_.refs_3_, ...), custom_call_target="tpu_custom_call" | custom-call | flops 100000000 | bytes 400000 | tf_op jit(solution)/shard_map/pallas_call | solution.py:465
  106.1 5.4 %all-to-all-start.3 = ((f32[16,24,128]{2,1,0:T(8,128)}), f32[16,24,128]{2,1,0:T(8,128)S(1)}, u32[]{:S(2)}, u32[]{:S(2)}) async-start(f32[16,24,128]{2,1,0:T(8,128)} %bitcast.11), calls=%async_computation.3 | async-start | bytes 393216 | tf_op jit(solution)/shard_map/all_to_all | solution.py:485
  111.5 2.5 %collective-permute-start.9 = (f32[24,128]{1,0:T(8,128)S(1)}, f32[24,128]{1,0:T(8,128)S(1)}, u32[]{:S(2)}, u32[]{:S(2)}) collective-permute-start(f32[24,128]{1,0:T(8,128)S(1)} %get-tuple-element.72), channel_id=1, source_target_pairs={{460,488},{396,424},{332,360},{268,296},{204,232},{140,168},{76,10... | collective-permute-start | bytes 36872 | tf_op jit(solution)/shard_map/ppermute | solution.py:490
  114.0 1.8 all_gather.17.refs_9_
  115.8 0.7 collective-permute-done.9.refs_10_
  116.5 3.1 %shard_map.89.refs_3_ = f32[96,128]{1,0:T(8,128)S(1)} custom-call(f32[1,128]{1,0:T(1,128)S(1)} %constant_dynamic-slice_fusion.refs_0_, f32[216,128]{1,0:T(8,128)S(1)} %collective-permute-done.refs_1_.refs_3_, f32[96,128]{1,0:T(8,128)S(1)} %get-tuple-element.63.refs_0_.refs_2_, f32[96,128]{1,0:T(8,128)S(1)} %get-tuple-element.64.refs_3_, ...), custom_call_target="tpu_custom_call" | custom-call | flops 200000000 | bytes 400000 | tf_op jit(solution)/shard_map/pallas_call | solution.py:465
  119.7 0.6 shard_map.92
  120.3 2.5 %collective-permute-start.12 = (f32[24,128]{1,0:T(8,128)S(1)}, f32[24,128]{1,0:T(8,128)S(1)}, u32[]{:S(2)}, u32[]{:S(2)}) collective-permute-start(f32[24,128]{1,0:T(8,128)S(1)} %get-tuple-element.79), channel_id=1, source_target_pairs={{460,488},{396,424},{332,360},{268,296},{204,232},{140,168},{76,10... | collective-permute-start | bytes 36872 | tf_op jit(solution)/shard_map/ppermute | solution.py:490
  122.8 4.0 %collective-permute-start.10 = (f32[48,128]{1,0:T(8,128)S(1)}, f32[48,128]{1,0:T(8,128)S(1)}, u32[]{:S(2)}, u32[]{:S(2)}) collective-permute-start(f32[48,128]{1,0:T(8,128)S(1)} %get-tuple-element.76), channel_id=1, source_target_pairs={{460,396},{396,332},{332,268},{268,204},{204,140},{140,76},{76,12}... | collective-permute-start | bytes 73736 | tf_op jit(solution)/shard_map/ppermute | solution.py:490
  126.8 1.9 collective-permute-start.11
  128.7 4.3 %shard_map.93.refs_4_ = f32[128,128]{1,0:T(8,128)S(1)} custom-call(f32[96,128]{1,0:T(8,128)S(1)} %get-tuple-element.74.refs_0_.refs_2_, f32[216,128]{1,0:T(8,128)S(1)} %collective-permute-done.refs_1_.refs_3_), custom_call_target="tpu_custom_call" | custom-call | flops 400000000 | bytes 400000 | tf_op jit(solution)/shard_map/pallas_call | solution.py:465
  132.9 2.3 %all_gather.18.refs_9_ = f32[48,128]{1,0:T(8,128)S(1)} all-gather(f32[24,128]{1,0:T(8,128)S(1)} %get-tuple-element.78), channel_id=1, replica_groups=mesh['z2'=2,'z1'=2,'z0'=2,'core'=2,'zh'=2,'x1'=2,'x0'=2,'y1'=2,'y0'=2] {..., dimensions={0}, use_global_device_ids=true | all-gather | bytes 36864 | tf_op jit(solution)/shard_map/all_gather | solution.py:494
  135.2 3.9 %shard_map.94 = (f32[96,128]{1,0:T(8,128)S(1)}, f32[96,128]{1,0:T(8,128)S(1)}, f32[48,128]{1,0:T(8,128)S(1)}, f32[48,128]{1,0:T(8,128)S(1)}, f32[24,128]{1,0:T(8...) custom-call(f32[1,128]{1,0:T(1,128)S(1)} %constant_dynamic-slice_fusion.refs_0_, ...), custom_call_target="tpu_custom_call" | custom-call | flops 200000000 | bytes 400000 | tf_op jit(solution)/shard_map/pallas_call | solution.py:465
  139.1 5.4 %all-to-all-start.4 = ((f32[16,24,128]{2,1,0:T(8,128)}), f32[16,24,128]{2,1,0:T(8,128)S(1)}, u32[]{:S(2)}, u32[]{:S(2)}) async-start(f32[16,24,128]{2,1,0:T(8,128)} %bitcast.14), calls=%async_computation.4 | async-start | bytes 393216 | tf_op jit(solution)/shard_map/all_to_all | solution.py:485
  144.5 4.3 %shard_map.95.refs_4_ = f32[128,128]{1,0:T(8,128)S(1)} custom-call(f32[96,128]{1,0:T(8,128)S(1)} %get-tuple-element.81.refs_0_.refs_2_, f32[216,128]{1,0:T(8,128)S(1)} %collective-permute-done.refs_1_.refs_3_), custom_call_target="tpu_custom_call" | custom-call | flops 400000000 | bytes 400000 | tf_op jit(solution)/shard_map/pallas_call | solution.py:465
  148.8 5.0 %collective-permute-start.14 = (f32[72,128]{1,0:T(8,128)S(1)}, f32[72,128]{1,0:T(8,128)S(1)}, u32[]{:S(2)}, u32[]{:S(2)}) collective-permute-start(f32[72,128]{1,0:T(8,128)S(1)} %get-tuple-element.87), channel_id=1, source_target_pairs={{460,396},{396,332},{332,268},{268,204},{204,140},{140,76},{76,12}... | collective-permute-start | bytes 110600 | tf_op jit(solution)/shard_map/ppermute | solution.py:490
  153.8 2.1 %collective-permute-start.15 = (f32[72,128]{1,0:T(8,128)S(1)}, f32[72,128]{1,0:T(8,128)S(1)}, u32[]{:S(2)}, u32[]{:S(2)}) collective-permute-start(f32[72,128]{1,0:T(8,128)S(1)} %get-tuple-element.88), channel_id=1, source_target_pairs={{460,28},{396,460},{332,396},{268,332},{204,268},{140,204},{76,140... | collective-permute-start | bytes 110600 | tf_op jit(solution)/shard_map/ppermute | solution.py:490
  156.0 1.2 shard_map.98.refs_2_
  157.2 3.8 %collective-permute-done.15.refs_6_.refs_4_ = f32[72,128]{1,0:T(8,128)S(1)} collective-permute-done((f32[72,128]{1,0:T(8,128)S(1)}, f32[72,128]{1,0:T(8,128)S(1)}, u32[]{:S(2)}, u32[]{:S(2)}) %collective-permute-start.15) | collective-permute-done | bytes 36896 | tf_op jit(solution)/shard_map/ppermute | solution.py:490
  161.0 2.4 %shard_map.99 = f32[384,128]{1,0:T(8,128)} custom-call(f32[24,128]{1,0:T(8,128)S(1)} %get-tuple-element.91.refs_0_, f32[216,128]{1,0:T(8,128)S(1)} %collective-permute-done.refs_1_.refs_3_, f32[32,128]{1,0:T(8,128)S(1)} %shard_map.98.refs_2_, f32[72,128]{1,0:T(8,128)S(1)} %collective-permute-done.14.refs_5_.refs_3_, ...), custom_call_target="tpu_custom_call" | custom-call | flops 100000000 | bytes 400000 | tf_op jit(solution)/shard_map/pallas_call | solution.py:465
  163.4 5.4 %all-to-all-start.5 = ((f32[16,24,128]{2,1,0:T(8,128)}), f32[16,24,128]{2,1,0:T(8,128)S(1)}, u32[]{:S(2)}, u32[]{:S(2)}) async-start(f32[16,24,128]{2,1,0:T(8,128)} %bitcast.16), calls=%async_computation.5 | async-start | bytes 393216 | tf_op jit(solution)/shard_map/all_to_all | solution.py:485
  168.9 2.5 %collective-permute-start.16 = (f32[24,128]{1,0:T(8,128)S(1)}, f32[24,128]{1,0:T(8,128)S(1)}, u32[]{:S(2)}, u32[]{:S(2)}) collective-permute-start(f32[24,128]{1,0:T(8,128)S(1)} %get-tuple-element.90), channel_id=1, source_target_pairs={{460,488},{396,424},{332,360},{268,296},{204,232},{140,168},{76,10... | collective-permute-start | bytes 36872 | tf_op jit(solution)/shard_map/ppermute | solution.py:490
  171.3 11.6 %collective-permute-start.13 = (f32[3,4,1024]{2,1,0:T(4,128)S(1)}, f32[3,4,1024]{2,1,0:T(4,128)S(1)}, u32[]{:S(2)}, u32[]{:S(2)}) collective-permute-start(f32[3,4,1024]{2,1,0:T(4,128)S(1)} %get-tuple-element.80), channel_id=1, source_target_pairs={{460,0},{396,1},{332,2},{268,3},{204,4},{140,5},{76,6},{12,7},{0,8... | collective-permute-start | bytes 147464 | tf_op jit(solution)/shard_map/ppermute | solution.py:592
  182.9 1.9 all_gather.19.refs_9_
  184.8 3.1 %shard_map.97.refs_2_ = f32[96,128]{1,0:T(8,128)S(1)} custom-call(f32[1,128]{1,0:T(1,128)S(1)} %constant_dynamic-slice_fusion.refs_0_, f32[216,128]{1,0:T(8,128)S(1)} %collective-permute-done.refs_1_.refs_3_, f32[96,128]{1,0:T(8,128)S(1)} %get-tuple-element.81.refs_0_.refs_2_, f32[96,128]{1,0:T(8,128)S(1)} %get-tuple-element.82.refs_3_, ...), custom_call_target="tpu_custom_call" | custom-call | flops 200000000 | bytes 400000 | tf_op jit(solution)/shard_map/pallas_call | solution.py:465
  188.0 0.6 shard_map.100
  188.6 3.2 %collective-permute-start.17 = (f32[3,4,1024]{2,1,0:T(4,128)S(1)}, f32[3,4,1024]{2,1,0:T(4,128)S(1)}, u32[]{:S(2)}, u32[]{:S(2)}) collective-permute-start(f32[3,4,1024]{2,1,0:T(4,128)S(1)} %shard_map.100), channel_id=1, source_target_pairs={{460,0},{396,1},{332,2},{268,3},{204,4},{140,5},{76,6},{12,7},{0,8... | collective-permute-start | bytes 147464 | tf_op jit(solution)/shard_map/ppermute | solution.py:593
  191.8 13.6 %collective-permute-done.17 = f32[3,4,1024]{2,1,0:T(4,128)S(1)} collective-permute-done((f32[3,4,1024]{2,1,0:T(4,128)S(1)}, f32[3,4,1024]{2,1,0:T(4,128)S(1)}, u32[]{:S(2)}, u32[]{:S(2)}) %collective-permute-start.17) | collective-permute-done | bytes 49184 | tf_op jit(solution)/shard_map/ppermute | solution.py:593
  205.4 0.6 copy.16
  206.0 0.6 copy.17
  (26 shorter events, 0.2 us)
Async XLA Ops:
  0.6 0.7 copy-start.3
  0.6 0.7 copy-start.2
  1.3 0.8 copy-start
  2.1 0.8 copy-start.1
  2.9 0.7 copy-start.4
  3.6 20.6 %collective-permute-start = (f32[216,128]{1,0:T(8,128)S(1)}, f32[216,128]{1,0:T(8,128)S(1)}, u32[]{:S(2)}, u32[]{:S(2)}) collective-permute-start(f32[216,128]{1,0:T(8,128)S(1)} %shard_map.77), channel_id=1, source_target_pairs={{0,460},{1,396},{2,332},{3,268},{4,204},{5,140},{6,76},{7,12},{8,0... | collective-permute-start | bytes 331784 | tf_op jit(solution)/shard_map/ppermute | solution.py:513
  25.6 13.4 %all-to-all-start = ((f32[16,24,128]{2,1,0:T(8,128)}), f32[16,24,128]{2,1,0:T(8,128)S(1)}, u32[]{:S(2)}, u32[]{:S(2)}) async-start(f32[16,24,128]{2,1,0:T(8,128)} %bitcast.5), calls=%async_computation | async-start | bytes 393216 | tf_op jit(solution)/shard_map/all_to_all | solution.py:485
  39.0 7.1 %collective-permute-start.1 = (f32[88,128]{1,0:T(8,128)S(1)}, f32[88,128]{1,0:T(8,128)S(1)}, u32[]{:S(2)}, u32[]{:S(2)}) collective-permute-start(f32[88,128]{1,0:T(8,128)S(1)} %get-tuple-element.52), channel_id=1, source_target_pairs={{460,396},{396,332},{332,268},{268,204},{204,140},{140,76},{76,12}... | collective-permute-start | bytes 135176 | tf_op jit(solution)/shard_map/ppermute | solution.py:490
  41.4 7.2 %collective-permute-start.2 = (f32[88,128]{1,0:T(8,128)S(1)}, f32[88,128]{1,0:T(8,128)S(1)}, u32[]{:S(2)}, u32[]{:S(2)}) collective-permute-start(f32[88,128]{1,0:T(8,128)S(1)} %get-tuple-element.53), channel_id=1, source_target_pairs={{460,28},{396,460},{332,396},{268,332},{204,268},{140,204},{76,140... | collective-permute-start | bytes 135176 | tf_op jit(solution)/shard_map/ppermute | solution.py:490
  51.0 13.5 %all-to-all-start.1 = ((f32[16,24,128]{2,1,0:T(8,128)}), f32[16,24,128]{2,1,0:T(8,128)S(1)}, u32[]{:S(2)}, u32[]{:S(2)}) async-start(f32[16,24,128]{2,1,0:T(8,128)} %bitcast.7), calls=%async_computation.1 | async-start | bytes 393216 | tf_op jit(solution)/shard_map/all_to_all | solution.py:485
  56.4 5.0 %collective-permute-start.3 = (f32[24,128]{1,0:T(8,128)S(1)}, f32[24,128]{1,0:T(8,128)S(1)}, u32[]{:S(2)}, u32[]{:S(2)}) collective-permute-start(f32[24,128]{1,0:T(8,128)S(1)} %get-tuple-element.55), channel_id=1, source_target_pairs={{460,488},{396,424},{332,360},{268,296},{204,232},{140,168},{76,10... | collective-permute-start | bytes 36872 | tf_op jit(solution)/shard_map/ppermute | solution.py:490
  65.1 14.4 %collective-permute-start.6 = (f32[24,128]{1,0:T(8,128)S(1)}, f32[24,128]{1,0:T(8,128)S(1)}, u32[]{:S(2)}, u32[]{:S(2)}) collective-permute-start(f32[24,128]{1,0:T(8,128)S(1)} %get-tuple-element.62), channel_id=1, source_target_pairs={{460,488},{396,424},{332,360},{268,296},{204,232},{140,168},{76,10... | collective-permute-start | bytes 36872 | tf_op jit(solution)/shard_map/ppermute | solution.py:490
  67.6 11.9 %collective-permute-start.4 = (f32[48,128]{1,0:T(8,128)S(1)}, f32[48,128]{1,0:T(8,128)S(1)}, u32[]{:S(2)}, u32[]{:S(2)}) collective-permute-start(f32[48,128]{1,0:T(8,128)S(1)} %get-tuple-element.59), channel_id=1, source_target_pairs={{460,396},{396,332},{332,268},{268,204},{204,140},{140,76},{76,12}... | collective-permute-start | bytes 73736 | tf_op jit(solution)/shard_map/ppermute | solution.py:490
  69.6 10.0 %collective-permute-start.5 = (f32[48,128]{1,0:T(8,128)S(1)}, f32[48,128]{1,0:T(8,128)S(1)}, u32[]{:S(2)}, u32[]{:S(2)}) collective-permute-start(f32[48,128]{1,0:T(8,128)S(1)} %get-tuple-element.60), channel_id=1, source_target_pairs={{460,28},{396,460},{332,396},{268,332},{204,268},{140,204},{76,140... | collective-permute-start | bytes 73736 | tf_op jit(solution)/shard_map/ppermute | solution.py:490
  83.5 9.9 %all-to-all-start.2 = ((f32[16,24,128]{2,1,0:T(8,128)}), f32[16,24,128]{2,1,0:T(8,128)S(1)}, u32[]{:S(2)}, u32[]{:S(2)}) async-start(f32[16,24,128]{2,1,0:T(8,128)} %bitcast.9), calls=%async_computation.2 | async-start | bytes 393216 | tf_op jit(solution)/shard_map/all_to_all | solution.py:485
  93.4 7.1 %collective-permute-start.7 = (f32[72,128]{1,0:T(8,128)S(1)}, f32[72,128]{1,0:T(8,128)S(1)}, u32[]{:S(2)}, u32[]{:S(2)}) collective-permute-start(f32[72,128]{1,0:T(8,128)S(1)} %get-tuple-element.69), channel_id=1, source_target_pairs={{460,396},{396,332},{332,268},{268,204},{204,140},{140,76},{76,12}... | collective-permute-start | bytes 110600 | tf_op jit(solution)/shard_map/ppermute | solution.py:490
  96.6 7.1 %collective-permute-start.8 = (f32[72,128]{1,0:T(8,128)S(1)}, f32[72,128]{1,0:T(8,128)S(1)}, u32[]{:S(2)}, u32[]{:S(2)}) collective-permute-start(f32[72,128]{1,0:T(8,128)S(1)} %get-tuple-element.70), channel_id=1, source_target_pairs={{460,28},{396,460},{332,396},{268,332},{204,268},{140,204},{76,140... | collective-permute-start | bytes 110600 | tf_op jit(solution)/shard_map/ppermute | solution.py:490
  106.1 13.5 %all-to-all-start.3 = ((f32[16,24,128]{2,1,0:T(8,128)}), f32[16,24,128]{2,1,0:T(8,128)S(1)}, u32[]{:S(2)}, u32[]{:S(2)}) async-start(f32[16,24,128]{2,1,0:T(8,128)} %bitcast.11), calls=%async_computation.3 | async-start | bytes 393216 | tf_op jit(solution)/shard_map/all_to_all | solution.py:485
  111.5 5.0 %collective-permute-start.9 = (f32[24,128]{1,0:T(8,128)S(1)}, f32[24,128]{1,0:T(8,128)S(1)}, u32[]{:S(2)}, u32[]{:S(2)}) collective-permute-start(f32[24,128]{1,0:T(8,128)S(1)} %get-tuple-element.72), channel_id=1, source_target_pairs={{460,488},{396,424},{332,360},{268,296},{204,232},{140,168},{76,10... | collective-permute-start | bytes 36872 | tf_op jit(solution)/shard_map/ppermute | solution.py:490
  120.3 14.9 %collective-permute-start.12 = (f32[24,128]{1,0:T(8,128)S(1)}, f32[24,128]{1,0:T(8,128)S(1)}, u32[]{:S(2)}, u32[]{:S(2)}) collective-permute-start(f32[24,128]{1,0:T(8,128)S(1)} %get-tuple-element.79), channel_id=1, source_target_pairs={{460,488},{396,424},{332,360},{268,296},{204,232},{140,168},{76,10... | collective-permute-start | bytes 36872 | tf_op jit(solution)/shard_map/ppermute | solution.py:490
  122.8 12.4 %collective-permute-start.10 = (f32[48,128]{1,0:T(8,128)S(1)}, f32[48,128]{1,0:T(8,128)S(1)}, u32[]{:S(2)}, u32[]{:S(2)}) collective-permute-start(f32[48,128]{1,0:T(8,128)S(1)} %get-tuple-element.76), channel_id=1, source_target_pairs={{460,396},{396,332},{332,268},{268,204},{204,140},{140,76},{76,12}... | collective-permute-start | bytes 73736 | tf_op jit(solution)/shard_map/ppermute | solution.py:490
  126.8 8.4 %collective-permute-start.11 = (f32[48,128]{1,0:T(8,128)S(1)}, f32[48,128]{1,0:T(8,128)S(1)}, u32[]{:S(2)}, u32[]{:S(2)}) collective-permute-start(f32[48,128]{1,0:T(8,128)S(1)} %get-tuple-element.77), channel_id=1, source_target_pairs={{460,28},{396,460},{332,396},{268,332},{204,268},{140,204},{76,140... | collective-permute-start | bytes 73736 | tf_op jit(solution)/shard_map/ppermute | solution.py:490
  139.1 9.7 %all-to-all-start.4 = ((f32[16,24,128]{2,1,0:T(8,128)}), f32[16,24,128]{2,1,0:T(8,128)S(1)}, u32[]{:S(2)}, u32[]{:S(2)}) async-start(f32[16,24,128]{2,1,0:T(8,128)} %bitcast.14), calls=%async_computation.4 | async-start | bytes 393216 | tf_op jit(solution)/shard_map/all_to_all | solution.py:485
  148.8 8.4 %collective-permute-start.14 = (f32[72,128]{1,0:T(8,128)S(1)}, f32[72,128]{1,0:T(8,128)S(1)}, u32[]{:S(2)}, u32[]{:S(2)}) collective-permute-start(f32[72,128]{1,0:T(8,128)S(1)} %get-tuple-element.87), channel_id=1, source_target_pairs={{460,396},{396,332},{332,268},{268,204},{204,140},{140,76},{76,12}... | collective-permute-start | bytes 110600 | tf_op jit(solution)/shard_map/ppermute | solution.py:490
  153.8 7.2 %collective-permute-start.15 = (f32[72,128]{1,0:T(8,128)S(1)}, f32[72,128]{1,0:T(8,128)S(1)}, u32[]{:S(2)}, u32[]{:S(2)}) collective-permute-start(f32[72,128]{1,0:T(8,128)S(1)} %get-tuple-element.88), channel_id=1, source_target_pairs={{460,28},{396,460},{332,396},{268,332},{204,268},{140,204},{76,140... | collective-permute-start | bytes 110600 | tf_op jit(solution)/shard_map/ppermute | solution.py:490
  163.4 24.5 %all-to-all-start.5 = ((f32[16,24,128]{2,1,0:T(8,128)}), f32[16,24,128]{2,1,0:T(8,128)S(1)}, u32[]{:S(2)}, u32[]{:S(2)}) async-start(f32[16,24,128]{2,1,0:T(8,128)} %bitcast.16), calls=%async_computation.5 | async-start | bytes 393216 | tf_op jit(solution)/shard_map/all_to_all | solution.py:485
  168.9 16.0 %collective-permute-start.16 = (f32[24,128]{1,0:T(8,128)S(1)}, f32[24,128]{1,0:T(8,128)S(1)}, u32[]{:S(2)}, u32[]{:S(2)}) collective-permute-start(f32[24,128]{1,0:T(8,128)S(1)} %get-tuple-element.90), channel_id=1, source_target_pairs={{460,488},{396,424},{332,360},{268,296},{204,232},{140,168},{76,10... | collective-permute-start | bytes 36872 | tf_op jit(solution)/shard_map/ppermute | solution.py:490
  171.3 20.4 %collective-permute-start.13 = (f32[3,4,1024]{2,1,0:T(4,128)S(1)}, f32[3,4,1024]{2,1,0:T(4,128)S(1)}, u32[]{:S(2)}, u32[]{:S(2)}) collective-permute-start(f32[3,4,1024]{2,1,0:T(4,128)S(1)} %get-tuple-element.80), channel_id=1, source_target_pairs={{460,0},{396,1},{332,2},{268,3},{204,4},{140,5},{76,6},{12,7},{0,8... | collective-permute-start | bytes 147464 | tf_op jit(solution)/shard_map/ppermute | solution.py:592
  188.6 16.8 %collective-permute-start.17 = (f32[3,4,1024]{2,1,0:T(4,128)S(1)}, f32[3,4,1024]{2,1,0:T(4,128)S(1)}, u32[]{:S(2)}, u32[]{:S(2)}) collective-permute-start(f32[3,4,1024]{2,1,0:T(4,128)S(1)} %shard_map.100), channel_id=1, source_target_pairs={{460,0},{396,1},{332,2},{268,3},{204,4},{140,5},{76,6},{12,7},{0,8... | collective-permute-start | bytes 147464 | tf_op jit(solution)/shard_map/ppermute | solution.py:593
where the time goes:
time: 208 us; the launch traced here: 207 us
  starting transfers between devices  107 us (51%)
  Pallas kernels  52.5 us (25%)
  waiting for transfers between devices  31.7 us (15%)
  blocking collectives  9.65 us (5%)
  local copies, waits for them, and re-layouts  4.91 us (2%)
    pallas_call x24, Pallas kernels, call(): pl.pallas_call(body, out_shape=shapes, in_specs=specs, out_specs=[pl.Bloc...  52.5 us
    ppermute x15, starting transfers between devices, send(): return lax.ppermute(x, AXES, moves)  43 us
    all_to_all x6, starting transfers between devices, exchange_team(): lax.all_to_all(x.reshape(TEAM_ROWS), TEAM, split_axis=0, concat_axis=0, t...  36.5 us
    ppermute x1, waiting for transfers between devices, shards(): speeds = lax.ppermute(v, AXES, MOVE_OUT)  13.6 us
    ppermute x1, starting transfers between devices, shards(): p = lax.ppermute(packed, AXES, MOVE_IN)  12.7 us
    ppermute x1, starting transfers between devices, shards(): moved = lax.ppermute(moved, AXES, MOVE_OUT)  11.6 us
    ppermute x15, waiting for transfers between devices, send(): return lax.ppermute(x, AXES, moves)  10.9 us
    all_gather x5, blocking collectives, pair(): return lax.all_gather(x, 'core', axis=0, tiled=True)  9.65 us
  transfers between devices with their start and end apart: 24, of which 7 were waited for; matrix products, arithmetic and copies ran while one was open for 0% of the time, Pallas kernels for 17%

commit v1 on v0

--- a/solution.py
+++ b/solution.py
@@ -22,12 +22,10 @@
 WIDTH = 256
 AHEAD = 4
 
-X_ROWS = 0
-V_ROWS = 96
-M_ROW = 192
-A_ROW = 200
-Q_ROW = 208
-PACKED = 216
+M_ROW = 96
+A_ROW = 104
+Q_ROW = 112
+PACKED = 120
 WIDE = 72
 
 AXES = ("z2", "z1", "z0", "core", "zh", "x1", "x0", "y1", "y0")
@@ -78,11 +76,14 @@
         out[d, : 16 * MINE] = table[MEMBER[HALF[s]]][:, b * MINE : (b + 1) * MINE].reshape(-1)
         out[d, SLAB_AT] = s
         out[d, CORE_AT] = b % 2
+        edges = table[MEMBER[HALF[s]]][:, [(b * MINE - 1) % BEADS, (b * MINE + MINE) % BEADS]]
+        out[d, EDGE_AT : EDGE_AT + 32] = edges.reshape(-1)
     return out
 
 
 SLAB_AT = 16 * MINE
 CORE_AT = SLAB_AT + 1
+EDGE_AT = SLAB_AT + 2
 SETTINGS = _settings()
 
 
@@ -245,16 +246,23 @@
     lax.fori_loop(0, MINE // 2, two, 0)
 
 
-def emit(y_refs, up_ref, down_ref, inner_ref, outer_ref, core):
+def emit(y_refs, up_ref, down_ref):
     for i in range(12):
         y = y_refs[8 * i : 8 * i + 8, :]
         down_ref[4 * i : 4 * i + 4, :] = y[0:4]
         up_ref[4 * i : 4 * i + 4, :] = y[4:8]
-    first = y_refs[0:24, :]
-    last = y_refs[72:96, :]
+
+
+def emit_edges(first, last, inner_ref, outer_ref, core):
     odd = core > 0.5
     inner_ref[...] = jnp.where(odd, first, last)
     outer_ref[...] = jnp.where(odd, last, first)
+
+
+def edges_of(inner, outer, core):
+    odd = core > 0.5
+    from_pair = jnp.where(odd, inner[0:24, :], inner[24:48, :])
+    return jnp.where(odd, from_pair, outer[...]), jnp.where(odd, outer[...], from_pair)
 
 
 def emit_partial(y_refs, cols_ref, part_ref):
@@ -266,12 +274,15 @@
         part_ref[24 * r : 24 * r + 24, :] = total
 
 
-def pack_kernel(x_ref, v_ref, m_ref, a_ref, q_ref, out_ref):
-    for base, ref in ((X_ROWS, x_ref), (V_ROWS, v_ref)):
-        for k in range(3):
-            for block in range(8):
-                row = base + 8 * k + block
-                out_ref[pl.ds(row, 4, stride=24), :] = ref[k, :, 128 * block : 128 * block + 128]
+def spread(ref, out_ref, centre):
+    for k in range(3):
+        for block in range(8):
+            value = ref[k, :, 128 * block : 128 * block + 128]
+            out_ref[pl.ds(8 * k + block, 4, stride=24), :] = value if centre is None else value - centre[k]
+
+
+def pack_kernel(v_ref, m_ref, a_ref, q_ref, out_ref):
+    spread(v_ref, out_ref, None)
     out_ref[M_ROW : M_ROW + 8, :] = m_ref[...]
     out_ref[A_ROW : A_ROW + 8, :] = a_ref[...]
     out_ref[Q_ROW : Q_ROW + 8, :] = q_ref[...]
@@ -283,17 +294,14 @@
             out_ref[k, :, 128 * block : 128 * block + 128] = value_ref[pl.ds(8 * k + block, 4, stride=24), :]
 
 
-def start_kernel(cols_ref, p_ref, y_ref, up_ref, down_ref, inner_ref, outer_ref, part_ref):
-    centre = 2.0 * cols_ref[0, SLAB_AT] + 1.0
-    for b in range(MINE):
-        for k in range(3):
-            i = 8 * (3 * b + k)
-            y_ref[i : i + 8, :] = p_ref[i : i + 8, :] - (centre if k == 0 else 1.0)
-    emit(y_ref, up_ref, down_ref, inner_ref, outer_ref, cols_ref[0, CORE_AT])
+def start_kernel(cols_ref, x_ref, y_ref, up_ref, down_ref, inner_ref, outer_ref, part_ref):
+    spread(x_ref, y_ref, (2.0 * cols_ref[0, SLAB_AT] + 1.0, 1.0, 1.0))
+    emit(y_ref, up_ref, down_ref)
+    emit_edges(y_ref[0:24, :], y_ref[72:96, :], inner_ref, outer_ref, cols_ref[0, CORE_AT])
     emit_partial(y_ref, cols_ref, part_ref)
 
 
-def near_halo_body(rate, cols_ref, p_ref, y_ref, v_ref, r_ref, left, right, wide_l, wide_r, inner, outer, store, scr):
+def near_halo_body(rate, p_ref, y_ref, v_ref, r_ref, left, right, wide_l, wide_r, edges, store, scr):
     chain = scr[10]
     for i in range(2):
         init_rows(*slot(scr, i)[:2])
@@ -301,11 +309,8 @@
     mass = p_ref[M_ROW : M_ROW + 8, :]
     inverse = 1.0 / mass
     share = halves(wide_l[WIDE + 4 : WIDE + 8, :], wide_r[WIDE : WIDE + 4, :])
-    odd = cols_ref[0, CORE_AT] > 0.5
-    from_pair = jnp.where(odd, inner[0:24, :], inner[24:48, :])
-    chain[0:24, :] = jnp.where(odd, from_pair, outer[...])
+    chain[0:24, :], chain[120:144, :] = edges
     chain[24:120, :] = y_ref[...]
-    chain[120:144, :] = jnp.where(odd, outer[...], from_pair)
     shift = jnp.where(lax.broadcasted_iota(jnp.int32, (8, 128), 0) < 4, -2.0, 2.0).astype(f32)
 
     def two(i, carry):
@@ -338,24 +343,27 @@
                 r = at + 24 * j + 8 * k
                 spring = 2.0 * coords[k] - chain[pl.ds(r, 8), :] - chain[pl.ds(r + 48, 8), :]
                 total = force[k] - SPRING * mass * spring
-                store(r, coords[k], v_ref[pl.ds(V_AT(v_ref) + r, 8), :] + rate * total * inverse)
+                store(r, coords[k], v_ref[pl.ds(r, 8), :] + rate * total * inverse)
         return carry
 
     lax.fori_loop(0, MINE // 2, two, 0)
 
 
-def V_AT(ref):
-    return V_ROWS if ref.shape[0] == PACKED else 0
-
-
-def near_slow_kernel(rate, cols_ref, p_ref, y_ref, v_ref, r_ref, left, right, wide_l, wide_r, inner, outer, vo_ref, *scr):
+def near_slow_kernel(rate, cols_ref, p_ref, y_ref, v_ref, r_ref, left, right, wide_l, wide_r, inner, outer, vo_ref, *rest):
     def store(r, y, v):
         vo_ref[pl.ds(r, 8), :] = v
 
-    near_halo_body(rate, cols_ref, p_ref, y_ref, v_ref, r_ref, left, right, wide_l, wide_r, inner, outer, store, scr)
-
-
-def near_fast_kernel(last, cols_ref, p_ref, y_ref, v_ref, r_ref, left, right, wide_l, wide_r, inner, outer, *rest):
+    core = cols_ref[0, CORE_AT]
+    edges = edges_of(inner, outer, core)
+    scr = rest[-len(SCRATCH) - 1 :]
+    near_halo_body(rate, p_ref, y_ref, v_ref, r_ref, left, right, wide_l, wide_r, edges, store, scr)
+    if len(rest) > len(scr):
+        first = y_ref[0:24, :] + TIME_STEP * vo_ref[0:24, :]
+        last = y_ref[72:96, :] + TIME_STEP * vo_ref[72:96, :]
+        emit_edges(first, last, rest[0], rest[1], core)
+
+
+def near_fast_kernel(last, cols_ref, p_ref, y_ref, v_ref, r_ref, left, right, wide_l, wide_r, before, after, *rest):
     if last:
         first_ref, vo_ref, yo_ref, up_ref, down_ref, in_ref, ou_ref, part_ref, moved_ref = rest[:9]
         scr = rest[9:]
@@ -367,8 +375,10 @@
         vo_ref[pl.ds(r, 8), :] = v
         yo_ref[pl.ds(r, 8), :] = y + TIME_STEP * v
 
-    near_halo_body(TIME_STEP, cols_ref, p_ref, y_ref, v_ref, r_ref, left, right, wide_l, wide_r, inner, outer, store, scr)
-    emit(yo_ref, up_ref, down_ref, in_ref, ou_ref, cols_ref[0, CORE_AT])
+    edges = (before[...], after[...])
+    near_halo_body(TIME_STEP, p_ref, y_ref, v_ref, r_ref, left, right, wide_l, wide_r, edges, store, scr)
+    emit(yo_ref, up_ref, down_ref)
+    emit_edges(yo_ref[0:24, :], yo_ref[72:96, :], in_ref, ou_ref, cols_ref[0, CORE_AT])
     emit_partial(yo_ref, cols_ref, part_ref)
     if last:
         rows = scr[-1]
@@ -437,11 +447,20 @@
     return out
 
 
-def update_kernel(rate, cols_ref, p_ref, y_ref, v_ref, far_ref, vo_ref, yo_ref, up_ref, down_ref, in_ref, ou_ref):
+def update_kernel(rate, cols_ref, p_ref, y_ref, v_ref, far_ref, inner, outer,
+                  vo_ref, yo_ref, up_ref, down_ref, before_ref, after_ref):
     for b, v in enumerate(kick(rate, cols_ref, p_ref, v_ref, far_ref)):
         vo_ref[24 * b : 24 * b + 24, :] = v
         yo_ref[24 * b : 24 * b + 24, :] = y_ref[24 * b : 24 * b + 24, :] + TIME_STEP * v
-    emit(yo_ref, up_ref, down_ref, in_ref, ou_ref, cols_ref[0, CORE_AT])
+    emit(yo_ref, up_ref, down_ref)
+    inverse = (TIME_STEP * rate * BEADS / CBEADS) / p_ref[M_ROW : M_ROW + 8, :]
+    inverse = jnp.concatenate([inverse] * 3, axis=0)
+    edges = edges_of(inner, outer, cols_ref[0, CORE_AT])
+    for e, out in enumerate((before_ref, after_ref)):
+        total = cols_ref[0, EDGE_AT + e] * far_ref[0:24, :]
+        for r in range(1, 16):
+            total = total + cols_ref[0, EDGE_AT + 2 * r + e] * far_ref[24 * r : 24 * r + 24, :]
+        out[...] = edges[e] + inverse * total
 
 
 def final_kernel(rate, cols_ref, p_ref, v_ref, far_ref, out_ref, rows):
@@ -498,22 +517,21 @@
 
 
 def shards(positions, velocities, masses, amplitudes, charges):
+    x = send(jnp.transpose(positions, (1, 0, 2)), MOVE_IN)
     (packed,) = call(
         pack_kernel,
         [(PACKED, 128)],
         None,
         [
-            jnp.transpose(positions, (1, 0, 2)),
             jnp.transpose(velocities, (1, 0, 2)),
             masses.reshape(8, 128),
             amplitudes.reshape(8, 128),
             charges.reshape(8, 128),
         ],
     )
-    p = lax.ppermute(packed, AXES, MOVE_IN)
+    p = send(packed, MOVE_IN)
     cols = lax.dynamic_slice_in_dim(jnp.asarray(SETTINGS), lax.axis_index(AXES), 1, 0)
-
-    y, up, down, inner, outer, part = call(start_kernel, [STATE, HALO, HALO, BEAD, BEAD, (384, 128)], cols, [p])
+    y, up, down, inner, outer, part = call(start_kernel, [STATE, HALO, HALO, BEAD, BEAD, (384, 128)], cols, [x])
     first = y
     v = p
     wide_l = wide_r = None
@@ -523,8 +541,6 @@
         if not slow:
             left = send(up, SLAB_UP)
             right = send(down, SLAB_DOWN)
-            outer = send(outer, BEAD_SWAP)
-            inner = pair(inner)
             (sums,) = call(near_own_kernel, [(128, 128)], None, [y, p], SCRATCH, big)
             last = stage == 3
 
@@ -535,7 +551,7 @@
                 near_fast,
                 [STATE, STATE, HALO, HALO, BEAD, BEAD, (384, 128)] + [PLAIN] * last,
                 cols,
-                [p, y, v, sums, left, right, wide_l, wide_r, inner, outer] + [first] * last,
+                [p, y, v, sums, left, right, wide_l, wide_r, before, after] + [first] * last,
                 SCRATCH + [CHAIN] + [pltpu.VMEM(STATE, f32)] * last,
                 big // 2,
             )
@@ -568,9 +584,9 @@
         def near_slow(*refs, rate=rate):
             near_slow_kernel(rate, *refs)
 
-        (v,) = call(
+        v, *ends = call(
             near_slow,
-            [STATE],
+            [STATE] + [BEAD] * (2 * (stage < 4)),
             cols,
             [p, y, v, sums, left, right, wide_l, wide_r, inner, outer],
             SCRATCH + [CHAIN],
@@ -588,7 +604,11 @@
             def update(*refs, rate=rate):
                 update_kernel(rate, *refs)
 
-            v, y, up, down, inner, outer = call(update, [STATE, STATE, HALO, HALO, BEAD, BEAD], cols, [p, y, v, far])
+            inner = pair(ends[0])
+            outer = send(ends[1], BEAD_SWAP)
+            v, y, up, down, before, after = call(
+                update, [STATE, STATE, HALO, HALO, BEAD, BEAD], cols, [p, y, v, far, inner, outer]
+            )
     moved = lax.ppermute(moved, AXES, MOVE_OUT)
     speeds = lax.ppermute(v, AXES, MOVE_OUT)
     return jnp.transpose(moved, (1, 0, 2)), jnp.transpose(speeds, (1, 0, 2))

time: 208 us -> 216 us (1.038)
  the two profiles are of different devices: /device:TPU:30 before, /device:TPU:1 now
where the time goes in v1:
time: 216 us; the launch traced here: 212 us
  starting transfers between devices  132 us (61%)
  Pallas kernels  52.6 us (24%)
  waiting for transfers between devices  15.2 us (7%)
  blocking collectives  9.39 us (4%)
  local copies, waits for them, and re-layouts  2.6 us (1%)
    ppermute x17, starting transfers between devices, send(): return lax.ppermute(x, AXES, moves)  81.2 us
    pallas_call x24, Pallas kernels, call(): pl.pallas_call(body, out_shape=shapes, in_specs=specs, out_specs=[pl.Bloc...  52.6 us
    all_to_all x6, starting transfers between devices, exchange_team(): lax.all_to_all(x.reshape(TEAM_ROWS), TEAM, split_axis=0, concat_axis=0, t...  30.7 us
    ppermute x1, starting transfers between devices, shards(): speeds = lax.ppermute(v, AXES, MOVE_OUT)  16.5 us
    all_gather x5, blocking collectives, pair(): return lax.all_gather(x, 'core', axis=0, tiled=True)  9.39 us
    ppermute x17, waiting for transfers between devices, send(): return lax.ppermute(x, AXES, moves)  7.76 us
    all_to_all x6, waiting for transfers between devices, exchange_team(): lax.all_to_all(x.reshape(TEAM_ROWS), TEAM, split_axis=0, concat_axis=0, t...  4.81 us
  transfers between devices with their start and end apart: 25, of which 12 were waited for; matrix products, arithmetic and copies ran while one was open for 0% of the time, Pallas kernels for 16%

profile of v1, /device:TPU:1, one launch (start us, length us, event | category | flops | bytes accessed | tf_op | source)
XLA Modules:
  0.0 212.5 jit_solution(14035559687397715224)
XLA Ops:
  0.6 15.9 %collective-permute-start.1 = (f32[3,4,1024]{2,1,0:T(4,128)}, f32[3,4,1024]{2,1,0:T(4,128)S(1)}, u32[]{:S(2)}, u32[]{:S(2)}) collective-permute-start(f32[3,4,1024]{2,1,0:T(4,128)} %bitcast.31), channel_id=1, source_target_pairs={{0,460},{1,396},{2,332},{3,268},{4,204},{5,140},{6,76},{7,12},{8,0... | collective-permute-start | bytes 147464 | tf_op jit(solution)/shard_map/ppermute | solution.py:509
  16.5 0.7 constant_dynamic-slice_fusion.refs_0_
  17.2 0.8 collective-permute-done.1.refs_1_
  18.0 1.3 shard_map.78
  19.3 5.7 %all-to-all-start = ((f32[16,24,128]{2,1,0:T(8,128)}), f32[16,24,128]{2,1,0:T(8,128)S(1)}, u32[]{:S(2)}, u32[]{:S(2)}) async-start(f32[16,24,128]{2,1,0:T(8,128)} %bitcast.5), calls=%async_computation | async-start | bytes 393216 | tf_op jit(solution)/shard_map/all_to_all | solution.py:504
  25.0 0.6 copy-done.1
  25.7 15.9 %collective-permute-start = (f32[120,128]{1,0:T(8,128)S(1)}, f32[120,128]{1,0:T(8,128)S(1)}, u32[]{:S(2)}, u32[]{:S(2)}) collective-permute-start(f32[120,128]{1,0:T(8,128)S(1)} %shard_map.77), channel_id=1, source_target_pairs={{0,460},{1,396},{2,332},{3,268},{4,204},{5,140},{6,76},{7,12},{8,0... | collective-permute-start | bytes 184328 | tf_op jit(solution)/shard_map/ppermute | solution.py:509
  41.6 1.3 collective-permute-done.refs_1_.refs_3_
  42.9 4.3 %shard_map.79.refs_4_ = f32[128,128]{1,0:T(8,128)S(1)} custom-call(f32[96,128]{1,0:T(8,128)S(1)} %get-tuple-element.53.refs_0_.refs_2_.refs_11_, f32[120,128]{1,0:T(8,128)S(1)} %collective-permute-done.refs_1_.refs_3_), custom_call_target="tpu_custom_call" | custom-call | flops 400000000 | bytes 400000 | tf_op jit(solution)/shard_map/pallas_call | solution.py:484
  47.2 4.8 %collective-permute-start.2 = (f32[88,128]{1,0:T(8,128)S(1)}, f32[88,128]{1,0:T(8,128)S(1)}, u32[]{:S(2)}, u32[]{:S(2)}) collective-permute-start(f32[88,128]{1,0:T(8,128)S(1)} %get-tuple-element.58), channel_id=1, source_target_pairs={{460,396},{396,332},{332,268},{268,204},{204,140},{140,76},{76,12}... | collective-permute-start | bytes 135176 | tf_op jit(solution)/shard_map/ppermute | solution.py:509
  52.0 1.9 collective-permute-start.3
  53.9 1.2 shard_map.82.refs_2_
  55.2 2.7 %collective-permute-done.3.refs_6_.refs_8_.refs_4_ = f32[88,128]{1,0:T(8,128)S(1)} collective-permute-done((f32[88,128]{1,0:T(8,128)S(1)}, f32[88,128]{1,0:T(8,128)S(1)}, u32[]{:S(2)}, u32[]{:S(2)}) %collective-permute-start.3) | collective-permute-done | bytes 45088 | tf_op jit(solution)/shard_map/ppermute | solution.py:509
  57.9 2.4 %shard_map.83 = f32[384,128]{1,0:T(8,128)} custom-call(f32[24,128]{1,0:T(8,128)S(1)} %get-tuple-element.63.refs_0_, f32[120,128]{1,0:T(8,128)S(1)} %collective-permute-done.refs_1_.refs_3_, f32[32,128]{1,0:T(8,128)S(1)} %shard_map.82.refs_2_, f32[88,128]{1,0:T(8,128)S(1)} %collective-permute-done.2.refs_5_.refs_7_.refs_3_, ...), custom_call_target="tpu_custom_call" | custom-call | flops 100000000 | bytes 400000 | tf_op jit(solution)/shard_map/pallas_call | solution.py:484
  60.3 4.9 %all-to-all-start.1 = ((f32[16,24,128]{2,1,0:T(8,128)}), f32[16,24,128]{2,1,0:T(8,128)S(1)}, u32[]{:S(2)}, u32[]{:S(2)}) async-start(f32[16,24,128]{2,1,0:T(8,128)} %bitcast.7), calls=%async_computation.1 | async-start | bytes 393216 | tf_op jit(solution)/shard_map/all_to_all | solution.py:504
  65.3 3.5 %collective-permute-start.4 = (f32[24,128]{1,0:T(8,128)S(1)}, f32[24,128]{1,0:T(8,128)S(1)}, u32[]{:S(2)}, u32[]{:S(2)}) collective-permute-start(f32[24,128]{1,0:T(8,128)S(1)} %get-tuple-element.61), channel_id=1, source_target_pairs={{460,488},{396,424},{332,360},{268,296},{204,232},{140,168},{76,10... | collective-permute-start | bytes 36872 | tf_op jit(solution)/shard_map/ppermute | solution.py:509
  68.8 1.8 all_gather.15.refs_9_
  70.6 0.2 collective-permute-done.4.refs_10_
  70.9 3.1 %shard_map.81 = (f32[96,128]{1,0:T(8,128)S(1)}, f32[24,128]{1,0:T(8,128)S(1)}, f32[24,128]{1,0:T(8,128)S(1)}) custom-call(f32[1,128]{1,0:T(1,128)S(1)} %constant_dynamic-slice_fusion.refs_0_, f32[120,128]{1,0:T(8,128)S(1)} %collective-permute-done.refs_1_.refs_3_, f32[96,128]{1,0:T(8,128)S(1)} %get-tuple-element.53.refs_0_.refs_2_.refs_11_, ...), custom_call_target="tpu_custom_call" | custom-call | flops 200000000 | bytes 400000 | tf_op jit(solution)/shard_map/pallas_call | solution.py:484
  74.0 2.9 %collective-permute-start.5 = (f32[24,128]{1,0:T(8,128)S(1)}, f32[24,128]{1,0:T(8,128)S(1)}, u32[]{:S(2)}, u32[]{:S(2)}) collective-permute-start(f32[24,128]{1,0:T(8,128)S(1)} %get-tuple-element.65), channel_id=1, source_target_pairs={{460,488},{396,424},{332,360},{268,296},{204,232},{140,168},{76,10... | collective-permute-start | bytes 36872 | tf_op jit(solution)/shard_map/ppermute | solution.py:509
  76.9 1.9 all_gather.16.refs_5_
  79.0 0.7 shard_map.84
  79.7 3.8 %collective-permute-start.6 = (f32[48,128]{1,0:T(8,128)S(1)}, f32[48,128]{1,0:T(8,128)S(1)}, u32[]{:S(2)}, u32[]{:S(2)}) collective-permute-start(f32[48,128]{1,0:T(8,128)S(1)} %get-tuple-element.68), channel_id=1, source_target_pairs={{460,396},{396,332},{332,268},{268,204},{204,140},{140,76},{76,12}... | collective-permute-start | bytes 73736 | tf_op jit(solution)/shard_map/ppermute | solution.py:509
  83.5 2.7 %collective-permute-start.7 = (f32[48,128]{1,0:T(8,128)S(1)}, f32[48,128]{1,0:T(8,128)S(1)}, u32[]{:S(2)}, u32[]{:S(2)}) collective-permute-start(f32[48,128]{1,0:T(8,128)S(1)} %get-tuple-element.69), channel_id=1, source_target_pairs={{460,28},{396,460},{332,396},{268,332},{204,268},{140,204},{76,140... | collective-permute-start | bytes 73736 | tf_op jit(solution)/shard_map/ppermute | solution.py:509
  86.2 4.3 %shard_map.85.refs_4_ = f32[128,128]{1,0:T(8,128)S(1)} custom-call(f32[96,128]{1,0:T(8,128)S(1)} %get-tuple-element.66.refs_0_.refs_2_, f32[120,128]{1,0:T(8,128)S(1)} %collective-permute-done.refs_1_.refs_3_), custom_call_target="tpu_custom_call" | custom-call | flops 400000000 | bytes 400000 | tf_op jit(solution)/shard_map/pallas_call | solution.py:484
  90.4 3.9 %shard_map.86 = (f32[96,128]{1,0:T(8,128)S(1)}, f32[96,128]{1,0:T(8,128)S(1)}, f32[48,128]{1,0:T(8,128)S(1)}, f32[48,128]{1,0:T(8,128)S(1)}, f32[24,128]{1,0:T(8...) custom-call(f32[1,128]{1,0:T(1,128)S(1)} %constant_dynamic-slice_fusion.refs_0_, ...), custom_call_target="tpu_custom_call" | custom-call | flops 200000000 | bytes 400000 | tf_op jit(solution)/shard_map/pallas_call | solution.py:484
  94.3 4.8 %all-to-all-start.2 = ((f32[16,24,128]{2,1,0:T(8,128)}), f32[16,24,128]{2,1,0:T(8,128)S(1)}, u32[]{:S(2)}, u32[]{:S(2)}) async-start(f32[16,24,128]{2,1,0:T(8,128)} %bitcast.9), calls=%async_computation.2 | async-start | bytes 393216 | tf_op jit(solution)/shard_map/all_to_all | solution.py:504
  99.1 4.3 %shard_map.87.refs_4_ = f32[128,128]{1,0:T(8,128)S(1)} custom-call(f32[96,128]{1,0:T(8,128)S(1)} %get-tuple-element.72.refs_0_.refs_2_, f32[120,128]{1,0:T(8,128)S(1)} %collective-permute-done.refs_1_.refs_3_), custom_call_target="tpu_custom_call" | custom-call | flops 400000000 | bytes 400000 | tf_op jit(solution)/shard_map/pallas_call | solution.py:484
  103.4 2.4 %all-to-all-done.2 = f32[16,24,128]{2,1,0:T(8,128)S(1)} async-done(((f32[16,24,128]{2,1,0:T(8,128)}), f32[16,24,128]{2,1,0:T(8,128)S(1)}, u32[]{:S(2)}, u32[]{:S(2)}) %all-to-all-start.2) | async-done | bytes 196640 | tf_op jit(solution)/shard_map/all_to_all | solution.py:504
  105.8 3.5 %collective-permute-start.8 = (f32[72,128]{1,0:T(8,128)S(1)}, f32[72,128]{1,0:T(8,128)S(1)}, u32[]{:S(2)}, u32[]{:S(2)}) collective-permute-start(f32[72,128]{1,0:T(8,128)S(1)} %get-tuple-element.78), channel_id=1, source_target_pairs={{460,396},{396,332},{332,268},{268,204},{204,140},{140,76},{76,12}... | collective-permute-start | bytes 110600 | tf_op jit(solution)/shard_map/ppermute | solution.py:509
  109.3 2.9 %collective-permute-start.9 = (f32[72,128]{1,0:T(8,128)S(1)}, f32[72,128]{1,0:T(8,128)S(1)}, u32[]{:S(2)}, u32[]{:S(2)}) collective-permute-start(f32[72,128]{1,0:T(8,128)S(1)} %get-tuple-element.79), channel_id=1, source_target_pairs={{460,28},{396,460},{332,396},{268,332},{204,268},{140,204},{76,140... | collective-permute-start | bytes 110600 | tf_op jit(solution)/shard_map/ppermute | solution.py:509
  112.3 1.2 shard_map.90.refs_2_
  113.5 0.8 collective-permute-done.9.refs_6_.refs_4_
  114.3 2.4 %shard_map.91 = f32[384,128]{1,0:T(8,128)} custom-call(f32[24,128]{1,0:T(8,128)S(1)} %get-tuple-element.83.refs_0_, f32[120,128]{1,0:T(8,128)S(1)} %collective-permute-done.refs_1_.refs_3_, f32[32,128]{1,0:T(8,128)S(1)} %shard_map.90.refs_2_, f32[72,128]{1,0:T(8,128)S(1)} %collective-permute-done.8.refs_5_.refs_3_, ...), custom_call_target="tpu_custom_call" | custom-call | flops 100000000 | bytes 400000 | tf_op jit(solution)/shard_map/pallas_call | solution.py:484
  116.7 5.3 %all-to-all-start.3 = ((f32[16,24,128]{2,1,0:T(8,128)}), f32[16,24,128]{2,1,0:T(8,128)S(1)}, u32[]{:S(2)}, u32[]{:S(2)}) async-start(f32[16,24,128]{2,1,0:T(8,128)} %bitcast.11), calls=%async_computation.3 | async-start | bytes 393216 | tf_op jit(solution)/shard_map/all_to_all | solution.py:504
  122.0 3.5 %collective-permute-start.10 = (f32[24,128]{1,0:T(8,128)S(1)}, f32[24,128]{1,0:T(8,128)S(1)}, u32[]{:S(2)}, u32[]{:S(2)}) collective-permute-start(f32[24,128]{1,0:T(8,128)S(1)} %get-tuple-element.81), channel_id=1, source_target_pairs={{460,488},{396,424},{332,360},{268,296},{204,232},{140,168},{76,10... | collective-permute-start | bytes 36872 | tf_op jit(solution)/shard_map/ppermute | solution.py:509
  125.5 1.8 all_gather.17.refs_9_
  127.4 0.2 collective-permute-done.10.refs_10_
  127.6 3.1 %shard_map.89 = (f32[96,128]{1,0:T(8,128)S(1)}, f32[24,128]{1,0:T(8,128)S(1)}, f32[24,128]{1,0:T(8,128)S(1)}) custom-call(f32[1,128]{1,0:T(1,128)S(1)} %constant_dynamic-slice_fusion.refs_0_, f32[120,128]{1,0:T(8,128)S(1)} %collective-permute-done.refs_1_.refs_3_, f32[96,128]{1,0:T(8,128)S(1)} %get-tuple-element.72.refs_0_.refs_2_, ...), custom_call_target="tpu_custom_call" | custom-call | flops 200000000 | bytes 400000 | tf_op jit(solution)/shard_map/pallas_call | solution.py:484
  130.7 2.9 %collective-permute-start.11 = (f32[24,128]{1,0:T(8,128)S(1)}, f32[24,128]{1,0:T(8,128)S(1)}, u32[]{:S(2)}, u32[]{:S(2)}) collective-permute-start(f32[24,128]{1,0:T(8,128)S(1)} %get-tuple-element.85), channel_id=1, source_target_pairs={{460,488},{396,424},{332,360},{268,296},{204,232},{140,168},{76,10... | collective-permute-start | bytes 36872 | tf_op jit(solution)/shard_map/ppermute | solution.py:509
  133.7 1.9 all_gather.18.refs_5_
  135.7 0.7 shard_map.92
  136.4 3.6 %collective-permute-start.12 = (f32[48,128]{1,0:T(8,128)S(1)}, f32[48,128]{1,0:T(8,128)S(1)}, u32[]{:S(2)}, u32[]{:S(2)}) collective-permute-start(f32[48,128]{1,0:T(8,128)S(1)} %get-tuple-element.88), channel_id=1, source_target_pairs={{460,396},{396,332},{332,268},{268,204},{204,140},{140,76},{76,12}... | collective-permute-start | bytes 73736 | tf_op jit(solution)/shard_map/ppermute | solution.py:509
  140.0 2.8 %collective-permute-start.13 = (f32[48,128]{1,0:T(8,128)S(1)}, f32[48,128]{1,0:T(8,128)S(1)}, u32[]{:S(2)}, u32[]{:S(2)}) collective-permute-start(f32[48,128]{1,0:T(8,128)S(1)} %get-tuple-element.89), channel_id=1, source_target_pairs={{460,28},{396,460},{332,396},{268,332},{204,268},{140,204},{76,140... | collective-permute-start | bytes 73736 | tf_op jit(solution)/shard_map/ppermute | solution.py:509
  142.9 4.2 %shard_map.93.refs_4_ = f32[128,128]{1,0:T(8,128)S(1)} custom-call(f32[96,128]{1,0:T(8,128)S(1)} %get-tuple-element.86.refs_0_.refs_2_, f32[120,128]{1,0:T(8,128)S(1)} %collective-permute-done.refs_1_.refs_3_), custom_call_target="tpu_custom_call" | custom-call | flops 400000000 | bytes 400000 | tf_op jit(solution)/shard_map/pallas_call | solution.py:484
  147.2 3.9 %shard_map.94 = (f32[96,128]{1,0:T(8,128)S(1)}, f32[96,128]{1,0:T(8,128)S(1)}, f32[48,128]{1,0:T(8,128)S(1)}, f32[48,128]{1,0:T(8,128)S(1)}, f32[24,128]{1,0:T(8...) custom-call(f32[1,128]{1,0:T(1,128)S(1)} %constant_dynamic-slice_fusion.refs_0_, ...), custom_call_target="tpu_custom_call" | custom-call | flops 200000000 | bytes 400000 | tf_op jit(solution)/shard_map/pallas_call | solution.py:484
  151.0 4.8 %all-to-all-start.4 = ((f32[16,24,128]{2,1,0:T(8,128)}), f32[16,24,128]{2,1,0:T(8,128)S(1)}, u32[]{:S(2)}, u32[]{:S(2)}) async-start(f32[16,24,128]{2,1,0:T(8,128)} %bitcast.14), calls=%async_computation.4 | async-start | bytes 393216 | tf_op jit(solution)/shard_map/all_to_all | solution.py:504
  155.8 4.3 %shard_map.95.refs_4_ = f32[128,128]{1,0:T(8,128)S(1)} custom-call(f32[96,128]{1,0:T(8,128)S(1)} %get-tuple-element.93.refs_0_.refs_2_, f32[120,128]{1,0:T(8,128)S(1)} %collective-permute-done.refs_1_.refs_3_), custom_call_target="tpu_custom_call" | custom-call | flops 400000000 | bytes 400000 | tf_op jit(solution)/shard_map/pallas_call | solution.py:484
  160.1 2.4 %all-to-all-done.4 = f32[16,24,128]{2,1,0:T(8,128)S(1)} async-done(((f32[16,24,128]{2,1,0:T(8,128)}), f32[16,24,128]{2,1,0:T(8,128)S(1)}, u32[]{:S(2)}, u32[]{:S(2)}) %all-to-all-start.4) | async-done | bytes 196640 | tf_op jit(solution)/shard_map/all_to_all | solution.py:504
  162.5 3.7 %collective-permute-start.15 = (f32[72,128]{1,0:T(8,128)S(1)}, f32[72,128]{1,0:T(8,128)S(1)}, u32[]{:S(2)}, u32[]{:S(2)}) collective-permute-start(f32[72,128]{1,0:T(8,128)S(1)} %get-tuple-element.99), channel_id=1, source_target_pairs={{460,396},{396,332},{332,268},{268,204},{204,140},{140,76},{76,12}... | collective-permute-start | bytes 110600 | tf_op jit(solution)/shard_map/ppermute | solution.py:509
  166.2 3.0 %collective-permute-start.16 = (f32[72,128]{1,0:T(8,128)S(1)}, f32[72,128]{1,0:T(8,128)S(1)}, u32[]{:S(2)}, u32[]{:S(2)}) collective-permute-start(f32[72,128]{1,0:T(8,128)S(1)} %get-tuple-element.100), channel_id=1, source_target_pairs={{460,28},{396,460},{332,396},{268,332},{204,268},{140,204},{76,140... | collective-permute-start | bytes 110600 | tf_op jit(solution)/shard_map/ppermute | solution.py:509
  169.2 1.2 shard_map.98.refs_2_
  170.5 1.4 collective-permute-done.16.refs_6_.refs_4_
  171.9 2.4 %shard_map.99 = f32[384,128]{1,0:T(8,128)} custom-call(f32[24,128]{1,0:T(8,128)S(1)} %get-tuple-element.103.refs_0_, f32[120,128]{1,0:T(8,128)S(1)} %collective-permute-done.refs_1_.refs_3_, f32[32,128]{1,0:T(8,128)S(1)} %shard_map.98.refs_2_, f32[72,128]{1,0:T(8,128)S(1)} %collective-permute-done.15.refs_5_.refs_3_, ...), custom_call_target="tpu_custom_call" | custom-call | flops 100000000 | bytes 400000 | tf_op jit(solution)/shard_map/pallas_call | solution.py:484
  174.4 5.3 %all-to-all-start.5 = ((f32[16,24,128]{2,1,0:T(8,128)}), f32[16,24,128]{2,1,0:T(8,128)S(1)}, u32[]{:S(2)}, u32[]{:S(2)}) async-start(f32[16,24,128]{2,1,0:T(8,128)} %bitcast.16), calls=%async_computation.5 | async-start | bytes 393216 | tf_op jit(solution)/shard_map/all_to_all | solution.py:504
  179.6 3.5 %collective-permute-start.17 = (f32[24,128]{1,0:T(8,128)S(1)}, f32[24,128]{1,0:T(8,128)S(1)}, u32[]{:S(2)}, u32[]{:S(2)}) collective-permute-start(f32[24,128]{1,0:T(8,128)S(1)} %get-tuple-element.102), channel_id=1, source_target_pairs={{460,488},{396,424},{332,360},{268,296},{204,232},{140,168},{76,10... | collective-permute-start | bytes 36872 | tf_op jit(solution)/shard_map/ppermute | solution.py:509
  183.1 3.3 %collective-permute-start.14 = (f32[3,4,1024]{2,1,0:T(4,128)S(1)}, f32[3,4,1024]{2,1,0:T(4,128)S(1)}, u32[]{:S(2)}, u32[]{:S(2)}) collective-permute-start(f32[3,4,1024]{2,1,0:T(4,128)S(1)} %get-tuple-element.92), channel_id=1, source_target_pairs={{460,0},{396,1},{332,2},{268,3},{204,4},{140,5},{76,6},{12,7},{0,8... | collective-permute-start | bytes 147464 | tf_op jit(solution)/shard_map/ppermute | solution.py:612
  186.4 1.9 all_gather.19.refs_9_
  188.3 3.1 %shard_map.97.refs_2_ = f32[96,128]{1,0:T(8,128)S(1)} custom-call(f32[1,128]{1,0:T(1,128)S(1)} %constant_dynamic-slice_fusion.refs_0_, f32[120,128]{1,0:T(8,128)S(1)} %collective-permute-done.refs_1_.refs_3_, f32[96,128]{1,0:T(8,128)S(1)} %get-tuple-element.93.refs_0_.refs_2_, f32[96,128]{1,0:T(8,128)S(1)} %get-tuple-element.94.refs_3_, ...), custom_call_target="tpu_custom_call" | custom-call | flops 200000000 | bytes 400000 | tf_op jit(solution)/shard_map/pallas_call | solution.py:484
  191.4 0.6 shard_map.100
  192.1 16.5 %collective-permute-start.18 = (f32[3,4,1024]{2,1,0:T(4,128)S(1)}, f32[3,4,1024]{2,1,0:T(4,128)S(1)}, u32[]{:S(2)}, u32[]{:S(2)}) collective-permute-start(f32[3,4,1024]{2,1,0:T(4,128)S(1)} %shard_map.100), channel_id=1, source_target_pairs={{460,0},{396,1},{332,2},{268,3},{204,4},{140,5},{76,6},{12,7},{0,8... | collective-permute-start | bytes 147464 | tf_op jit(solution)/shard_map/ppermute | solution.py:613
  208.6 2.7 %collective-permute-done.18 = f32[3,4,1024]{2,1,0:T(4,128)S(1)} collective-permute-done((f32[3,4,1024]{2,1,0:T(4,128)S(1)}, f32[3,4,1024]{2,1,0:T(4,128)S(1)}, u32[]{:S(2)}, u32[]{:S(2)}) %collective-permute-start.18) | collective-permute-done | bytes 49184 | tf_op jit(solution)/shard_map/ppermute | solution.py:613
  211.3 0.6 copy.16
  211.9 0.6 copy.17
  (26 shorter events, 0.4 us)
Async XLA Ops:
  0.6 17.4 %collective-permute-start.1 = (f32[3,4,1024]{2,1,0:T(4,128)}, f32[3,4,1024]{2,1,0:T(4,128)S(1)}, u32[]{:S(2)}, u32[]{:S(2)}) collective-permute-start(f32[3,4,1024]{2,1,0:T(4,128)} %bitcast.31), channel_id=1, source_target_pairs={{0,460},{1,396},{2,332},{3,268},{4,204},{5,140},{6,76},{7,12},{8,0... | collective-permute-start | bytes 147464 | tf_op jit(solution)/shard_map/ppermute | solution.py:509
  19.3 5.7 %copy-start = (f32[4,3,1024]{2,0,1:T(4,128)S(1)}, f32[4,3,1024]{2,0,1:T(4,128)}, u32[]{:S(2)}) copy-start(f32[4,3,1024]{2,0,1:T(4,128)} %param.7) | copy-start | bytes 147460
  19.3 5.7 %copy-start.2 = (f32[1024]{0:T(1024)S(1)}, f32[1024]{0:T(1024)}, u32[]{:S(2)}) copy-start(f32[1024]{0:T(1024)} %param.9) | copy-start | bytes 12292
  19.3 5.7 %copy-start.3 = (f32[1024]{0:T(1024)S(1)}, f32[1024]{0:T(1024)}, u32[]{:S(2)}) copy-start(f32[1024]{0:T(1024)} %param.10) | copy-start | bytes 12292
  19.3 27.8 %all-to-all-start = ((f32[16,24,128]{2,1,0:T(8,128)}), f32[16,24,128]{2,1,0:T(8,128)S(1)}, u32[]{:S(2)}, u32[]{:S(2)}) async-start(f32[16,24,128]{2,1,0:T(8,128)} %bitcast.5), calls=%async_computation | async-start | bytes 393216 | tf_op jit(solution)/shard_map/all_to_all | solution.py:504
  25.0 0.7 copy-start.1
  25.7 17.2 %collective-permute-start = (f32[120,128]{1,0:T(8,128)S(1)}, f32[120,128]{1,0:T(8,128)S(1)}, u32[]{:S(2)}, u32[]{:S(2)}) collective-permute-start(f32[120,128]{1,0:T(8,128)S(1)} %shard_map.77), channel_id=1, source_target_pairs={{0,460},{1,396},{2,332},{3,268},{4,204},{5,140},{6,76},{7,12},{8,0... | collective-permute-start | bytes 184328 | tf_op jit(solution)/shard_map/ppermute | solution.py:509
  47.2 8.0 %collective-permute-start.2 = (f32[88,128]{1,0:T(8,128)S(1)}, f32[88,128]{1,0:T(8,128)S(1)}, u32[]{:S(2)}, u32[]{:S(2)}) collective-permute-start(f32[88,128]{1,0:T(8,128)S(1)} %get-tuple-element.58), channel_id=1, source_target_pairs={{460,396},{396,332},{332,268},{268,204},{204,140},{140,76},{76,12}... | collective-permute-start | bytes 135176 | tf_op jit(solution)/shard_map/ppermute | solution.py:509
  52.0 5.9 %collective-permute-start.3 = (f32[88,128]{1,0:T(8,128)S(1)}, f32[88,128]{1,0:T(8,128)S(1)}, u32[]{:S(2)}, u32[]{:S(2)}) collective-permute-start(f32[88,128]{1,0:T(8,128)S(1)} %get-tuple-element.59), channel_id=1, source_target_pairs={{460,28},{396,460},{332,396},{268,332},{204,268},{140,204},{76,140... | collective-permute-start | bytes 135176 | tf_op jit(solution)/shard_map/ppermute | solution.py:509
  60.3 18.7 %all-to-all-start.1 = ((f32[16,24,128]{2,1,0:T(8,128)}), f32[16,24,128]{2,1,0:T(8,128)S(1)}, u32[]{:S(2)}, u32[]{:S(2)}) async-start(f32[16,24,128]{2,1,0:T(8,128)} %bitcast.7), calls=%async_computation.1 | async-start | bytes 393216 | tf_op jit(solution)/shard_map/all_to_all | solution.py:504
  65.3 5.6 %collective-permute-start.4 = (f32[24,128]{1,0:T(8,128)S(1)}, f32[24,128]{1,0:T(8,128)S(1)}, u32[]{:S(2)}, u32[]{:S(2)}) collective-permute-start(f32[24,128]{1,0:T(8,128)S(1)} %get-tuple-element.61), channel_id=1, source_target_pairs={{460,488},{396,424},{332,360},{268,296},{204,232},{140,168},{76,10... | collective-permute-start | bytes 36872 | tf_op jit(solution)/shard_map/ppermute | solution.py:509
  74.0 5.0 %collective-permute-start.5 = (f32[24,128]{1,0:T(8,128)S(1)}, f32[24,128]{1,0:T(8,128)S(1)}, u32[]{:S(2)}, u32[]{:S(2)}) collective-permute-start(f32[24,128]{1,0:T(8,128)S(1)} %get-tuple-element.65), channel_id=1, source_target_pairs={{460,488},{396,424},{332,360},{268,296},{204,232},{140,168},{76,10... | collective-permute-start | bytes 36872 | tf_op jit(solution)/shard_map/ppermute | solution.py:509
  79.7 10.8 %collective-permute-start.6 = (f32[48,128]{1,0:T(8,128)S(1)}, f32[48,128]{1,0:T(8,128)S(1)}, u32[]{:S(2)}, u32[]{:S(2)}) collective-permute-start(f32[48,128]{1,0:T(8,128)S(1)} %get-tuple-element.68), channel_id=1, source_target_pairs={{460,396},{396,332},{332,268},{268,204},{204,140},{140,76},{76,12}... | collective-permute-start | bytes 73736 | tf_op jit(solution)/shard_map/ppermute | solution.py:509
  83.5 7.0 %collective-permute-start.7 = (f32[48,128]{1,0:T(8,128)S(1)}, f32[48,128]{1,0:T(8,128)S(1)}, u32[]{:S(2)}, u32[]{:S(2)}) collective-permute-start(f32[48,128]{1,0:T(8,128)S(1)} %get-tuple-element.69), channel_id=1, source_target_pairs={{460,28},{396,460},{332,396},{268,332},{204,268},{140,204},{76,140... | collective-permute-start | bytes 73736 | tf_op jit(solution)/shard_map/ppermute | solution.py:509
  94.3 11.4 %all-to-all-start.2 = ((f32[16,24,128]{2,1,0:T(8,128)}), f32[16,24,128]{2,1,0:T(8,128)S(1)}, u32[]{:S(2)}, u32[]{:S(2)}) async-start(f32[16,24,128]{2,1,0:T(8,128)} %bitcast.9), calls=%async_computation.2 | async-start | bytes 393216 | tf_op jit(solution)/shard_map/all_to_all | solution.py:504
  105.8 7.8 %collective-permute-start.8 = (f32[72,128]{1,0:T(8,128)S(1)}, f32[72,128]{1,0:T(8,128)S(1)}, u32[]{:S(2)}, u32[]{:S(2)}) collective-permute-start(f32[72,128]{1,0:T(8,128)S(1)} %get-tuple-element.78), channel_id=1, source_target_pairs={{460,396},{396,332},{332,268},{268,204},{204,140},{140,76},{76,12}... | collective-permute-start | bytes 110600 | tf_op jit(solution)/shard_map/ppermute | solution.py:509
  109.3 5.0 %collective-permute-start.9 = (f32[72,128]{1,0:T(8,128)S(1)}, f32[72,128]{1,0:T(8,128)S(1)}, u32[]{:S(2)}, u32[]{:S(2)}) collective-permute-start(f32[72,128]{1,0:T(8,128)S(1)} %get-tuple-element.79), channel_id=1, source_target_pairs={{460,28},{396,460},{332,396},{268,332},{204,268},{140,204},{76,140... | collective-permute-start | bytes 110600 | tf_op jit(solution)/shard_map/ppermute | solution.py:509
  116.7 19.0 %all-to-all-start.3 = ((f32[16,24,128]{2,1,0:T(8,128)}), f32[16,24,128]{2,1,0:T(8,128)S(1)}, u32[]{:S(2)}, u32[]{:S(2)}) async-start(f32[16,24,128]{2,1,0:T(8,128)} %bitcast.11), calls=%async_computation.3 | async-start | bytes 393216 | tf_op jit(solution)/shard_map/all_to_all | solution.py:504
  122.0 5.6 %collective-permute-start.10 = (f32[24,128]{1,0:T(8,128)S(1)}, f32[24,128]{1,0:T(8,128)S(1)}, u32[]{:S(2)}, u32[]{:S(2)}) collective-permute-start(f32[24,128]{1,0:T(8,128)S(1)} %get-tuple-element.81), channel_id=1, source_target_pairs={{460,488},{396,424},{332,360},{268,296},{204,232},{140,168},{76,10... | collective-permute-start | bytes 36872 | tf_op jit(solution)/shard_map/ppermute | solution.py:509
  130.7 5.0 %collective-permute-start.11 = (f32[24,128]{1,0:T(8,128)S(1)}, f32[24,128]{1,0:T(8,128)S(1)}, u32[]{:S(2)}, u32[]{:S(2)}) collective-permute-start(f32[24,128]{1,0:T(8,128)S(1)} %get-tuple-element.85), channel_id=1, source_target_pairs={{460,488},{396,424},{332,360},{268,296},{204,232},{140,168},{76,10... | collective-permute-start | bytes 36872 | tf_op jit(solution)/shard_map/ppermute | solution.py:509
  136.4 10.8 %collective-permute-start.12 = (f32[48,128]{1,0:T(8,128)S(1)}, f32[48,128]{1,0:T(8,128)S(1)}, u32[]{:S(2)}, u32[]{:S(2)}) collective-permute-start(f32[48,128]{1,0:T(8,128)S(1)} %get-tuple-element.88), channel_id=1, source_target_pairs={{460,396},{396,332},{332,268},{268,204},{204,140},{140,76},{76,12}... | collective-permute-start | bytes 73736 | tf_op jit(solution)/shard_map/ppermute | solution.py:509
  140.0 7.1 %collective-permute-start.13 = (f32[48,128]{1,0:T(8,128)S(1)}, f32[48,128]{1,0:T(8,128)S(1)}, u32[]{:S(2)}, u32[]{:S(2)}) collective-permute-start(f32[48,128]{1,0:T(8,128)S(1)} %get-tuple-element.89), channel_id=1, source_target_pairs={{460,28},{396,460},{332,396},{268,332},{204,268},{140,204},{76,140... | collective-permute-start | bytes 73736 | tf_op jit(solution)/shard_map/ppermute | solution.py:509
  151.0 11.4 %all-to-all-start.4 = ((f32[16,24,128]{2,1,0:T(8,128)}), f32[16,24,128]{2,1,0:T(8,128)S(1)}, u32[]{:S(2)}, u32[]{:S(2)}) async-start(f32[16,24,128]{2,1,0:T(8,128)} %bitcast.14), calls=%async_computation.4 | async-start | bytes 393216 | tf_op jit(solution)/shard_map/all_to_all | solution.py:504
  162.5 8.0 %collective-permute-start.15 = (f32[72,128]{1,0:T(8,128)S(1)}, f32[72,128]{1,0:T(8,128)S(1)}, u32[]{:S(2)}, u32[]{:S(2)}) collective-permute-start(f32[72,128]{1,0:T(8,128)S(1)} %get-tuple-element.99), channel_id=1, source_target_pairs={{460,396},{396,332},{332,268},{268,204},{204,140},{140,76},{76,12}... | collective-permute-start | bytes 110600 | tf_op jit(solution)/shard_map/ppermute | solution.py:509
  166.2 5.7 %collective-permute-start.16 = (f32[72,128]{1,0:T(8,128)S(1)}, f32[72,128]{1,0:T(8,128)S(1)}, u32[]{:S(2)}, u32[]{:S(2)}) collective-permute-start(f32[72,128]{1,0:T(8,128)S(1)} %get-tuple-element.100), channel_id=1, source_target_pairs={{460,28},{396,460},{332,396},{268,332},{204,268},{140,204},{76,140... | collective-permute-start | bytes 110600 | tf_op jit(solution)/shard_map/ppermute | solution.py:509
  174.4 17.1 %all-to-all-start.5 = ((f32[16,24,128]{2,1,0:T(8,128)}), f32[16,24,128]{2,1,0:T(8,128)S(1)}, u32[]{:S(2)}, u32[]{:S(2)}) async-start(f32[16,24,128]{2,1,0:T(8,128)} %bitcast.16), calls=%async_computation.5 | async-start | bytes 393216 | tf_op jit(solution)/shard_map/all_to_all | solution.py:504
  179.6 8.7 %collective-permute-start.17 = (f32[24,128]{1,0:T(8,128)S(1)}, f32[24,128]{1,0:T(8,128)S(1)}, u32[]{:S(2)}, u32[]{:S(2)}) collective-permute-start(f32[24,128]{1,0:T(8,128)S(1)} %get-tuple-element.102), channel_id=1, source_target_pairs={{460,488},{396,424},{332,360},{268,296},{204,232},{140,168},{76,10... | collective-permute-start | bytes 36872 | tf_op jit(solution)/shard_map/ppermute | solution.py:509
  183.1 25.4 %collective-permute-start.14 = (f32[3,4,1024]{2,1,0:T(4,128)S(1)}, f32[3,4,1024]{2,1,0:T(4,128)S(1)}, u32[]{:S(2)}, u32[]{:S(2)}) collective-permute-start(f32[3,4,1024]{2,1,0:T(4,128)S(1)} %get-tuple-element.92), channel_id=1, source_target_pairs={{460,0},{396,1},{332,2},{268,3},{204,4},{140,5},{76,6},{12,7},{0,8... | collective-permute-start | bytes 147464 | tf_op jit(solution)/shard_map/ppermute | solution.py:612
  192.1 19.2 %collective-permute-start.18 = (f32[3,4,1024]{2,1,0:T(4,128)S(1)}, f32[3,4,1024]{2,1,0:T(4,128)S(1)}, u32[]{:S(2)}, u32[]{:S(2)}) collective-permute-start(f32[3,4,1024]{2,1,0:T(4,128)S(1)} %shard_map.100), channel_id=1, source_target_pairs={{460,0},{396,1},{332,2},{268,3},{204,4},{140,5},{76,6},{12,7},{0,8... | collective-permute-start | bytes 147464 | tf_op jit(solution)/shard_map/ppermute | solution.py:613

commit v2 on v1

--- a/solution.py
+++ b/solution.py
@@ -288,10 +288,10 @@
     out_ref[Q_ROW : Q_ROW + 8, :] = q_ref[...]
 
 
-def unpack(value_ref, out_ref):
+def unpack(value_ref, out_ref, base):
     for k in range(3):
         for block in range(8):
-            out_ref[k, :, 128 * block : 128 * block + 128] = value_ref[pl.ds(8 * k + block, 4, stride=24), :]
+            out_ref[base + k, :, 128 * block : 128 * block + 128] = value_ref[pl.ds(8 * k + block, 4, stride=24), :]
 
 
 def start_kernel(cols_ref, x_ref, y_ref, up_ref, down_ref, inner_ref, outer_ref, part_ref):
@@ -363,13 +363,9 @@
         emit_edges(first, last, rest[0], rest[1], core)
 
 
-def near_fast_kernel(last, cols_ref, p_ref, y_ref, v_ref, r_ref, left, right, wide_l, wide_r, before, after, *rest):
-    if last:
-        first_ref, vo_ref, yo_ref, up_ref, down_ref, in_ref, ou_ref, part_ref, moved_ref = rest[:9]
-        scr = rest[9:]
-    else:
-        vo_ref, yo_ref, up_ref, down_ref, in_ref, ou_ref, part_ref = rest[:7]
-        scr = rest[7:]
+def near_fast_kernel(cols_ref, p_ref, y_ref, v_ref, r_ref, left, right, wide_l, wide_r, before, after, *rest):
+    vo_ref, yo_ref, up_ref, down_ref, in_ref, ou_ref, part_ref = rest[:7]
+    scr = rest[7:]
 
     def store(r, y, v):
         vo_ref[pl.ds(r, 8), :] = v
@@ -380,10 +376,6 @@
     emit(yo_ref, up_ref, down_ref)
     emit_edges(yo_ref[0:24, :], yo_ref[72:96, :], in_ref, ou_ref, cols_ref[0, CORE_AT])
     emit_partial(yo_ref, cols_ref, part_ref)
-    if last:
-        rows = scr[-1]
-        rows[...] = yo_ref[...] - first_ref[...]
-        unpack(rows, moved_ref)
 
 
 def gather_kernel(wide, recv_ref, up_ref, down_ref, p_ref, yc_ref, up_out, down_out):
@@ -463,10 +455,13 @@
         out[...] = edges[e] + inverse * total
 
 
-def final_kernel(rate, cols_ref, p_ref, v_ref, far_ref, out_ref, rows):
+def final_kernel(rate, cols_ref, p_ref, v_ref, y_ref, first_ref, far_ref, out_ref, rows):
+    for i in range(12):
+        rows[8 * i : 8 * i + 8, :] = y_ref[8 * i : 8 * i + 8, :] - first_ref[8 * i : 8 * i + 8, :]
+    unpack(rows, out_ref, 0)
     for b, v in enumerate(kick(rate, cols_ref, p_ref, v_ref, far_ref)):
         rows[24 * b : 24 * b + 24, :] = v
-    unpack(rows, out_ref)
+    unpack(rows, out_ref, 3)
 
 
 def call(kernel, outs, cols, args, scratch=(), flops=1000, order=(), passed=()):
@@ -497,7 +492,7 @@
 BEAD = (24, 128)
 STATE = (96, 128)
 TEAM_ROWS = (16, 24, 128)
-PLAIN = (3, 4, 1024)
+BOTH = (6, 4, 1024)
 
 
 def exchange_team(x):
@@ -542,22 +537,14 @@
             left = send(up, SLAB_UP)
             right = send(down, SLAB_DOWN)
             (sums,) = call(near_own_kernel, [(128, 128)], None, [y, p], SCRATCH, big)
-            last = stage == 3
-
-            def near_fast(*refs, last=last):
-                near_fast_kernel(last, *refs)
-
-            result = call(
-                near_fast,
-                [STATE, STATE, HALO, HALO, BEAD, BEAD, (384, 128)] + [PLAIN] * last,
+            v, y, up, down, inner, outer, part = call(
+                near_fast_kernel,
+                [STATE, STATE, HALO, HALO, BEAD, BEAD, (384, 128)],
                 cols,
-                [p, y, v, sums, left, right, wide_l, wide_r, before, after] + [first] * last,
-                SCRATCH + [CHAIN] + [pltpu.VMEM(STATE, f32)] * last,
+                [p, y, v, sums, left, right, wide_l, wide_r, before, after],
+                SCRATCH + [CHAIN],
                 big // 2,
             )
-            v, y, up, down, inner, outer, part = result[:7]
-            if last:
-                moved = result[7]
             continue
         edge = stage in (0, 4)
         got = exchange_team(part)
@@ -598,7 +585,7 @@
             def final(*refs, rate=rate):
                 final_kernel(rate, *refs)
 
-            (v,) = call(final, [PLAIN], cols, [p, v, far], [pltpu.VMEM(STATE, f32)])
+            (both,) = call(final, [BOTH], cols, [p, v, y, first, far], [pltpu.VMEM(STATE, f32)])
         else:
 
             def update(*refs, rate=rate):
@@ -609,9 +596,8 @@
             v, y, up, down, before, after = call(
                 update, [STATE, STATE, HALO, HALO, BEAD, BEAD], cols, [p, y, v, far, inner, outer]
             )
-    moved = lax.ppermute(moved, AXES, MOVE_OUT)
-    speeds = lax.ppermute(v, AXES, MOVE_OUT)
-    return jnp.transpose(moved, (1, 0, 2)), jnp.transpose(speeds, (1, 0, 2))
+    both = jnp.transpose(lax.ppermute(both, AXES, MOVE_OUT), (1, 0, 2))
+    return both[:, 0:3], both[:, 3:6]
 
 
 def solution(mesh):

time: 216 us -> 213 us (0.986)
  the two profiles are of different devices: /device:TPU:1 before, /device:TPU:19 now
where the time goes in v2:
time: 213 us; the launch traced here: 212 us
  starting transfers between devices  107 us (50%)
  Pallas kernels  52.6 us (25%)
  waiting for transfers between devices  38.7 us (18%)
  blocking collectives  10.9 us (5%)
    pallas_call x24, Pallas kernels, call(): pl.pallas_call(body, out_shape=shapes, in_specs=specs, out_specs=[pl.Bloc...  52.6 us
    all_to_all x6, starting transfers between devices, exchange_team(): lax.all_to_all(x.reshape(TEAM_ROWS), TEAM, split_axis=0, concat_axis=0, t...  49.8 us
    ppermute x17, starting transfers between devices, send(): return lax.ppermute(x, AXES, moves)  49.3 us
    ppermute x17, waiting for transfers between devices, send(): return lax.ppermute(x, AXES, moves)  22.7 us
    ppermute x1, waiting for transfers between devices, shards(): both = jnp.transpose(lax.ppermute(both, AXES, MOVE_OUT), (1, 0, 2))  16 us
    all_gather x5, blocking collectives, pair(): return lax.all_gather(x, 'core', axis=0, tiled=True)  10.9 us
    ppermute x1, starting transfers between devices, shards(): both = jnp.transpose(lax.ppermute(both, AXES, MOVE_OUT), (1, 0, 2))  7.63 us
  transfers between devices with their start and end apart: 24, of which 11 were waited for; matrix products, arithmetic and copies ran while one was open for 0% of the time, Pallas kernels for 16%

profile of v2, /device:TPU:19, one launch (start us, length us, event | category | flops | bytes accessed | tf_op | source)
XLA Modules:
  0.0 211.8 jit_solution(6939970278997696782)
XLA Ops:
  0.6 4.9 %collective-permute-start.1 = (f32[3,4,1024]{2,1,0:T(4,128)}, f32[3,4,1024]{2,1,0:T(4,128)S(1)}, u32[]{:S(2)}, u32[]{:S(2)}) collective-permute-start(f32[3,4,1024]{2,1,0:T(4,128)} %bitcast.29), channel_id=1, source_target_pairs={{0,460},{1,396},{2,332},{3,268},{4,204},{5,140},{6,76},{7,12},{8,0... | collective-permute-start | bytes 147464 | tf_op jit(solution)/shard_map/ppermute | solution.py:504
  5.5 0.7 constant_dynamic-slice_fusion.refs_0_
  6.2 7.6 %collective-permute-done.1.refs_1_ = f32[3,4,1024]{2,1,0:T(4,128)S(1)} collective-permute-done((f32[3,4,1024]{2,1,0:T(4,128)}, f32[3,4,1024]{2,1,0:T(4,128)S(1)}, u32[]{:S(2)}, u32[]{:S(2)}) %collective-permute-start.1) | collective-permute-done | bytes 49184 | tf_op jit(solution)/shard_map/ppermute | solution.py:504
  13.8 1.3 shard_map.78
  15.1 9.0 %all-to-all-start = ((f32[16,24,128]{2,1,0:T(8,128)}), f32[16,24,128]{2,1,0:T(8,128)S(1)}, u32[]{:S(2)}, u32[]{:S(2)}) async-start(f32[16,24,128]{2,1,0:T(8,128)} %bitcast.5), calls=%async_computation | async-start | bytes 393216 | tf_op jit(solution)/shard_map/all_to_all | solution.py:499
  24.1 0.6 copy-done.1
  24.8 4.0 %collective-permute-start = (f32[120,128]{1,0:T(8,128)S(1)}, f32[120,128]{1,0:T(8,128)S(1)}, u32[]{:S(2)}, u32[]{:S(2)}) collective-permute-start(f32[120,128]{1,0:T(8,128)S(1)} %shard_map.77), channel_id=1, source_target_pairs={{0,460},{1,396},{2,332},{3,268},{4,204},{5,140},{6,76},{7,12},{8,0... | collective-permute-start | bytes 184328 | tf_op jit(solution)/shard_map/ppermute | solution.py:504
  28.8 9.2 %collective-permute-done.refs_1_.refs_3_ = f32[120,128]{1,0:T(8,128)S(1)} collective-permute-done((f32[120,128]{1,0:T(8,128)S(1)}, f32[120,128]{1,0:T(8,128)S(1)}, u32[]{:S(2)}, u32[]{:S(2)}) %collective-permute-start) | collective-permute-done | bytes 61472 | tf_op jit(solution)/shard_map/ppermute | solution.py:504
  38.0 4.3 %shard_map.79.refs_4_ = f32[128,128]{1,0:T(8,128)S(1)} custom-call(f32[96,128]{1,0:T(8,128)S(1)} %get-tuple-element.52.refs_0_.refs_2_.refs_4_, f32[120,128]{1,0:T(8,128)S(1)} %collective-permute-done.refs_1_.refs_3_), custom_call_target="tpu_custom_call" | custom-call | flops 400000000 | bytes 400000 | tf_op jit(solution)/shard_map/pallas_call | solution.py:479
  42.3 1.9 collective-permute-start.2
  44.2 3.4 %collective-permute-start.3 = (f32[88,128]{1,0:T(8,128)S(1)}, f32[88,128]{1,0:T(8,128)S(1)}, u32[]{:S(2)}, u32[]{:S(2)}) collective-permute-start(f32[88,128]{1,0:T(8,128)S(1)} %get-tuple-element.58), channel_id=1, source_target_pairs={{460,28},{396,460},{332,396},{268,332},{204,268},{140,204},{76,140... | collective-permute-start | bytes 135176 | tf_op jit(solution)/shard_map/ppermute | solution.py:504
  47.6 1.2 shard_map.82.refs_2_
  48.8 0.2 collective-permute-done.3.refs_6_.refs_8_.refs_4_
  49.0 2.4 %shard_map.83 = f32[384,128]{1,0:T(8,128)} custom-call(f32[24,128]{1,0:T(8,128)S(1)} %get-tuple-element.62.refs_0_, f32[120,128]{1,0:T(8,128)S(1)} %collective-permute-done.refs_1_.refs_3_, f32[32,128]{1,0:T(8,128)S(1)} %shard_map.82.refs_2_, f32[88,128]{1,0:T(8,128)S(1)} %collective-permute-done.2.refs_5_.refs_7_.refs_3_, ...), custom_call_target="tpu_custom_call" | custom-call | flops 100000000 | bytes 400000 | tf_op jit(solution)/shard_map/pallas_call | solution.py:479
  51.4 13.0 %all-to-all-start.1 = ((f32[16,24,128]{2,1,0:T(8,128)}), f32[16,24,128]{2,1,0:T(8,128)S(1)}, u32[]{:S(2)}, u32[]{:S(2)}) async-start(f32[16,24,128]{2,1,0:T(8,128)} %bitcast.7), calls=%async_computation.1 | async-start | bytes 393216 | tf_op jit(solution)/shard_map/all_to_all | solution.py:499
  64.4 2.4 %collective-permute-start.4 = (f32[24,128]{1,0:T(8,128)S(1)}, f32[24,128]{1,0:T(8,128)S(1)}, u32[]{:S(2)}, u32[]{:S(2)}) collective-permute-start(f32[24,128]{1,0:T(8,128)S(1)} %get-tuple-element.60), channel_id=1, source_target_pairs={{460,488},{396,424},{332,360},{268,296},{204,232},{140,168},{76,10... | collective-permute-start | bytes 36872 | tf_op jit(solution)/shard_map/ppermute | solution.py:504
  66.9 2.2 %all_gather.15.refs_9_ = f32[48,128]{1,0:T(8,128)S(1)} all-gather(f32[24,128]{1,0:T(8,128)S(1)} %get-tuple-element.59), channel_id=1, replica_groups=mesh['z2'=2,'z1'=2,'z0'=2,'core'=2,'zh'=2,'x1'=2,'x0'=2,'y1'=2,'y0'=2] {..., dimensions={0}, use_global_device_ids=true | all-gather | bytes 36864 | tf_op jit(solution)/shard_map/all_gather | solution.py:508
  69.1 0.3 collective-permute-done.4.refs_10_
  69.4 3.1 %shard_map.81 = (f32[96,128]{1,0:T(8,128)S(1)}, f32[24,128]{1,0:T(8,128)S(1)}, f32[24,128]{1,0:T(8,128)S(1)}) custom-call(f32[1,128]{1,0:T(1,128)S(1)} %constant_dynamic-slice_fusion.refs_0_, f32[120,128]{1,0:T(8,128)S(1)} %collective-permute-done.refs_1_.refs_3_, f32[96,128]{1,0:T(8,128)S(1)} %get-tuple-element.52.refs_0_.refs_2_.refs_4_, ...), custom_call_target="tpu_custom_call" | custom-call | flops 200000000 | bytes 400000 | tf_op jit(solution)/shard_map/pallas_call | solution.py:479
  72.6 2.6 %collective-permute-start.5 = (f32[24,128]{1,0:T(8,128)S(1)}, f32[24,128]{1,0:T(8,128)S(1)}, u32[]{:S(2)}, u32[]{:S(2)}) collective-permute-start(f32[24,128]{1,0:T(8,128)S(1)} %get-tuple-element.64), channel_id=1, source_target_pairs={{460,488},{396,424},{332,360},{268,296},{204,232},{140,168},{76,10... | collective-permute-start | bytes 36872 | tf_op jit(solution)/shard_map/ppermute | solution.py:504
  75.2 2.1 all_gather.16.refs_5_
  77.3 0.3 collective-permute-done.5.refs_6_
  77.6 0.7 shard_map.84
  78.2 3.8 %collective-permute-start.6 = (f32[48,128]{1,0:T(8,128)S(1)}, f32[48,128]{1,0:T(8,128)S(1)}, u32[]{:S(2)}, u32[]{:S(2)}) collective-permute-start(f32[48,128]{1,0:T(8,128)S(1)} %get-tuple-element.67), channel_id=1, source_target_pairs={{460,396},{396,332},{332,268},{268,204},{204,140},{140,76},{76,12}... | collective-permute-start | bytes 73736 | tf_op jit(solution)/shard_map/ppermute | solution.py:504
  82.0 1.9 collective-permute-start.7
  84.0 4.3 %shard_map.85.refs_4_ = f32[128,128]{1,0:T(8,128)S(1)} custom-call(f32[96,128]{1,0:T(8,128)S(1)} %get-tuple-element.65.refs_0_.refs_2_, f32[120,128]{1,0:T(8,128)S(1)} %collective-permute-done.refs_1_.refs_3_), custom_call_target="tpu_custom_call" | custom-call | flops 400000000 | bytes 400000 | tf_op jit(solution)/shard_map/pallas_call | solution.py:479
  88.2 3.9 %shard_map.86 = (f32[96,128]{1,0:T(8,128)S(1)}, f32[96,128]{1,0:T(8,128)S(1)}, f32[48,128]{1,0:T(8,128)S(1)}, f32[48,128]{1,0:T(8,128)S(1)}, f32[24,128]{1,0:T(8...) custom-call(f32[1,128]{1,0:T(1,128)S(1)} %constant_dynamic-slice_fusion.refs_0_, ...), custom_call_target="tpu_custom_call" | custom-call | flops 200000000 | bytes 400000 | tf_op jit(solution)/shard_map/pallas_call | solution.py:479
  92.1 6.1 %all-to-all-start.2 = ((f32[16,24,128]{2,1,0:T(8,128)}), f32[16,24,128]{2,1,0:T(8,128)S(1)}, u32[]{:S(2)}, u32[]{:S(2)}) async-start(f32[16,24,128]{2,1,0:T(8,128)} %bitcast.9), calls=%async_computation.2 | async-start | bytes 393216 | tf_op jit(solution)/shard_map/all_to_all | solution.py:499
  98.2 4.3 %shard_map.87.refs_4_ = f32[128,128]{1,0:T(8,128)S(1)} custom-call(f32[96,128]{1,0:T(8,128)S(1)} %get-tuple-element.71.refs_0_.refs_2_, f32[120,128]{1,0:T(8,128)S(1)} %collective-permute-done.refs_1_.refs_3_), custom_call_target="tpu_custom_call" | custom-call | flops 400000000 | bytes 400000 | tf_op jit(solution)/shard_map/pallas_call | solution.py:479
  102.5 3.5 %collective-permute-start.8 = (f32[72,128]{1,0:T(8,128)S(1)}, f32[72,128]{1,0:T(8,128)S(1)}, u32[]{:S(2)}, u32[]{:S(2)}) collective-permute-start(f32[72,128]{1,0:T(8,128)S(1)} %get-tuple-element.77), channel_id=1, source_target_pairs={{460,396},{396,332},{332,268},{268,204},{204,140},{140,76},{76,12}... | collective-permute-start | bytes 110600 | tf_op jit(solution)/shard_map/ppermute | solution.py:504
  106.0 1.9 collective-permute-start.9
  108.0 1.2 shard_map.90.refs_2_
  109.2 0.0 collective-permute-done.8.refs_5_.refs_3_
  109.2 1.8 collective-permute-done.9.refs_6_.refs_4_
  111.0 2.4 %shard_map.91 = f32[384,128]{1,0:T(8,128)} custom-call(f32[24,128]{1,0:T(8,128)S(1)} %get-tuple-element.82.refs_0_, f32[120,128]{1,0:T(8,128)S(1)} %collective-permute-done.refs_1_.refs_3_, f32[32,128]{1,0:T(8,128)S(1)} %shard_map.90.refs_2_, f32[72,128]{1,0:T(8,128)S(1)} %collective-permute-done.8.refs_5_.refs_3_, ...), custom_call_target="tpu_custom_call" | custom-call | flops 100000000 | bytes 400000 | tf_op jit(solution)/shard_map/pallas_call | solution.py:479
  113.4 7.7 %all-to-all-start.3 = ((f32[16,24,128]{2,1,0:T(8,128)}), f32[16,24,128]{2,1,0:T(8,128)S(1)}, u32[]{:S(2)}, u32[]{:S(2)}) async-start(f32[16,24,128]{2,1,0:T(8,128)} %bitcast.11), calls=%async_computation.3 | async-start | bytes 393216 | tf_op jit(solution)/shard_map/all_to_all | solution.py:499
  121.2 2.4 %collective-permute-start.10 = (f32[24,128]{1,0:T(8,128)S(1)}, f32[24,128]{1,0:T(8,128)S(1)}, u32[]{:S(2)}, u32[]{:S(2)}) collective-permute-start(f32[24,128]{1,0:T(8,128)S(1)} %get-tuple-element.80), channel_id=1, source_target_pairs={{460,488},{396,424},{332,360},{268,296},{204,232},{140,168},{76,10... | collective-permute-start | bytes 36872 | tf_op jit(solution)/shard_map/ppermute | solution.py:504
  123.6 2.2 %all_gather.17.refs_9_ = f32[48,128]{1,0:T(8,128)S(1)} all-gather(f32[24,128]{1,0:T(8,128)S(1)} %get-tuple-element.79), channel_id=1, replica_groups=mesh['z2'=2,'z1'=2,'z0'=2,'core'=2,'zh'=2,'x1'=2,'x0'=2,'y1'=2,'y0'=2] {..., dimensions={0}, use_global_device_ids=true | all-gather | bytes 36864 | tf_op jit(solution)/shard_map/all_gather | solution.py:508
  125.8 0.3 collective-permute-done.10.refs_10_
  126.2 3.1 %shard_map.89 = (f32[96,128]{1,0:T(8,128)S(1)}, f32[24,128]{1,0:T(8,128)S(1)}, f32[24,128]{1,0:T(8,128)S(1)}) custom-call(f32[1,128]{1,0:T(1,128)S(1)} %constant_dynamic-slice_fusion.refs_0_, f32[120,128]{1,0:T(8,128)S(1)} %collective-permute-done.refs_1_.refs_3_, f32[96,128]{1,0:T(8,128)S(1)} %get-tuple-element.71.refs_0_.refs_2_, ...), custom_call_target="tpu_custom_call" | custom-call | flops 200000000 | bytes 400000 | tf_op jit(solution)/shard_map/pallas_call | solution.py:479
  129.3 2.6 %collective-permute-start.11 = (f32[24,128]{1,0:T(8,128)S(1)}, f32[24,128]{1,0:T(8,128)S(1)}, u32[]{:S(2)}, u32[]{:S(2)}) collective-permute-start(f32[24,128]{1,0:T(8,128)S(1)} %get-tuple-element.84), channel_id=1, source_target_pairs={{460,488},{396,424},{332,360},{268,296},{204,232},{140,168},{76,10... | collective-permute-start | bytes 36872 | tf_op jit(solution)/shard_map/ppermute | solution.py:504
  131.9 2.1 all_gather.18.refs_5_
  134.0 0.3 collective-permute-done.11.refs_6_
  134.3 0.7 shard_map.92
  135.0 3.6 %collective-permute-start.12 = (f32[48,128]{1,0:T(8,128)S(1)}, f32[48,128]{1,0:T(8,128)S(1)}, u32[]{:S(2)}, u32[]{:S(2)}) collective-permute-start(f32[48,128]{1,0:T(8,128)S(1)} %get-tuple-element.87), channel_id=1, source_target_pairs={{460,396},{396,332},{332,268},{268,204},{204,140},{140,76},{76,12}... | collective-permute-start | bytes 73736 | tf_op jit(solution)/shard_map/ppermute | solution.py:504
  138.6 1.9 collective-permute-start.13
  140.5 4.3 %shard_map.93.refs_4_ = f32[128,128]{1,0:T(8,128)S(1)} custom-call(f32[96,128]{1,0:T(8,128)S(1)} %get-tuple-element.85.refs_0_.refs_2_, f32[120,128]{1,0:T(8,128)S(1)} %collective-permute-done.refs_1_.refs_3_), custom_call_target="tpu_custom_call" | custom-call | flops 400000000 | bytes 400000 | tf_op jit(solution)/shard_map/pallas_call | solution.py:479
  144.8 3.9 %shard_map.94 = (f32[96,128]{1,0:T(8,128)S(1)}, f32[96,128]{1,0:T(8,128)S(1)}, f32[48,128]{1,0:T(8,128)S(1)}, f32[48,128]{1,0:T(8,128)S(1)}, f32[24,128]{1,0:T(8...) custom-call(f32[1,128]{1,0:T(1,128)S(1)} %constant_dynamic-slice_fusion.refs_0_, ...), custom_call_target="tpu_custom_call" | custom-call | flops 200000000 | bytes 400000 | tf_op jit(solution)/shard_map/pallas_call | solution.py:479
  148.7 6.2 %all-to-all-start.4 = ((f32[16,24,128]{2,1,0:T(8,128)}), f32[16,24,128]{2,1,0:T(8,128)S(1)}, u32[]{:S(2)}, u32[]{:S(2)}) async-start(f32[16,24,128]{2,1,0:T(8,128)} %bitcast.13), calls=%async_computation.4 | async-start | bytes 393216 | tf_op jit(solution)/shard_map/all_to_all | solution.py:499
  154.9 4.3 %shard_map.95.refs_4_ = f32[128,128]{1,0:T(8,128)S(1)} custom-call(f32[96,128]{1,0:T(8,128)S(1)} %get-tuple-element.91.refs_0_.refs_2_.refs_3_, f32[120,128]{1,0:T(8,128)S(1)} %collective-permute-done.refs_1_.refs_3_), custom_call_target="tpu_custom_call" | custom-call | flops 400000000 | bytes 400000 | tf_op jit(solution)/shard_map/pallas_call | solution.py:479
  159.2 3.7 %collective-permute-start.14 = (f32[72,128]{1,0:T(8,128)S(1)}, f32[72,128]{1,0:T(8,128)S(1)}, u32[]{:S(2)}, u32[]{:S(2)}) collective-permute-start(f32[72,128]{1,0:T(8,128)S(1)} %get-tuple-element.97), channel_id=1, source_target_pairs={{460,396},{396,332},{332,268},{268,204},{204,140},{140,76},{76,12}... | collective-permute-start | bytes 110600 | tf_op jit(solution)/shard_map/ppermute | solution.py:504
  163.0 2.1 %collective-permute-start.15 = (f32[72,128]{1,0:T(8,128)S(1)}, f32[72,128]{1,0:T(8,128)S(1)}, u32[]{:S(2)}, u32[]{:S(2)}) collective-permute-start(f32[72,128]{1,0:T(8,128)S(1)} %get-tuple-element.98), channel_id=1, source_target_pairs={{460,28},{396,460},{332,396},{268,332},{204,268},{140,204},{76,140... | collective-permute-start | bytes 110600 | tf_op jit(solution)/shard_map/ppermute | solution.py:504
  165.1 1.2 shard_map.98.refs_2_
  166.4 2.3 %collective-permute-done.15.refs_6_.refs_4_ = f32[72,128]{1,0:T(8,128)S(1)} collective-permute-done((f32[72,128]{1,0:T(8,128)S(1)}, f32[72,128]{1,0:T(8,128)S(1)}, u32[]{:S(2)}, u32[]{:S(2)}) %collective-permute-start.15) | collective-permute-done | bytes 36896 | tf_op jit(solution)/shard_map/ppermute | solution.py:504
  168.7 2.4 %shard_map.99 = f32[384,128]{1,0:T(8,128)} custom-call(f32[24,128]{1,0:T(8,128)S(1)} %get-tuple-element.101.refs_0_, f32[120,128]{1,0:T(8,128)S(1)} %collective-permute-done.refs_1_.refs_3_, f32[32,128]{1,0:T(8,128)S(1)} %shard_map.98.refs_2_, f32[72,128]{1,0:T(8,128)S(1)} %collective-permute-done.14.refs_5_.refs_3_, ...), custom_call_target="tpu_custom_call" | custom-call | flops 100000000 | bytes 400000 | tf_op jit(solution)/shard_map/pallas_call | solution.py:479
  171.1 7.7 %all-to-all-start.5 = ((f32[16,24,128]{2,1,0:T(8,128)}), f32[16,24,128]{2,1,0:T(8,128)S(1)}, u32[]{:S(2)}, u32[]{:S(2)}) async-start(f32[16,24,128]{2,1,0:T(8,128)} %bitcast.15), calls=%async_computation.5 | async-start | bytes 393216 | tf_op jit(solution)/shard_map/all_to_all | solution.py:499
  178.8 2.4 %collective-permute-start.16 = (f32[24,128]{1,0:T(8,128)S(1)}, f32[24,128]{1,0:T(8,128)S(1)}, u32[]{:S(2)}, u32[]{:S(2)}) collective-permute-start(f32[24,128]{1,0:T(8,128)S(1)} %get-tuple-element.100), channel_id=1, source_target_pairs={{460,488},{396,424},{332,360},{268,296},{204,232},{140,168},{76,10... | collective-permute-start | bytes 36872 | tf_op jit(solution)/shard_map/ppermute | solution.py:504
  181.2 2.2 %all_gather.19.refs_9_ = f32[48,128]{1,0:T(8,128)S(1)} all-gather(f32[24,128]{1,0:T(8,128)S(1)} %get-tuple-element.99), channel_id=1, replica_groups=mesh['z2'=2,'z1'=2,'z0'=2,'core'=2,'zh'=2,'x1'=2,'x0'=2,'y1'=2,'y0'=2] {..., dimensions={0}, use_global_device_ids=true | all-gather | bytes 36864 | tf_op jit(solution)/shard_map/all_gather | solution.py:508
  183.5 0.3 collective-permute-done.16.refs_10_
  183.8 3.1 %shard_map.97.refs_2_ = f32[96,128]{1,0:T(8,128)S(1)} custom-call(f32[1,128]{1,0:T(1,128)S(1)} %constant_dynamic-slice_fusion.refs_0_, f32[120,128]{1,0:T(8,128)S(1)} %collective-permute-done.refs_1_.refs_3_, f32[96,128]{1,0:T(8,128)S(1)} %get-tuple-element.91.refs_0_.refs_2_.refs_3_, f32[96,128]{1,0:T(8,128)S(1)} %get-tuple-element.92.refs_3_, ...), custom_call_target="tpu_custom_call" | custom-call | flops 200000000 | bytes 400000 | tf_op jit(solution)/shard_map/pallas_call | solution.py:479
  186.9 0.6 shard_map.100
  187.5 7.6 %collective-permute-start.17 = (f32[6,4,1024]{2,1,0:T(4,128)S(1)}, f32[6,4,1024]{2,1,0:T(4,128)S(1)}, u32[]{:S(2)}, u32[]{:S(2)}) collective-permute-start(f32[6,4,1024]{2,1,0:T(4,128)S(1)} %shard_map.100), channel_id=1, source_target_pairs={{460,0},{396,1},{332,2},{268,3},{204,4},{140,5},{76,6},{12,7},{0,8... | collective-permute-start | bytes 294920 | tf_op jit(solution)/shard_map/ppermute | solution.py:599
  195.2 16.0 %collective-permute-done.17 = f32[6,4,1024]{2,1,0:T(4,128)S(1)} collective-permute-done((f32[6,4,1024]{2,1,0:T(4,128)S(1)}, f32[6,4,1024]{2,1,0:T(4,128)S(1)}, u32[]{:S(2)}, u32[]{:S(2)}) %collective-permute-start.17) | collective-permute-done | bytes 98336 | tf_op jit(solution)/shard_map/ppermute | solution.py:599
  211.2 0.6 fusion
  (23 shorter events, 0.1 us)
Async XLA Ops:
  0.6 13.2 %collective-permute-start.1 = (f32[3,4,1024]{2,1,0:T(4,128)}, f32[3,4,1024]{2,1,0:T(4,128)S(1)}, u32[]{:S(2)}, u32[]{:S(2)}) collective-permute-start(f32[3,4,1024]{2,1,0:T(4,128)} %bitcast.29), channel_id=1, source_target_pairs={{0,460},{1,396},{2,332},{3,268},{4,204},{5,140},{6,76},{7,12},{8,0... | collective-permute-start | bytes 147464 | tf_op jit(solution)/shard_map/ppermute | solution.py:504
  15.1 9.0 %copy-start = (f32[4,3,1024]{2,0,1:T(4,128)S(1)}, f32[4,3,1024]{2,0,1:T(4,128)}, u32[]{:S(2)}) copy-start(f32[4,3,1024]{2,0,1:T(4,128)} %param.7) | copy-start | bytes 147460
  15.1 9.0 %copy-start.2 = (f32[1024]{0:T(1024)S(1)}, f32[1024]{0:T(1024)}, u32[]{:S(2)}) copy-start(f32[1024]{0:T(1024)} %param.9) | copy-start | bytes 12292
  15.1 9.0 %copy-start.3 = (f32[1024]{0:T(1024)S(1)}, f32[1024]{0:T(1024)}, u32[]{:S(2)}) copy-start(f32[1024]{0:T(1024)} %param.10) | copy-start | bytes 12292
  15.1 27.1 %all-to-all-start = ((f32[16,24,128]{2,1,0:T(8,128)}), f32[16,24,128]{2,1,0:T(8,128)S(1)}, u32[]{:S(2)}, u32[]{:S(2)}) async-start(f32[16,24,128]{2,1,0:T(8,128)} %bitcast.5), calls=%async_computation | async-start | bytes 393216 | tf_op jit(solution)/shard_map/all_to_all | solution.py:499
  24.1 0.7 copy-start.1
  24.8 13.2 %collective-permute-start = (f32[120,128]{1,0:T(8,128)S(1)}, f32[120,128]{1,0:T(8,128)S(1)}, u32[]{:S(2)}, u32[]{:S(2)}) collective-permute-start(f32[120,128]{1,0:T(8,128)S(1)} %shard_map.77), channel_id=1, source_target_pairs={{0,460},{1,396},{2,332},{3,268},{4,204},{5,140},{6,76},{7,12},{8,0... | collective-permute-start | bytes 184328 | tf_op jit(solution)/shard_map/ppermute | solution.py:504
  42.3 6.5 %collective-permute-start.2 = (f32[88,128]{1,0:T(8,128)S(1)}, f32[88,128]{1,0:T(8,128)S(1)}, u32[]{:S(2)}, u32[]{:S(2)}) collective-permute-start(f32[88,128]{1,0:T(8,128)S(1)} %get-tuple-element.57), channel_id=1, source_target_pairs={{460,396},{396,332},{332,268},{268,204},{204,140},{140,76},{76,12}... | collective-permute-start | bytes 135176 | tf_op jit(solution)/shard_map/ppermute | solution.py:504
  44.2 4.8 %collective-permute-start.3 = (f32[88,128]{1,0:T(8,128)S(1)}, f32[88,128]{1,0:T(8,128)S(1)}, u32[]{:S(2)}, u32[]{:S(2)}) collective-permute-start(f32[88,128]{1,0:T(8,128)S(1)} %get-tuple-element.58), channel_id=1, source_target_pairs={{460,28},{396,460},{332,396},{268,332},{204,268},{140,204},{76,140... | collective-permute-start | bytes 135176 | tf_op jit(solution)/shard_map/ppermute | solution.py:504
  51.4 26.2 %all-to-all-start.1 = ((f32[16,24,128]{2,1,0:T(8,128)}), f32[16,24,128]{2,1,0:T(8,128)S(1)}, u32[]{:S(2)}, u32[]{:S(2)}) async-start(f32[16,24,128]{2,1,0:T(8,128)} %bitcast.7), calls=%async_computation.1 | async-start | bytes 393216 | tf_op jit(solution)/shard_map/all_to_all | solution.py:499
  64.4 5.0 %collective-permute-start.4 = (f32[24,128]{1,0:T(8,128)S(1)}, f32[24,128]{1,0:T(8,128)S(1)}, u32[]{:S(2)}, u32[]{:S(2)}) collective-permute-start(f32[24,128]{1,0:T(8,128)S(1)} %get-tuple-element.60), channel_id=1, source_target_pairs={{460,488},{396,424},{332,360},{268,296},{204,232},{140,168},{76,10... | collective-permute-start | bytes 36872 | tf_op jit(solution)/shard_map/ppermute | solution.py:504
  72.6 5.0 %collective-permute-start.5 = (f32[24,128]{1,0:T(8,128)S(1)}, f32[24,128]{1,0:T(8,128)S(1)}, u32[]{:S(2)}, u32[]{:S(2)}) collective-permute-start(f32[24,128]{1,0:T(8,128)S(1)} %get-tuple-element.64), channel_id=1, source_target_pairs={{460,488},{396,424},{332,360},{268,296},{204,232},{140,168},{76,10... | collective-permute-start | bytes 36872 | tf_op jit(solution)/shard_map/ppermute | solution.py:504
  78.2 10.0 %collective-permute-start.6 = (f32[48,128]{1,0:T(8,128)S(1)}, f32[48,128]{1,0:T(8,128)S(1)}, u32[]{:S(2)}, u32[]{:S(2)}) collective-permute-start(f32[48,128]{1,0:T(8,128)S(1)} %get-tuple-element.67), channel_id=1, source_target_pairs={{460,396},{396,332},{332,268},{268,204},{204,140},{140,76},{76,12}... | collective-permute-start | bytes 73736 | tf_op jit(solution)/shard_map/ppermute | solution.py:504
  82.0 6.2 %collective-permute-start.7 = (f32[48,128]{1,0:T(8,128)S(1)}, f32[48,128]{1,0:T(8,128)S(1)}, u32[]{:S(2)}, u32[]{:S(2)}) collective-permute-start(f32[48,128]{1,0:T(8,128)S(1)} %get-tuple-element.68), channel_id=1, source_target_pairs={{460,28},{396,460},{332,396},{268,332},{204,268},{140,204},{76,140... | collective-permute-start | bytes 73736 | tf_op jit(solution)/shard_map/ppermute | solution.py:504
  92.1 10.4 %all-to-all-start.2 = ((f32[16,24,128]{2,1,0:T(8,128)}), f32[16,24,128]{2,1,0:T(8,128)S(1)}, u32[]{:S(2)}, u32[]{:S(2)}) async-start(f32[16,24,128]{2,1,0:T(8,128)} %bitcast.9), calls=%async_computation.2 | async-start | bytes 393216 | tf_op jit(solution)/shard_map/all_to_all | solution.py:499
  102.5 6.7 %collective-permute-start.8 = (f32[72,128]{1,0:T(8,128)S(1)}, f32[72,128]{1,0:T(8,128)S(1)}, u32[]{:S(2)}, u32[]{:S(2)}) collective-permute-start(f32[72,128]{1,0:T(8,128)S(1)} %get-tuple-element.77), channel_id=1, source_target_pairs={{460,396},{396,332},{332,268},{268,204},{204,140},{140,76},{76,12}... | collective-permute-start | bytes 110600 | tf_op jit(solution)/shard_map/ppermute | solution.py:504
  106.0 5.0 %collective-permute-start.9 = (f32[72,128]{1,0:T(8,128)S(1)}, f32[72,128]{1,0:T(8,128)S(1)}, u32[]{:S(2)}, u32[]{:S(2)}) collective-permute-start(f32[72,128]{1,0:T(8,128)S(1)} %get-tuple-element.78), channel_id=1, source_target_pairs={{460,28},{396,460},{332,396},{268,332},{204,268},{140,204},{76,140... | collective-permute-start | bytes 110600 | tf_op jit(solution)/shard_map/ppermute | solution.py:504
  113.4 20.8 %all-to-all-start.3 = ((f32[16,24,128]{2,1,0:T(8,128)}), f32[16,24,128]{2,1,0:T(8,128)S(1)}, u32[]{:S(2)}, u32[]{:S(2)}) async-start(f32[16,24,128]{2,1,0:T(8,128)} %bitcast.11), calls=%async_computation.3 | async-start | bytes 393216 | tf_op jit(solution)/shard_map/all_to_all | solution.py:499
  121.2 5.0 %collective-permute-start.10 = (f32[24,128]{1,0:T(8,128)S(1)}, f32[24,128]{1,0:T(8,128)S(1)}, u32[]{:S(2)}, u32[]{:S(2)}) collective-permute-start(f32[24,128]{1,0:T(8,128)S(1)} %get-tuple-element.80), channel_id=1, source_target_pairs={{460,488},{396,424},{332,360},{268,296},{204,232},{140,168},{76,10... | collective-permute-start | bytes 36872 | tf_op jit(solution)/shard_map/ppermute | solution.py:504
  129.3 5.0 %collective-permute-start.11 = (f32[24,128]{1,0:T(8,128)S(1)}, f32[24,128]{1,0:T(8,128)S(1)}, u32[]{:S(2)}, u32[]{:S(2)}) collective-permute-start(f32[24,128]{1,0:T(8,128)S(1)} %get-tuple-element.84), channel_id=1, source_target_pairs={{460,488},{396,424},{332,360},{268,296},{204,232},{140,168},{76,10... | collective-permute-start | bytes 36872 | tf_op jit(solution)/shard_map/ppermute | solution.py:504
  135.0 9.8 %collective-permute-start.12 = (f32[48,128]{1,0:T(8,128)S(1)}, f32[48,128]{1,0:T(8,128)S(1)}, u32[]{:S(2)}, u32[]{:S(2)}) collective-permute-start(f32[48,128]{1,0:T(8,128)S(1)} %get-tuple-element.87), channel_id=1, source_target_pairs={{460,396},{396,332},{332,268},{268,204},{204,140},{140,76},{76,12}... | collective-permute-start | bytes 73736 | tf_op jit(solution)/shard_map/ppermute | solution.py:504
  138.6 6.2 %collective-permute-start.13 = (f32[48,128]{1,0:T(8,128)S(1)}, f32[48,128]{1,0:T(8,128)S(1)}, u32[]{:S(2)}, u32[]{:S(2)}) collective-permute-start(f32[48,128]{1,0:T(8,128)S(1)} %get-tuple-element.88), channel_id=1, source_target_pairs={{460,28},{396,460},{332,396},{268,332},{204,268},{140,204},{76,140... | collective-permute-start | bytes 73736 | tf_op jit(solution)/shard_map/ppermute | solution.py:504
  148.7 10.5 %all-to-all-start.4 = ((f32[16,24,128]{2,1,0:T(8,128)}), f32[16,24,128]{2,1,0:T(8,128)S(1)}, u32[]{:S(2)}, u32[]{:S(2)}) async-start(f32[16,24,128]{2,1,0:T(8,128)} %bitcast.13), calls=%async_computation.4 | async-start | bytes 393216 | tf_op jit(solution)/shard_map/all_to_all | solution.py:499
  159.2 7.1 %collective-permute-start.14 = (f32[72,128]{1,0:T(8,128)S(1)}, f32[72,128]{1,0:T(8,128)S(1)}, u32[]{:S(2)}, u32[]{:S(2)}) collective-permute-start(f32[72,128]{1,0:T(8,128)S(1)} %get-tuple-element.97), channel_id=1, source_target_pairs={{460,396},{396,332},{332,268},{268,204},{204,140},{140,76},{76,12}... | collective-permute-start | bytes 110600 | tf_op jit(solution)/shard_map/ppermute | solution.py:504
  163.0 5.7 %collective-permute-start.15 = (f32[72,128]{1,0:T(8,128)S(1)}, f32[72,128]{1,0:T(8,128)S(1)}, u32[]{:S(2)}, u32[]{:S(2)}) collective-permute-start(f32[72,128]{1,0:T(8,128)S(1)} %get-tuple-element.98), channel_id=1, source_target_pairs={{460,28},{396,460},{332,396},{268,332},{204,268},{140,204},{76,140... | collective-permute-start | bytes 110600 | tf_op jit(solution)/shard_map/ppermute | solution.py:504
  171.1 15.8 %all-to-all-start.5 = ((f32[16,24,128]{2,1,0:T(8,128)}), f32[16,24,128]{2,1,0:T(8,128)S(1)}, u32[]{:S(2)}, u32[]{:S(2)}) async-start(f32[16,24,128]{2,1,0:T(8,128)} %bitcast.15), calls=%async_computation.5 | async-start | bytes 393216 | tf_op jit(solution)/shard_map/all_to_all | solution.py:499
  178.8 5.0 %collective-permute-start.16 = (f32[24,128]{1,0:T(8,128)S(1)}, f32[24,128]{1,0:T(8,128)S(1)}, u32[]{:S(2)}, u32[]{:S(2)}) collective-permute-start(f32[24,128]{1,0:T(8,128)S(1)} %get-tuple-element.100), channel_id=1, source_target_pairs={{460,488},{396,424},{332,360},{268,296},{204,232},{140,168},{76,10... | collective-permute-start | bytes 36872 | tf_op jit(solution)/shard_map/ppermute | solution.py:504
  187.5 23.7 %collective-permute-start.17 = (f32[6,4,1024]{2,1,0:T(4,128)S(1)}, f32[6,4,1024]{2,1,0:T(4,128)S(1)}, u32[]{:S(2)}, u32[]{:S(2)}) collective-permute-start(f32[6,4,1024]{2,1,0:T(4,128)S(1)} %shard_map.100), channel_id=1, source_target_pairs={{460,0},{396,1},{332,2},{268,3},{204,4},{140,5},{76,6},{12,7},{0,8... | collective-permute-start | bytes 294920 | tf_op jit(solution)/shard_map/ppermute | solution.py:599

commit v3 on v2

--- a/solution.py
+++ b/solution.py
@@ -19,13 +19,14 @@
 SLABS = 32
 MINE = BEADS // CBEADS
 STEP = 256
-WIDTH = 256
-AHEAD = 4
-
+WIDTH = 512
+AHEAD = 2
+
+A_ROW = 96
+Q_ROW = 104
 M_ROW = 96
-A_ROW = 104
-Q_ROW = 112
-PACKED = 120
+PLACES = (112, 128)
+MOTION = (104, 128)
 WIDE = 72
 
 AXES = ("z2", "z1", "z0", "core", "zh", "x1", "x0", "y1", "y0")
@@ -274,18 +275,17 @@
         part_ref[24 * r : 24 * r + 24, :] = total
 
 
-def spread(ref, out_ref, centre):
+def spread(ref, out_ref):
     for k in range(3):
         for block in range(8):
-            value = ref[k, :, 128 * block : 128 * block + 128]
-            out_ref[pl.ds(8 * k + block, 4, stride=24), :] = value if centre is None else value - centre[k]
-
-
-def pack_kernel(v_ref, m_ref, a_ref, q_ref, out_ref):
-    spread(v_ref, out_ref, None)
-    out_ref[M_ROW : M_ROW + 8, :] = m_ref[...]
-    out_ref[A_ROW : A_ROW + 8, :] = a_ref[...]
-    out_ref[Q_ROW : Q_ROW + 8, :] = q_ref[...]
+            out_ref[pl.ds(8 * k + block, 4, stride=24), :] = ref[k, :, 128 * block : 128 * block + 128]
+
+
+def pack_kernel(x_ref, *refs):
+    out_ref = refs[-1]
+    spread(x_ref, out_ref)
+    for i, ref in enumerate(refs[:-1]):
+        out_ref[96 + 8 * i : 104 + 8 * i, :] = ref[...]
 
 
 def unpack(value_ref, out_ref, base):
@@ -295,18 +295,20 @@
 
 
 def start_kernel(cols_ref, x_ref, y_ref, up_ref, down_ref, inner_ref, outer_ref, part_ref):
-    spread(x_ref, y_ref, (2.0 * cols_ref[0, SLAB_AT] + 1.0, 1.0, 1.0))
+    centre = (2.0 * cols_ref[0, SLAB_AT] + 1.0, 1.0, 1.0)
+    for i in range(12):
+        y_ref[8 * i : 8 * i + 8, :] = x_ref[8 * i : 8 * i + 8, :] - centre[i % 3]
     emit(y_ref, up_ref, down_ref)
     emit_edges(y_ref[0:24, :], y_ref[72:96, :], inner_ref, outer_ref, cols_ref[0, CORE_AT])
     emit_partial(y_ref, cols_ref, part_ref)
 
 
-def near_halo_body(rate, p_ref, y_ref, v_ref, r_ref, left, right, wide_l, wide_r, edges, store, scr):
+def near_halo_body(rate, p_ref, m_ref, y_ref, v_ref, r_ref, left, right, wide_l, wide_r, edges, store, scr):
     chain = scr[10]
     for i in range(2):
         init_rows(*slot(scr, i)[:2])
     own = p_ref[A_ROW : A_ROW + 8, :]
-    mass = p_ref[M_ROW : M_ROW + 8, :]
+    mass = m_ref[M_ROW : M_ROW + 8, :]
     inverse = 1.0 / mass
     share = halves(wide_l[WIDE + 4 : WIDE + 8, :], wide_r[WIDE : WIDE + 4, :])
     chain[0:24, :], chain[120:144, :] = edges
@@ -349,21 +351,21 @@
     lax.fori_loop(0, MINE // 2, two, 0)
 
 
-def near_slow_kernel(rate, cols_ref, p_ref, y_ref, v_ref, r_ref, left, right, wide_l, wide_r, inner, outer, vo_ref, *rest):
+def near_slow_kernel(rate, cols_ref, p_ref, m_ref, y_ref, v_ref, r_ref, left, right, wide_l, wide_r, inner, outer, vo_ref, *rest):
     def store(r, y, v):
         vo_ref[pl.ds(r, 8), :] = v
 
     core = cols_ref[0, CORE_AT]
     edges = edges_of(inner, outer, core)
     scr = rest[-len(SCRATCH) - 1 :]
-    near_halo_body(rate, p_ref, y_ref, v_ref, r_ref, left, right, wide_l, wide_r, edges, store, scr)
+    near_halo_body(rate, p_ref, m_ref, y_ref, v_ref, r_ref, left, right, wide_l, wide_r, edges, store, scr)
     if len(rest) > len(scr):
         first = y_ref[0:24, :] + TIME_STEP * vo_ref[0:24, :]
         last = y_ref[72:96, :] + TIME_STEP * vo_ref[72:96, :]
         emit_edges(first, last, rest[0], rest[1], core)
 
 
-def near_fast_kernel(cols_ref, p_ref, y_ref, v_ref, r_ref, left, right, wide_l, wide_r, before, after, *rest):
+def near_fast_kernel(cols_ref, p_ref, m_ref, y_ref, v_ref, r_ref, left, right, wide_l, wide_r, before, after, *rest):
     vo_ref, yo_ref, up_ref, down_ref, in_ref, ou_ref, part_ref = rest[:7]
     scr = rest[7:]
 
@@ -372,7 +374,7 @@
         yo_ref[pl.ds(r, 8), :] = y + TIME_STEP * v
 
     edges = (before[...], after[...])
-    near_halo_body(TIME_STEP, p_ref, y_ref, v_ref, r_ref, left, right, wide_l, wide_r, edges, store, scr)
+    near_halo_body(TIME_STEP, p_ref, m_ref, y_ref, v_ref, r_ref, left, right, wide_l, wide_r, edges, store, scr)
     emit(yo_ref, up_ref, down_ref)
     emit_edges(yo_ref[0:24, :], yo_ref[72:96, :], in_ref, ou_ref, cols_ref[0, CORE_AT])
     emit_partial(yo_ref, cols_ref, part_ref)
@@ -390,24 +392,16 @@
             out[WIDE : WIDE + 16, :] = p_ref[A_ROW : A_ROW + 16, :]
 
 
-def far_own_kernel(yc_ref, p_ref, out_ref, src, tgt, qs, lhs, rows):
+def far_kernel(yc_ref, p_ref, left, right, wide_l, wide_r, out_ref, *scr):
+    coords = bead_at(yc_ref, 0)
+    src, tgt, qs, lhs, rows_of = slot(scr, 0)
     init_rows(src, tgt)
-    coords = bead_at(yc_ref, 0)
     q = put_sources(src, qs, lhs, coords, p_ref[Q_ROW : Q_ROW + 8, :], FAR)
     rhs = put_targets(tgt, coords, FAR)
-    total = joined(stream(chunks(lhs, 0, 1024, rhs, 0, 1024, q, 0)), 0)
-    for k, r in enumerate(sums_of(total, rows)):
-        out_ref[8 * k : 8 * k + 8, :] = r
-
-
-def far_halo_kernel(yc_ref, p_ref, r_ref, left, right, wide_l, wide_r, out_ref, *scr):
-    coords = bead_at(yc_ref, 0)
-    tasks = []
+    tasks = chunks(lhs, 0, 1024, rhs, 0, 1024, q, 0)
     for i, (block, rows) in enumerate(((left, wide_l), (right, wide_r))):
-        src, tgt, qs, lhs, _ = slot(scr, i)
+        src, tgt, qs, lhs, _ = slot(scr, i + 1)
         init_rows(src, tgt)
-        if i == 0:
-            rhs = put_targets(tgt, coords, FAR)
         there = [block[48 + 8 * k : 56 + 8 * k, :] for k in range(3)]
         there[0] = there[0] + (2.0 if i else -2.0)
         q = put_sources(src, qs, lhs, there, rows[WIDE + 8 : WIDE + 16, :], FAR)
@@ -417,9 +411,7 @@
         else:
             tasks += chunks(lhs, 0, 512, rhs, 0, 1024, q, 0)
             tasks += chunks(lhs, 512, 1024, rhs, 512, 1024, q, 0)
-    totals = stream(tasks)
-    total = joined(totals, 0)
-    sums = [s + r_ref[8 * k : 8 * k + 8, :] for k, s in enumerate(sums_of(total, slot(scr, 0)[4]))]
+    sums = sums_of(joined(stream(tasks), 0), rows_of)
     force = field(coords, sums, p_ref[Q_ROW : Q_ROW + 8, :], FAR)
     for r in range(16):
         for k in range(3):
@@ -504,6 +496,12 @@
     return lax.ppermute(x, AXES, moves)
 
 
+def pack(x, rows, shape):
+    args = [jnp.transpose(x, (1, 0, 2))] + [r.reshape(8, 128) for r in rows]
+    (packed,) = call(pack_kernel, [shape], None, args)
+    return packed
+
+
 def pair(x):
     return lax.all_gather(x, "core", axis=0, tiled=True)
 
@@ -512,23 +510,12 @@
 
 
 def shards(positions, velocities, masses, amplitudes, charges):
-    x = send(jnp.transpose(positions, (1, 0, 2)), MOVE_IN)
-    (packed,) = call(
-        pack_kernel,
-        [(PACKED, 128)],
-        None,
-        [
-            jnp.transpose(velocities, (1, 0, 2)),
-            masses.reshape(8, 128),
-            amplitudes.reshape(8, 128),
-            charges.reshape(8, 128),
-        ],
-    )
-    p = send(packed, MOVE_IN)
+    places = pack(positions, (amplitudes, charges), PLACES)
+    p = send(places, MOVE_IN)
+    motion = pack(velocities, (masses,), MOTION)
     cols = lax.dynamic_slice_in_dim(jnp.asarray(SETTINGS), lax.axis_index(AXES), 1, 0)
-    y, up, down, inner, outer, part = call(start_kernel, [STATE, HALO, HALO, BEAD, BEAD, (384, 128)], cols, [x])
+    y, up, down, inner, outer, part = call(start_kernel, [STATE, HALO, HALO, BEAD, BEAD, (384, 128)], cols, [p])
     first = y
-    v = p
     wide_l = wide_r = None
     big = 400_000_000
     for stage in range(5):
@@ -541,7 +528,7 @@
                 near_fast_kernel,
                 [STATE, STATE, HALO, HALO, BEAD, BEAD, (384, 128)],
                 cols,
-                [p, y, v, sums, left, right, wide_l, wide_r, before, after],
+                [p, motion, y, v, sums, left, right, wide_l, wide_r, before, after],
                 SCRATCH + [CHAIN],
                 big // 2,
             )
@@ -549,7 +536,11 @@
         edge = stage in (0, 4)
         got = exchange_team(part)
         inner = pair(inner)
-        (sums,) = call(near_own_kernel, [(128, 128)], None, [y, p], SCRATCH, big)
+        if stage == 0:
+            sums, motion = call(near_own_kernel, [(128, 128)], None, [y, p], SCRATCH, big, passed=[motion])
+            v = motion = send(motion, MOVE_IN)
+        else:
+            (sums,) = call(near_own_kernel, [(128, 128)], None, [y, p], SCRATCH, big)
 
         def gather(*refs, wide=stage == 0):
             gather_kernel(wide, *refs)
@@ -561,9 +552,8 @@
         outer = send(outer, BEAD_SWAP)
         if stage == 0:
             wide_l, wide_r = left, right
-        (far_sums,) = call(far_own_kernel, [(32, 128)], None, [yc, p], SCRATCH[:5], big // 4)
         (copies,) = call(
-            far_halo_kernel, [(384, 128)], None, [yc, p, far_sums, left, right, wide_l, wide_r], SCRATCH, big // 4
+            far_kernel, [(384, 128)], None, [yc, p, left, right, wide_l, wide_r], SCRATCH + SCRATCH[:5], big // 2
         )
         far = exchange_team(copies)
         rate = TIME_STEP * (0.5 if edge else 1.0)
@@ -575,7 +565,7 @@
             near_slow,
             [STATE] + [BEAD] * (2 * (stage < 4)),
             cols,
-            [p, y, v, sums, left, right, wide_l, wide_r, inner, outer],
+            [p, motion, y, v, sums, left, right, wide_l, wide_r, inner, outer],
             SCRATCH + [CHAIN],
             big // 2,
         )
@@ -585,7 +575,7 @@
             def final(*refs, rate=rate):
                 final_kernel(rate, *refs)
 
-            (both,) = call(final, [BOTH], cols, [p, v, y, first, far], [pltpu.VMEM(STATE, f32)])
+            (both,) = call(final, [BOTH], cols, [motion, v, y, first, far], [pltpu.VMEM(STATE, f32)])
         else:
 
             def update(*refs, rate=rate):
@@ -594,7 +584,7 @@
             inner = pair(ends[0])
             outer = send(ends[1], BEAD_SWAP)
             v, y, up, down, before, after = call(
-                update, [STATE, STATE, HALO, HALO, BEAD, BEAD], cols, [p, y, v, far, inner, outer]
+                update, [STATE, STATE, HALO, HALO, BEAD, BEAD], cols, [motion, y, v, far, inner, outer]
             )
     both = jnp.transpose(lax.ppermute(both, AXES, MOVE_OUT), (1, 0, 2))
     return both[:, 0:3], both[:, 3:6]

time: 213 us -> 216 us (1.014)
  the two profiles are of different devices: /device:TPU:19 before, /device:TPU:240 now
where the time goes in v3:
time: 216 us; the launch traced here: 215 us
  starting transfers between devices  85.1 us (39%)
  waiting for transfers between devices  57.4 us (27%)
  Pallas kernels  55.9 us (26%)
  blocking collectives  11.6 us (5%)
  local copies, waits for them, and re-layouts  3.51 us (2%)
    pallas_call x22, Pallas kernels, call(): pl.pallas_call(body, out_shape=shapes, in_specs=specs, out_specs=[pl.Bloc...  55.9 us
    ppermute x17, starting transfers between devices, send(): return lax.ppermute(x, AXES, moves)  47.9 us
    ppermute x17, waiting for transfers between devices, send(): return lax.ppermute(x, AXES, moves)  36.4 us
    all_to_all x6, starting transfers between devices, exchange_team(): lax.all_to_all(x.reshape(TEAM_ROWS), TEAM, split_axis=0, concat_axis=0, t...  35.3 us
    ppermute x1, waiting for transfers between devices, shards(): both = jnp.transpose(lax.ppermute(both, AXES, MOVE_OUT), (1, 0, 2))  21 us
    all_gather x5, blocking collectives, pair(): return lax.all_gather(x, 'core', axis=0, tiled=True)  11.6 us
  transfers between devices with their start and end apart: 24, of which 10 were waited for; matrix products, arithmetic and copies ran while one was open for 0% of the time, Pallas kernels for 16%

profile of v3, /device:TPU:240, one launch (start us, length us, event | category | flops | bytes accessed | tf_op | source)
XLA Modules:
  0.0 214.6 jit_solution(17456567384086624276)
XLA Ops:
  0.6 0.7 copy-done.2
  1.3 0.8 copy-done
  2.1 0.7 copy-done.3
  2.8 3.8 %collective-permute-start = (f32[112,128]{1,0:T(8,128)S(1)}, f32[112,128]{1,0:T(8,128)S(1)}, u32[]{:S(2)}, u32[]{:S(2)}) collective-permute-start(f32[112,128]{1,0:T(8,128)S(1)} %shard_map.77), channel_id=1, source_target_pairs={{0,460},{1,396},{2,332},{3,268},{4,204},{5,140},{6,76},{7,12},{8,0... | collective-permute-start | bytes 172040 | tf_op jit(solution)/shard_map/ppermute | solution.py:496
  6.6 0.7 constant_dynamic-slice_fusion.refs_0_
  7.3 11.9 %collective-permute-done.refs_1_.refs_3_ = f32[112,128]{1,0:T(8,128)S(1)} collective-permute-done((f32[112,128]{1,0:T(8,128)S(1)}, f32[112,128]{1,0:T(8,128)S(1)}, u32[]{:S(2)}, u32[]{:S(2)}) %collective-permute-start) | collective-permute-done | bytes 57376 | tf_op jit(solution)/shard_map/ppermute | solution.py:496
  19.2 1.3 shard_map.78
  20.5 5.6 %all-to-all-start = ((f32[16,24,128]{2,1,0:T(8,128)}), f32[16,24,128]{2,1,0:T(8,128)S(1)}, u32[]{:S(2)}, u32[]{:S(2)}) async-start(f32[16,24,128]{2,1,0:T(8,128)} %bitcast.5), calls=%async_computation | async-start | bytes 393216 | tf_op jit(solution)/shard_map/all_to_all | solution.py:491
  26.1 4.8 %shard_map.80 = (f32[128,128]{1,0:T(8,128)S(1)}, f32[104,128]{1,0:T(8,128)S(1)}) custom-call(f32[96,128]{1,0:T(8,128)S(1)} %get-tuple-element.54.refs_0_.refs_3_.refs_2_.refs_4_, f32[112,128]{1,0:T(8,128)S(1)} %collective-permute-done.refs_1_.refs_3_, f32[104,128]{1,0:T(8,128)S(1)} %shard_map.79.refs_2_), custom_call_target="tpu_custom_call", output_to_operand_aliasing={{1}: (2, {})} | custom-call | flops 400000000 | bytes 400000 | tf_op jit(solution)/shard_map/pallas_call | solution.py:471
  30.9 0.0 all-to-all-done
  31.0 4.9 %collective-permute-start.2 = (f32[88,128]{1,0:T(8,128)S(1)}, f32[88,128]{1,0:T(8,128)S(1)}, u32[]{:S(2)}, u32[]{:S(2)}) collective-permute-start(f32[88,128]{1,0:T(8,128)S(1)} %get-tuple-element.61), channel_id=1, source_target_pairs={{460,396},{396,332},{332,268},{268,204},{204,140},{140,76},{76,12}... | collective-permute-start | bytes 135176 | tf_op jit(solution)/shard_map/ppermute | solution.py:496
  35.9 1.9 collective-permute-start.3
  37.8 0.0 collective-permute-done.2.refs_6_.refs_8_.refs_2_.refs_4_
  37.8 5.2 %collective-permute-done.3.refs_7_.refs_9_.refs_3_.refs_5_ = f32[88,128]{1,0:T(8,128)S(1)} collective-permute-done((f32[88,128]{1,0:T(8,128)S(1)}, f32[88,128]{1,0:T(8,128)S(1)}, u32[]{:S(2)}, u32[]{:S(2)}) %collective-permute-start.3) | collective-permute-done | bytes 45088 | tf_op jit(solution)/shard_map/ppermute | solution.py:496
  43.0 3.7 %shard_map.83 = f32[384,128]{1,0:T(8,128)} custom-call(f32[24,128]{1,0:T(8,128)S(1)} %get-tuple-element.66.refs_0_, f32[112,128]{1,0:T(8,128)S(1)} %collective-permute-done.refs_1_.refs_3_, f32[88,128]{1,0:T(8,128)S(1)} %collective-permute-done.2.refs_6_.refs_8_.refs_2_.refs_4_, f32[88,128]{1,0:T(8,128)S(1)} %collective-permute-done.3.refs_7_.refs_9_.refs_3_.refs_5_, ...), custom_call_target="tpu_custom_call" | custom-call | flops 200000000 | bytes 400000 | tf_op jit(solution)/shard_map/pallas_call | solution.py:471
  46.7 5.9 %all-to-all-start.1 = ((f32[16,24,128]{2,1,0:T(8,128)}), f32[16,24,128]{2,1,0:T(8,128)S(1)}, u32[]{:S(2)}, u32[]{:S(2)}) async-start(f32[16,24,128]{2,1,0:T(8,128)} %bitcast.7), calls=%async_computation.1 | async-start | bytes 393216 | tf_op jit(solution)/shard_map/all_to_all | solution.py:491
  52.6 1.9 collective-permute-start.1
  54.5 2.2 %collective-permute-start.4 = (f32[24,128]{1,0:T(8,128)S(1)}, f32[24,128]{1,0:T(8,128)S(1)}, u32[]{:S(2)}, u32[]{:S(2)}) collective-permute-start(f32[24,128]{1,0:T(8,128)S(1)} %get-tuple-element.64), channel_id=1, source_target_pairs={{460,488},{396,424},{332,360},{268,296},{204,232},{140,168},{76,10... | collective-permute-start | bytes 36872 | tf_op jit(solution)/shard_map/ppermute | solution.py:496
  56.7 2.5 %all_gather.15.refs_10_ = f32[48,128]{1,0:T(8,128)S(1)} all-gather(f32[24,128]{1,0:T(8,128)S(1)} %get-tuple-element.63), channel_id=1, replica_groups=mesh['z2'=2,'z1'=2,'z0'=2,'core'=2,'zh'=2,'x1'=2,'x0'=2,'y1'=2,'y0'=2] {..., dimensions={0}, use_global_device_ids=true | all-gather | bytes 36864 | tf_op jit(solution)/shard_map/all_gather | solution.py:506
  59.2 9.6 %collective-permute-done.1.refs_2_.refs_4_.refs_1_ = f32[104,128]{1,0:T(8,128)S(1)} collective-permute-done((f32[104,128]{1,0:T(8,128)S(1)}, f32[104,128]{1,0:T(8,128)S(1)}, u32[]{:S(2)}, u32[]{:S(2)}) %collective-permute-start.1) | collective-permute-done | bytes 53280 | tf_op jit(solution)/shard_map/ppermute | solution.py:496
  68.8 0.0 collective-permute-done.4.refs_11_
  68.8 3.2 %shard_map.82 = (f32[96,128]{1,0:T(8,128)S(1)}, f32[24,128]{1,0:T(8,128)S(1)}, f32[24,128]{1,0:T(8,128)S(1)}) custom-call(f32[1,128]{1,0:T(1,128)S(1)} %constant_dynamic-slice_fusion.refs_0_, f32[112,128]{1,0:T(8,128)S(1)} %collective-permute-done.refs_1_.refs_3_, f32[104,128]{1,0:T(8,128)S(1)} %collective-permute-done.1.refs_2_.refs_4_.refs_1_, ...), custom_call_target="tpu_custom_call" | custom-call | flops 200000000 | bytes 400000 | tf_op jit(solution)/shard_map/pallas_call | solution.py:471
  72.0 2.8 %collective-permute-start.5 = (f32[24,128]{1,0:T(8,128)S(1)}, f32[24,128]{1,0:T(8,128)S(1)}, u32[]{:S(2)}, u32[]{:S(2)}) collective-permute-start(f32[24,128]{1,0:T(8,128)S(1)} %get-tuple-element.68), channel_id=1, source_target_pairs={{460,488},{396,424},{332,360},{268,296},{204,232},{140,168},{76,10... | collective-permute-start | bytes 36872 | tf_op jit(solution)/shard_map/ppermute | solution.py:496
  74.9 1.8 all_gather.16.refs_5_
  76.7 0.3 collective-permute-done.5.refs_6_
  77.0 0.7 shard_map.84
  77.7 1.9 collective-permute-start.6
  79.6 3.9 %collective-permute-start.7 = (f32[48,128]{1,0:T(8,128)S(1)}, f32[48,128]{1,0:T(8,128)S(1)}, u32[]{:S(2)}, u32[]{:S(2)}) collective-permute-start(f32[48,128]{1,0:T(8,128)S(1)} %get-tuple-element.72), channel_id=1, source_target_pairs={{460,28},{396,460},{332,396},{268,332},{204,268},{140,204},{76,140... | collective-permute-start | bytes 73736 | tf_op jit(solution)/shard_map/ppermute | solution.py:496
  83.5 4.8 %shard_map.85.refs_5_ = f32[128,128]{1,0:T(8,128)S(1)} custom-call(f32[96,128]{1,0:T(8,128)S(1)} %get-tuple-element.69.refs_0_.refs_3_, f32[112,128]{1,0:T(8,128)S(1)} %collective-permute-done.refs_1_.refs_3_), custom_call_target="tpu_custom_call" | custom-call | flops 400000000 | bytes 400000 | tf_op jit(solution)/shard_map/pallas_call | solution.py:471
  88.4 4.0 %shard_map.86 = (f32[96,128]{1,0:T(8,128)S(1)}, f32[96,128]{1,0:T(8,128)S(1)}, f32[48,128]{1,0:T(8,128)S(1)}, f32[48,128]{1,0:T(8,128)S(1)}, f32[24,128]{1,0:T(8...) custom-call(f32[1,128]{1,0:T(1,128)S(1)} %constant_dynamic-slice_fusion.refs_0_, ...), custom_call_target="tpu_custom_call" | custom-call | flops 200000000 | bytes 400000 | tf_op jit(solution)/shard_map/pallas_call | solution.py:471
  92.3 6.1 %all-to-all-start.2 = ((f32[16,24,128]{2,1,0:T(8,128)}), f32[16,24,128]{2,1,0:T(8,128)S(1)}, u32[]{:S(2)}, u32[]{:S(2)}) async-start(f32[16,24,128]{2,1,0:T(8,128)} %bitcast.9), calls=%async_computation.2 | async-start | bytes 393216 | tf_op jit(solution)/shard_map/all_to_all | solution.py:491
  98.4 4.8 %shard_map.87.refs_4_.refs_5_ = f32[128,128]{1,0:T(8,128)S(1)} custom-call(f32[96,128]{1,0:T(8,128)S(1)} %get-tuple-element.75.refs_0_.refs_3_.refs_2_, f32[112,128]{1,0:T(8,128)S(1)} %collective-permute-done.refs_1_.refs_3_), custom_call_target="tpu_custom_call" | custom-call | flops 400000000 | bytes 400000 | tf_op jit(solution)/shard_map/pallas_call | solution.py:471
  103.3 3.1 %collective-permute-start.8 = (f32[72,128]{1,0:T(8,128)S(1)}, f32[72,128]{1,0:T(8,128)S(1)}, u32[]{:S(2)}, u32[]{:S(2)}) collective-permute-start(f32[72,128]{1,0:T(8,128)S(1)} %get-tuple-element.81), channel_id=1, source_target_pairs={{460,396},{396,332},{332,268},{268,204},{204,140},{140,76},{76,12}... | collective-permute-start | bytes 110600 | tf_op jit(solution)/shard_map/ppermute | solution.py:496
  106.4 2.7 %collective-permute-start.9 = (f32[72,128]{1,0:T(8,128)S(1)}, f32[72,128]{1,0:T(8,128)S(1)}, u32[]{:S(2)}, u32[]{:S(2)}) collective-permute-start(f32[72,128]{1,0:T(8,128)S(1)} %get-tuple-element.82), channel_id=1, source_target_pairs={{460,28},{396,460},{332,396},{268,332},{204,268},{140,204},{76,140... | collective-permute-start | bytes 110600 | tf_op jit(solution)/shard_map/ppermute | solution.py:496
  109.1 4.3 %collective-permute-done.9.refs_7_.refs_3_ = f32[72,128]{1,0:T(8,128)S(1)} collective-permute-done((f32[72,128]{1,0:T(8,128)S(1)}, f32[72,128]{1,0:T(8,128)S(1)}, u32[]{:S(2)}, u32[]{:S(2)}) %collective-permute-start.9) | collective-permute-done | bytes 36896 | tf_op jit(solution)/shard_map/ppermute | solution.py:496
  113.5 3.7 %shard_map.90 = f32[384,128]{1,0:T(8,128)} custom-call(f32[24,128]{1,0:T(8,128)S(1)} %get-tuple-element.86.refs_0_, f32[112,128]{1,0:T(8,128)S(1)} %collective-permute-done.refs_1_.refs_3_, f32[72,128]{1,0:T(8,128)S(1)} %collective-permute-done.8.refs_6_.refs_2_, f32[72,128]{1,0:T(8,128)S(1)} %collective-permute-done.9.refs_7_.refs_3_, ...), custom_call_target="tpu_custom_call" | custom-call | flops 200000000 | bytes 400000 | tf_op jit(solution)/shard_map/pallas_call | solution.py:471
  117.1 6.0 %all-to-all-start.3 = ((f32[16,24,128]{2,1,0:T(8,128)}), f32[16,24,128]{2,1,0:T(8,128)S(1)}, u32[]{:S(2)}, u32[]{:S(2)}) async-start(f32[16,24,128]{2,1,0:T(8,128)} %bitcast.11), calls=%async_computation.3 | async-start | bytes 393216 | tf_op jit(solution)/shard_map/all_to_all | solution.py:491
  123.1 2.2 %collective-permute-start.10 = (f32[24,128]{1,0:T(8,128)S(1)}, f32[24,128]{1,0:T(8,128)S(1)}, u32[]{:S(2)}, u32[]{:S(2)}) collective-permute-start(f32[24,128]{1,0:T(8,128)S(1)} %get-tuple-element.84), channel_id=1, source_target_pairs={{460,488},{396,424},{332,360},{268,296},{204,232},{140,168},{76,10... | collective-permute-start | bytes 36872 | tf_op jit(solution)/shard_map/ppermute | solution.py:496
  125.3 2.5 %all_gather.17.refs_10_ = f32[48,128]{1,0:T(8,128)S(1)} all-gather(f32[24,128]{1,0:T(8,128)S(1)} %get-tuple-element.83), channel_id=1, replica_groups=mesh['z2'=2,'z1'=2,'z0'=2,'core'=2,'zh'=2,'x1'=2,'x0'=2,'y1'=2,'y0'=2] {..., dimensions={0}, use_global_device_ids=true | all-gather | bytes 36864 | tf_op jit(solution)/shard_map/all_gather | solution.py:506
  127.8 0.3 collective-permute-done.10.refs_11_
  128.1 3.2 %shard_map.89 = (f32[96,128]{1,0:T(8,128)S(1)}, f32[24,128]{1,0:T(8,128)S(1)}, f32[24,128]{1,0:T(8,128)S(1)}) custom-call(f32[1,128]{1,0:T(1,128)S(1)} %constant_dynamic-slice_fusion.refs_0_, f32[112,128]{1,0:T(8,128)S(1)} %collective-permute-done.refs_1_.refs_3_, f32[104,128]{1,0:T(8,128)S(1)} %collective-permute-done.1.refs_2_.refs_4_.refs_1_, ...), custom_call_target="tpu_custom_call" | custom-call | flops 200000000 | bytes 400000 | tf_op jit(solution)/shard_map/pallas_call | solution.py:471
  131.3 2.4 %collective-permute-start.11 = (f32[24,128]{1,0:T(8,128)S(1)}, f32[24,128]{1,0:T(8,128)S(1)}, u32[]{:S(2)}, u32[]{:S(2)}) collective-permute-start(f32[24,128]{1,0:T(8,128)S(1)} %get-tuple-element.88), channel_id=1, source_target_pairs={{460,488},{396,424},{332,360},{268,296},{204,232},{140,168},{76,10... | collective-permute-start | bytes 36872 | tf_op jit(solution)/shard_map/ppermute | solution.py:496
  133.7 2.3 %all_gather.18.refs_5_ = f32[48,128]{1,0:T(8,128)S(1)} all-gather(f32[24,128]{1,0:T(8,128)S(1)} %get-tuple-element.87), channel_id=1, replica_groups=mesh['z2'=2,'z1'=2,'z0'=2,'core'=2,'zh'=2,'x1'=2,'x0'=2,'y1'=2,'y0'=2] {..., dimensions={0}, use_global_device_ids=true | all-gather | bytes 36864 | tf_op jit(solution)/shard_map/all_gather | solution.py:506
  136.0 0.3 collective-permute-done.11.refs_6_
  136.3 0.7 shard_map.91
  137.0 1.9 collective-permute-start.12
  138.9 3.9 %collective-permute-start.13 = (f32[48,128]{1,0:T(8,128)S(1)}, f32[48,128]{1,0:T(8,128)S(1)}, u32[]{:S(2)}, u32[]{:S(2)}) collective-permute-start(f32[48,128]{1,0:T(8,128)S(1)} %get-tuple-element.92), channel_id=1, source_target_pairs={{460,28},{396,460},{332,396},{268,332},{204,268},{140,204},{76,140... | collective-permute-start | bytes 73736 | tf_op jit(solution)/shard_map/ppermute | solution.py:496
  142.9 4.8 %shard_map.92.refs_5_ = f32[128,128]{1,0:T(8,128)S(1)} custom-call(f32[96,128]{1,0:T(8,128)S(1)} %get-tuple-element.89.refs_0_.refs_3_, f32[112,128]{1,0:T(8,128)S(1)} %collective-permute-done.refs_1_.refs_3_), custom_call_target="tpu_custom_call" | custom-call | flops 400000000 | bytes 400000 | tf_op jit(solution)/shard_map/pallas_call | solution.py:471
  147.7 4.0 %shard_map.93 = (f32[96,128]{1,0:T(8,128)S(1)}, f32[96,128]{1,0:T(8,128)S(1)}, f32[48,128]{1,0:T(8,128)S(1)}, f32[48,128]{1,0:T(8,128)S(1)}, f32[24,128]{1,0:T(8...) custom-call(f32[1,128]{1,0:T(1,128)S(1)} %constant_dynamic-slice_fusion.refs_0_, ...), custom_call_target="tpu_custom_call" | custom-call | flops 200000000 | bytes 400000 | tf_op jit(solution)/shard_map/pallas_call | solution.py:471
  151.6 5.8 %all-to-all-start.4 = ((f32[16,24,128]{2,1,0:T(8,128)}), f32[16,24,128]{2,1,0:T(8,128)S(1)}, u32[]{:S(2)}, u32[]{:S(2)}) async-start(f32[16,24,128]{2,1,0:T(8,128)} %bitcast.13), calls=%async_computation.4 | async-start | bytes 393216 | tf_op jit(solution)/shard_map/all_to_all | solution.py:491
  157.4 4.8 %shard_map.94.refs_4_.refs_5_ = f32[128,128]{1,0:T(8,128)S(1)} custom-call(f32[96,128]{1,0:T(8,128)S(1)} %get-tuple-element.95.refs_0_.refs_3_, f32[112,128]{1,0:T(8,128)S(1)} %collective-permute-done.refs_1_.refs_3_), custom_call_target="tpu_custom_call" | custom-call | flops 400000000 | bytes 400000 | tf_op jit(solution)/shard_map/pallas_call | solution.py:471
  162.3 3.1 %collective-permute-start.14 = (f32[72,128]{1,0:T(8,128)S(1)}, f32[72,128]{1,0:T(8,128)S(1)}, u32[]{:S(2)}, u32[]{:S(2)}) collective-permute-start(f32[72,128]{1,0:T(8,128)S(1)} %get-tuple-element.101), channel_id=1, source_target_pairs={{460,396},{396,332},{332,268},{268,204},{204,140},{140,76},{76,12}... | collective-permute-start | bytes 110600 | tf_op jit(solution)/shard_map/ppermute | solution.py:496
  165.4 2.9 %collective-permute-start.15 = (f32[72,128]{1,0:T(8,128)S(1)}, f32[72,128]{1,0:T(8,128)S(1)}, u32[]{:S(2)}, u32[]{:S(2)}) collective-permute-start(f32[72,128]{1,0:T(8,128)S(1)} %get-tuple-element.102), channel_id=1, source_target_pairs={{460,28},{396,460},{332,396},{268,332},{204,268},{140,204},{76,140... | collective-permute-start | bytes 110600 | tf_op jit(solution)/shard_map/ppermute | solution.py:496
  168.4 4.1 %collective-permute-done.15.refs_7_.refs_3_ = f32[72,128]{1,0:T(8,128)S(1)} collective-permute-done((f32[72,128]{1,0:T(8,128)S(1)}, f32[72,128]{1,0:T(8,128)S(1)}, u32[]{:S(2)}, u32[]{:S(2)}) %collective-permute-start.15) | collective-permute-done | bytes 36896 | tf_op jit(solution)/shard_map/ppermute | solution.py:496
  172.5 3.7 %shard_map.97 = f32[384,128]{1,0:T(8,128)} custom-call(f32[24,128]{1,0:T(8,128)S(1)} %get-tuple-element.105.refs_0_, f32[112,128]{1,0:T(8,128)S(1)} %collective-permute-done.refs_1_.refs_3_, f32[72,128]{1,0:T(8,128)S(1)} %collective-permute-done.14.refs_6_.refs_2_, f32[72,128]{1,0:T(8,128)S(1)} %collective-permute-done.15.refs_7_.refs_3_, ...), custom_call_target="tpu_custom_call" | custom-call | flops 200000000 | bytes 400000 | tf_op jit(solution)/shard_map/pallas_call | solution.py:471
  176.1 6.0 %all-to-all-start.5 = ((f32[16,24,128]{2,1,0:T(8,128)}), f32[16,24,128]{2,1,0:T(8,128)S(1)}, u32[]{:S(2)}, u32[]{:S(2)}) async-start(f32[16,24,128]{2,1,0:T(8,128)} %bitcast.15), calls=%async_computation.5 | async-start | bytes 393216 | tf_op jit(solution)/shard_map/all_to_all | solution.py:491
  182.1 2.2 %collective-permute-start.16 = (f32[24,128]{1,0:T(8,128)S(1)}, f32[24,128]{1,0:T(8,128)S(1)}, u32[]{:S(2)}, u32[]{:S(2)}) collective-permute-start(f32[24,128]{1,0:T(8,128)S(1)} %get-tuple-element.104), channel_id=1, source_target_pairs={{460,488},{396,424},{332,360},{268,296},{204,232},{140,168},{76,10... | collective-permute-start | bytes 36872 | tf_op jit(solution)/shard_map/ppermute | solution.py:496
  184.3 2.5 %all_gather.19.refs_10_ = f32[48,128]{1,0:T(8,128)S(1)} all-gather(f32[24,128]{1,0:T(8,128)S(1)} %get-tuple-element.103), channel_id=1, replica_groups=mesh['z2'=2,'z1'=2,'z0'=2,'core'=2,'zh'=2,'x1'=2,'x0'=2,'y1'=2,'y0'=2] {..., dimensions={0}, use_global_device_ids=true | all-gather | bytes 36864 | tf_op jit(solution)/shard_map/all_gather | solution.py:506
  186.8 0.3 collective-permute-done.16.refs_11_
  187.1 3.2 %shard_map.96.refs_2_ = f32[96,128]{1,0:T(8,128)S(1)} custom-call(f32[1,128]{1,0:T(1,128)S(1)} %constant_dynamic-slice_fusion.refs_0_, f32[112,128]{1,0:T(8,128)S(1)} %collective-permute-done.refs_1_.refs_3_, f32[104,128]{1,0:T(8,128)S(1)} %collective-permute-done.1.refs_2_.refs_4_.refs_1_, f32[96,128]{1,0:T(8,128)S(1)} %get-tuple-element.95.refs_0_.refs_3_, ...), custom_call_target="tpu_custom_call" | custom-call | flops 200000000 | bytes 400000 | tf_op jit(solution)/shard_map/pallas_call | solution.py:471
  190.3 0.6 shard_map.98
  191.0 1.9 collective-permute-start.17
  192.9 21.0 %collective-permute-done.17 = f32[6,4,1024]{2,1,0:T(4,128)S(1)} collective-permute-done((f32[6,4,1024]{2,1,0:T(4,128)S(1)}, f32[6,4,1024]{2,1,0:T(4,128)S(1)}, u32[]{:S(2)}, u32[]{:S(2)}) %collective-permute-start.17) | collective-permute-done | bytes 98336 | tf_op jit(solution)/shard_map/ppermute | solution.py:589
  213.9 0.6 fusion
  (23 shorter events, 0.1 us)
Async XLA Ops:
  0.6 0.7 copy-start.2
  1.3 0.8 copy-start
  2.1 0.7 copy-start.3
  2.8 16.4 %collective-permute-start = (f32[112,128]{1,0:T(8,128)S(1)}, f32[112,128]{1,0:T(8,128)S(1)}, u32[]{:S(2)}, u32[]{:S(2)}) collective-permute-start(f32[112,128]{1,0:T(8,128)S(1)} %shard_map.77), channel_id=1, source_target_pairs={{0,460},{1,396},{2,332},{3,268},{4,204},{5,140},{6,76},{7,12},{8,0... | collective-permute-start | bytes 172040 | tf_op jit(solution)/shard_map/ppermute | solution.py:496
  20.5 5.6 %copy-start.1 = (f32[4,3,1024]{2,0,1:T(4,128)S(1)}, f32[4,3,1024]{2,0,1:T(4,128)}, u32[]{:S(2)}) copy-start(f32[4,3,1024]{2,0,1:T(4,128)} %param.7) | copy-start | bytes 147460
  20.5 5.6 %copy-start.4 = (f32[1024]{0:T(1024)S(1)}, f32[1024]{0:T(1024)}, u32[]{:S(2)}) copy-start(f32[1024]{0:T(1024)} %param.8) | copy-start | bytes 12292
  20.5 10.4 %all-to-all-start = ((f32[16,24,128]{2,1,0:T(8,128)}), f32[16,24,128]{2,1,0:T(8,128)S(1)}, u32[]{:S(2)}, u32[]{:S(2)}) async-start(f32[16,24,128]{2,1,0:T(8,128)} %bitcast.5), calls=%async_computation | async-start | bytes 393216 | tf_op jit(solution)/shard_map/all_to_all | solution.py:491
  31.0 6.8 %collective-permute-start.2 = (f32[88,128]{1,0:T(8,128)S(1)}, f32[88,128]{1,0:T(8,128)S(1)}, u32[]{:S(2)}, u32[]{:S(2)}) collective-permute-start(f32[88,128]{1,0:T(8,128)S(1)} %get-tuple-element.61), channel_id=1, source_target_pairs={{460,396},{396,332},{332,268},{268,204},{204,140},{140,76},{76,12}... | collective-permute-start | bytes 135176 | tf_op jit(solution)/shard_map/ppermute | solution.py:496
  35.9 7.2 %collective-permute-start.3 = (f32[88,128]{1,0:T(8,128)S(1)}, f32[88,128]{1,0:T(8,128)S(1)}, u32[]{:S(2)}, u32[]{:S(2)}) collective-permute-start(f32[88,128]{1,0:T(8,128)S(1)} %get-tuple-element.62), channel_id=1, source_target_pairs={{460,28},{396,460},{332,396},{268,332},{204,268},{140,204},{76,140... | collective-permute-start | bytes 135176 | tf_op jit(solution)/shard_map/ppermute | solution.py:496
  46.7 30.3 %all-to-all-start.1 = ((f32[16,24,128]{2,1,0:T(8,128)}), f32[16,24,128]{2,1,0:T(8,128)S(1)}, u32[]{:S(2)}, u32[]{:S(2)}) async-start(f32[16,24,128]{2,1,0:T(8,128)} %bitcast.7), calls=%async_computation.1 | async-start | bytes 393216 | tf_op jit(solution)/shard_map/all_to_all | solution.py:491
  52.6 16.2 %collective-permute-start.1 = (f32[104,128]{1,0:T(8,128)S(1)}, f32[104,128]{1,0:T(8,128)S(1)}, u32[]{:S(2)}, u32[]{:S(2)}) collective-permute-start(f32[104,128]{1,0:T(8,128)S(1)} %get-tuple-element.55), channel_id=1, source_target_pairs={{0,460},{1,396},{2,332},{3,268},{4,204},{5,140},{6,76},{7,12},{8,0... | collective-permute-start | bytes 159752 | tf_op jit(solution)/shard_map/ppermute | solution.py:496
  54.5 14.3 %collective-permute-start.4 = (f32[24,128]{1,0:T(8,128)S(1)}, f32[24,128]{1,0:T(8,128)S(1)}, u32[]{:S(2)}, u32[]{:S(2)}) collective-permute-start(f32[24,128]{1,0:T(8,128)S(1)} %get-tuple-element.64), channel_id=1, source_target_pairs={{460,488},{396,424},{332,360},{268,296},{204,232},{140,168},{76,10... | collective-permute-start | bytes 36872 | tf_op jit(solution)/shard_map/ppermute | solution.py:496
  72.0 5.0 %collective-permute-start.5 = (f32[24,128]{1,0:T(8,128)S(1)}, f32[24,128]{1,0:T(8,128)S(1)}, u32[]{:S(2)}, u32[]{:S(2)}) collective-permute-start(f32[24,128]{1,0:T(8,128)S(1)} %get-tuple-element.68), channel_id=1, source_target_pairs={{460,488},{396,424},{332,360},{268,296},{204,232},{140,168},{76,10... | collective-permute-start | bytes 36872 | tf_op jit(solution)/shard_map/ppermute | solution.py:496
  77.7 10.6 %collective-permute-start.6 = (f32[48,128]{1,0:T(8,128)S(1)}, f32[48,128]{1,0:T(8,128)S(1)}, u32[]{:S(2)}, u32[]{:S(2)}) collective-permute-start(f32[48,128]{1,0:T(8,128)S(1)} %get-tuple-element.71), channel_id=1, source_target_pairs={{460,396},{396,332},{332,268},{268,204},{204,140},{140,76},{76,12}... | collective-permute-start | bytes 73736 | tf_op jit(solution)/shard_map/ppermute | solution.py:496
  79.6 8.7 %collective-permute-start.7 = (f32[48,128]{1,0:T(8,128)S(1)}, f32[48,128]{1,0:T(8,128)S(1)}, u32[]{:S(2)}, u32[]{:S(2)}) collective-permute-start(f32[48,128]{1,0:T(8,128)S(1)} %get-tuple-element.72), channel_id=1, source_target_pairs={{460,28},{396,460},{332,396},{268,332},{204,268},{140,204},{76,140... | collective-permute-start | bytes 73736 | tf_op jit(solution)/shard_map/ppermute | solution.py:496
  92.3 10.9 %all-to-all-start.2 = ((f32[16,24,128]{2,1,0:T(8,128)}), f32[16,24,128]{2,1,0:T(8,128)S(1)}, u32[]{:S(2)}, u32[]{:S(2)}) async-start(f32[16,24,128]{2,1,0:T(8,128)} %bitcast.9), calls=%async_computation.2 | async-start | bytes 393216 | tf_op jit(solution)/shard_map/all_to_all | solution.py:491
  103.3 5.9 %collective-permute-start.8 = (f32[72,128]{1,0:T(8,128)S(1)}, f32[72,128]{1,0:T(8,128)S(1)}, u32[]{:S(2)}, u32[]{:S(2)}) collective-permute-start(f32[72,128]{1,0:T(8,128)S(1)} %get-tuple-element.81), channel_id=1, source_target_pairs={{460,396},{396,332},{332,268},{268,204},{204,140},{140,76},{76,12}... | collective-permute-start | bytes 110600 | tf_op jit(solution)/shard_map/ppermute | solution.py:496
  106.4 7.1 %collective-permute-start.9 = (f32[72,128]{1,0:T(8,128)S(1)}, f32[72,128]{1,0:T(8,128)S(1)}, u32[]{:S(2)}, u32[]{:S(2)}) collective-permute-start(f32[72,128]{1,0:T(8,128)S(1)} %get-tuple-element.82), channel_id=1, source_target_pairs={{460,28},{396,460},{332,396},{268,332},{204,268},{140,204},{76,140... | collective-permute-start | bytes 110600 | tf_op jit(solution)/shard_map/ppermute | solution.py:496
  117.1 19.2 %all-to-all-start.3 = ((f32[16,24,128]{2,1,0:T(8,128)}), f32[16,24,128]{2,1,0:T(8,128)S(1)}, u32[]{:S(2)}, u32[]{:S(2)}) async-start(f32[16,24,128]{2,1,0:T(8,128)} %bitcast.11), calls=%async_computation.3 | async-start | bytes 393216 | tf_op jit(solution)/shard_map/all_to_all | solution.py:491
  123.1 5.0 %collective-permute-start.10 = (f32[24,128]{1,0:T(8,128)S(1)}, f32[24,128]{1,0:T(8,128)S(1)}, u32[]{:S(2)}, u32[]{:S(2)}) collective-permute-start(f32[24,128]{1,0:T(8,128)S(1)} %get-tuple-element.84), channel_id=1, source_target_pairs={{460,488},{396,424},{332,360},{268,296},{204,232},{140,168},{76,10... | collective-permute-start | bytes 36872 | tf_op jit(solution)/shard_map/ppermute | solution.py:496
  131.3 5.0 %collective-permute-start.11 = (f32[24,128]{1,0:T(8,128)S(1)}, f32[24,128]{1,0:T(8,128)S(1)}, u32[]{:S(2)}, u32[]{:S(2)}) collective-permute-start(f32[24,128]{1,0:T(8,128)S(1)} %get-tuple-element.88), channel_id=1, source_target_pairs={{460,488},{396,424},{332,360},{268,296},{204,232},{140,168},{76,10... | collective-permute-start | bytes 36872 | tf_op jit(solution)/shard_map/ppermute | solution.py:496
  137.0 10.6 %collective-permute-start.12 = (f32[48,128]{1,0:T(8,128)S(1)}, f32[48,128]{1,0:T(8,128)S(1)}, u32[]{:S(2)}, u32[]{:S(2)}) collective-permute-start(f32[48,128]{1,0:T(8,128)S(1)} %get-tuple-element.91), channel_id=1, source_target_pairs={{460,396},{396,332},{332,268},{268,204},{204,140},{140,76},{76,12}... | collective-permute-start | bytes 73736 | tf_op jit(solution)/shard_map/ppermute | solution.py:496
  138.9 8.7 %collective-permute-start.13 = (f32[48,128]{1,0:T(8,128)S(1)}, f32[48,128]{1,0:T(8,128)S(1)}, u32[]{:S(2)}, u32[]{:S(2)}) collective-permute-start(f32[48,128]{1,0:T(8,128)S(1)} %get-tuple-element.92), channel_id=1, source_target_pairs={{460,28},{396,460},{332,396},{268,332},{204,268},{140,204},{76,140... | collective-permute-start | bytes 73736 | tf_op jit(solution)/shard_map/ppermute | solution.py:496
  151.6 10.6 %all-to-all-start.4 = ((f32[16,24,128]{2,1,0:T(8,128)}), f32[16,24,128]{2,1,0:T(8,128)S(1)}, u32[]{:S(2)}, u32[]{:S(2)}) async-start(f32[16,24,128]{2,1,0:T(8,128)} %bitcast.13), calls=%async_computation.4 | async-start | bytes 393216 | tf_op jit(solution)/shard_map/all_to_all | solution.py:491
  162.3 6.1 %collective-permute-start.14 = (f32[72,128]{1,0:T(8,128)S(1)}, f32[72,128]{1,0:T(8,128)S(1)}, u32[]{:S(2)}, u32[]{:S(2)}) collective-permute-start(f32[72,128]{1,0:T(8,128)S(1)} %get-tuple-element.101), channel_id=1, source_target_pairs={{460,396},{396,332},{332,268},{268,204},{204,140},{140,76},{76,12}... | collective-permute-start | bytes 110600 | tf_op jit(solution)/shard_map/ppermute | solution.py:496
  165.4 7.1 %collective-permute-start.15 = (f32[72,128]{1,0:T(8,128)S(1)}, f32[72,128]{1,0:T(8,128)S(1)}, u32[]{:S(2)}, u32[]{:S(2)}) collective-permute-start(f32[72,128]{1,0:T(8,128)S(1)} %get-tuple-element.102), channel_id=1, source_target_pairs={{460,28},{396,460},{332,396},{268,332},{204,268},{140,204},{76,140... | collective-permute-start | bytes 110600 | tf_op jit(solution)/shard_map/ppermute | solution.py:496
  176.1 14.2 %all-to-all-start.5 = ((f32[16,24,128]{2,1,0:T(8,128)}), f32[16,24,128]{2,1,0:T(8,128)S(1)}, u32[]{:S(2)}, u32[]{:S(2)}) async-start(f32[16,24,128]{2,1,0:T(8,128)} %bitcast.15), calls=%async_computation.5 | async-start | bytes 393216 | tf_op jit(solution)/shard_map/all_to_all | solution.py:491
  182.1 5.0 %collective-permute-start.16 = (f32[24,128]{1,0:T(8,128)S(1)}, f32[24,128]{1,0:T(8,128)S(1)}, u32[]{:S(2)}, u32[]{:S(2)}) collective-permute-start(f32[24,128]{1,0:T(8,128)S(1)} %get-tuple-element.104), channel_id=1, source_target_pairs={{460,488},{396,424},{332,360},{268,296},{204,232},{140,168},{76,10... | collective-permute-start | bytes 36872 | tf_op jit(solution)/shard_map/ppermute | solution.py:496
  191.0 22.9 %collective-permute-start.17 = (f32[6,4,1024]{2,1,0:T(4,128)S(1)}, f32[6,4,1024]{2,1,0:T(4,128)S(1)}, u32[]{:S(2)}, u32[]{:S(2)}) collective-permute-start(f32[6,4,1024]{2,1,0:T(4,128)S(1)} %shard_map.98), channel_id=1, source_target_pairs={{460,0},{396,1},{332,2},{268,3},{204,4},{140,5},{76,6},{12,7},{0,8... | collective-permute-start | bytes 294920 | tf_op jit(solution)/shard_map/ppermute | solution.py:589

commit v4 on v2

--- a/solution.py
+++ b/solution.py
@@ -261,7 +261,8 @@
 
 def edges_of(inner, outer, core):
     odd = core > 0.5
-    from_pair = jnp.where(odd, inner[0:24, :], inner[24:48, :])
+    n = outer.shape[0]
+    from_pair = jnp.where(odd, inner[0:n, :], inner[n : 2 * n, :])
     return jnp.where(odd, from_pair, outer[...]), jnp.where(odd, outer[...], from_pair)
 
 
@@ -349,18 +350,19 @@
     lax.fori_loop(0, MINE // 2, two, 0)
 
 
-def near_slow_kernel(rate, cols_ref, p_ref, y_ref, v_ref, r_ref, left, right, wide_l, wide_r, inner, outer, vo_ref, *rest):
+def near_slow_kernel(rate, cols_ref, p_ref, y_ref, v_ref, r_ref, left, right, wide_l, wide_r, vo_ref, *rest):
     def store(r, y, v):
         vo_ref[pl.ds(r, 8), :] = v
 
-    core = cols_ref[0, CORE_AT]
-    edges = edges_of(inner, outer, core)
+    none = jnp.zeros((24, 128), f32)
     scr = rest[-len(SCRATCH) - 1 :]
-    near_halo_body(rate, p_ref, y_ref, v_ref, r_ref, left, right, wide_l, wide_r, edges, store, scr)
+    near_halo_body(rate, p_ref, y_ref, v_ref, r_ref, left, right, wide_l, wide_r, (none, none), store, scr)
     if len(rest) > len(scr):
-        first = y_ref[0:24, :] + TIME_STEP * vo_ref[0:24, :]
-        last = y_ref[72:96, :] + TIME_STEP * vo_ref[72:96, :]
-        emit_edges(first, last, rest[0], rest[1], core)
+        ends = []
+        for at in (0, 72):
+            y = y_ref[at : at + 24, :]
+            ends.append(jnp.concatenate([y, y + TIME_STEP * vo_ref[at : at + 24, :]], axis=0))
+        emit_edges(ends[0], ends[1], rest[0], rest[1], cols_ref[0, CORE_AT])
 
 
 def near_fast_kernel(cols_ref, p_ref, y_ref, v_ref, r_ref, left, right, wide_l, wide_r, before, after, *rest):
@@ -439,27 +441,37 @@
     return out
 
 
-def update_kernel(rate, cols_ref, p_ref, y_ref, v_ref, far_ref, inner, outer,
+def pulled(speeds, pull, before, after):
+    speeds[0] = speeds[0] + pull * before
+    speeds[-1] = speeds[-1] + pull * after
+    return speeds
+
+
+def update_kernel(near_rate, rate, cols_ref, p_ref, y_ref, v_ref, far_ref, inner, outer,
                   vo_ref, yo_ref, up_ref, down_ref, before_ref, after_ref):
-    for b, v in enumerate(kick(rate, cols_ref, p_ref, v_ref, far_ref)):
+    pull = near_rate * SPRING
+    edges = edges_of(inner, outer, cols_ref[0, CORE_AT])
+    speeds = pulled(kick(rate, cols_ref, p_ref, v_ref, far_ref), pull, edges[0][0:24], edges[1][0:24])
+    for b, v in enumerate(speeds):
         vo_ref[24 * b : 24 * b + 24, :] = v
         yo_ref[24 * b : 24 * b + 24, :] = y_ref[24 * b : 24 * b + 24, :] + TIME_STEP * v
     emit(yo_ref, up_ref, down_ref)
     inverse = (TIME_STEP * rate * BEADS / CBEADS) / p_ref[M_ROW : M_ROW + 8, :]
     inverse = jnp.concatenate([inverse] * 3, axis=0)
-    edges = edges_of(inner, outer, cols_ref[0, CORE_AT])
     for e, out in enumerate((before_ref, after_ref)):
         total = cols_ref[0, EDGE_AT + e] * far_ref[0:24, :]
         for r in range(1, 16):
             total = total + cols_ref[0, EDGE_AT + 2 * r + e] * far_ref[24 * r : 24 * r + 24, :]
-        out[...] = edges[e] + inverse * total
-
-
-def final_kernel(rate, cols_ref, p_ref, v_ref, y_ref, first_ref, far_ref, out_ref, rows):
+        out[...] = edges[e][24:48] + (TIME_STEP * pull) * y_ref[72 * e : 72 * e + 24, :] + inverse * total
+
+
+def final_kernel(near_rate, rate, cols_ref, p_ref, v_ref, y_ref, first_ref, far_ref, inner, outer, out_ref, rows):
     for i in range(12):
         rows[8 * i : 8 * i + 8, :] = y_ref[8 * i : 8 * i + 8, :] - first_ref[8 * i : 8 * i + 8, :]
     unpack(rows, out_ref, 0)
-    for b, v in enumerate(kick(rate, cols_ref, p_ref, v_ref, far_ref)):
+    before, after = edges_of(inner, outer, cols_ref[0, CORE_AT])
+    speeds = pulled(kick(rate, cols_ref, p_ref, v_ref, far_ref), near_rate * SPRING, before, after)
+    for b, v in enumerate(speeds):
         rows[24 * b : 24 * b + 24, :] = v
     unpack(rows, out_ref, 3)
 
@@ -548,48 +560,56 @@
             continue
         edge = stage in (0, 4)
         got = exchange_team(part)
-        inner = pair(inner)
+        if stage == 4:
+            inner = pair(inner)
         (sums,) = call(near_own_kernel, [(128, 128)], None, [y, p], SCRATCH, big)
 
         def gather(*refs, wide=stage == 0):
             gather_kernel(wide, *refs)
 
         size = (WIDE + 16 * (stage == 0), 128)
-        yc, up, down, outer = call(gather, [BEAD, size, size], None, [got, up, down, p], order=[sums], passed=[outer])
+        yc, up, down = call(gather, [BEAD, size, size], None, [got, up, down, p], order=[sums])
         left = send(up, SLAB_UP)
         right = send(down, SLAB_DOWN)
-        outer = send(outer, BEAD_SWAP)
         if stage == 0:
             wide_l, wide_r = left, right
         (far_sums,) = call(far_own_kernel, [(32, 128)], None, [yc, p], SCRATCH[:5], big // 4)
-        (copies,) = call(
-            far_halo_kernel, [(384, 128)], None, [yc, p, far_sums, left, right, wide_l, wide_r], SCRATCH, big // 4
+        copies, *late = call(
+            far_halo_kernel,
+            [(384, 128)],
+            None,
+            [yc, p, far_sums, left, right, wide_l, wide_r],
+            SCRATCH,
+            big // 4,
+            passed=[outer] * (stage == 4),
         )
         far = exchange_team(copies)
-        rate = TIME_STEP * (0.5 if edge else 1.0)
-
-        def near_slow(*refs, rate=rate):
+        if stage == 4:
+            outer = send(late[0], BEAD_SWAP)
+        near_rate = TIME_STEP * (0.5 if edge else 1.0)
+
+        def near_slow(*refs, rate=near_rate):
             near_slow_kernel(rate, *refs)
 
         v, *ends = call(
             near_slow,
-            [STATE] + [BEAD] * (2 * (stage < 4)),
+            [STATE] + [HALO] * (2 * (stage < 4)),
             cols,
-            [p, y, v, sums, left, right, wide_l, wide_r, inner, outer],
+            [p, y, v, sums, left, right, wide_l, wide_r],
             SCRATCH + [CHAIN],
             big // 2,
         )
         rate = OUTER_STEP * (0.5 if edge else 1.0)
         if stage == 4:
 
-            def final(*refs, rate=rate):
-                final_kernel(rate, *refs)
-
-            (both,) = call(final, [BOTH], cols, [p, v, y, first, far], [pltpu.VMEM(STATE, f32)])
+            def final(*refs, rate=rate, near_rate=near_rate):
+                final_kernel(near_rate, rate, *refs)
+
+            (both,) = call(final, [BOTH], cols, [p, v, y, first, far, inner, outer], [pltpu.VMEM(STATE, f32)])
         else:
 
-            def update(*refs, rate=rate):
-                update_kernel(rate, *refs)
+            def update(*refs, rate=rate, near_rate=near_rate):
+                update_kernel(near_rate, rate, *refs)
 
             inner = pair(ends[0])
             outer = send(ends[1], BEAD_SWAP)

time: 213 us -> 203 us (0.953)
  the two profiles are of different devices: /device:TPU:19 before, /device:TPU:241 now
where the time goes in v4:
time: 203 us; the launch traced here: 201 us
  starting transfers between devices  92.9 us (46%)
  Pallas kernels  52.6 us (26%)
  waiting for transfers between devices  47.5 us (23%)
  blocking collectives  5.54 us (3%)
    pallas_call x24, Pallas kernels, call(): pl.pallas_call(body, out_shape=shapes, in_specs=specs, out_specs=[pl.Bloc...  52.6 us
    all_to_all x6, starting transfers between devices, exchange_team(): lax.all_to_all(x.reshape(TEAM_ROWS), TEAM, split_axis=0, concat_axis=0, t...  49.7 us
    ppermute x15, starting transfers between devices, send(): return lax.ppermute(x, AXES, moves)  41.3 us
    ppermute x15, waiting for transfers between devices, send(): return lax.ppermute(x, AXES, moves)  25.8 us
    ppermute x1, waiting for transfers between devices, shards(): both = jnp.transpose(lax.ppermute(both, AXES, MOVE_OUT), (1, 0, 2))  20.6 us
    all_gather x3, blocking collectives, pair(): return lax.all_gather(x, 'core', axis=0, tiled=True)  5.54 us
  transfers between devices with their start and end apart: 22, of which 10 were waited for; matrix products, arithmetic and copies ran while one was open for 0% of the time, Pallas kernels for 17%

profile of v4, /device:TPU:241, one launch (start us, length us, event | category | flops | bytes accessed | tf_op | source)
XLA Modules:
  0.0 201.4 jit_solution(2727771680296619937)
XLA Ops:
  0.6 3.5 %collective-permute-start.1 = (f32[3,4,1024]{2,1,0:T(4,128)}, f32[3,4,1024]{2,1,0:T(4,128)S(1)}, u32[]{:S(2)}, u32[]{:S(2)}) collective-permute-start(f32[3,4,1024]{2,1,0:T(4,128)} %bitcast.29), channel_id=1, source_target_pairs={{0,460},{1,396},{2,332},{3,268},{4,204},{5,140},{6,76},{7,12},{8,0... | collective-permute-start | bytes 147464 | tf_op jit(solution)/shard_map/ppermute | solution.py:516
  4.2 0.7 constant_dynamic-slice_fusion.refs_0_
  4.9 8.7 %collective-permute-done.1.refs_1_ = f32[3,4,1024]{2,1,0:T(4,128)S(1)} collective-permute-done((f32[3,4,1024]{2,1,0:T(4,128)}, f32[3,4,1024]{2,1,0:T(4,128)S(1)}, u32[]{:S(2)}, u32[]{:S(2)}) %collective-permute-start.1) | collective-permute-done | bytes 49184 | tf_op jit(solution)/shard_map/ppermute | solution.py:516
  13.5 1.3 shard_map.78
  14.8 8.4 %all-to-all-start = ((f32[16,24,128]{2,1,0:T(8,128)}), f32[16,24,128]{2,1,0:T(8,128)S(1)}, u32[]{:S(2)}, u32[]{:S(2)}) async-start(f32[16,24,128]{2,1,0:T(8,128)} %bitcast.5), calls=%async_computation | async-start | bytes 393216 | tf_op jit(solution)/shard_map/all_to_all | solution.py:511
  23.3 0.6 copy-done.1
  24.0 1.9 collective-permute-start
  25.9 11.0 %collective-permute-done.refs_1_.refs_3_ = f32[120,128]{1,0:T(8,128)S(1)} collective-permute-done((f32[120,128]{1,0:T(8,128)S(1)}, f32[120,128]{1,0:T(8,128)S(1)}, u32[]{:S(2)}, u32[]{:S(2)}) %collective-permute-start) | collective-permute-done | bytes 61472 | tf_op jit(solution)/shard_map/ppermute | solution.py:516
  36.9 4.2 %shard_map.79.refs_4_ = f32[128,128]{1,0:T(8,128)S(1)} custom-call(f32[96,128]{1,0:T(8,128)S(1)} %get-tuple-element.47.refs_0_.refs_2_.refs_4_, f32[120,128]{1,0:T(8,128)S(1)} %collective-permute-done.refs_1_.refs_3_), custom_call_target="tpu_custom_call" | custom-call | flops 400000000 | bytes 400000 | tf_op jit(solution)/shard_map/pallas_call | solution.py:491
  41.2 0.0 all-to-all-done
  41.2 1.9 collective-permute-start.2
  43.1 3.4 %collective-permute-start.3 = (f32[88,128]{1,0:T(8,128)S(1)}, f32[88,128]{1,0:T(8,128)S(1)}, u32[]{:S(2)}, u32[]{:S(2)}) collective-permute-start(f32[88,128]{1,0:T(8,128)S(1)} %get-tuple-element.52), channel_id=1, source_target_pairs={{460,28},{396,460},{332,396},{268,332},{204,268},{140,204},{76,140... | collective-permute-start | bytes 135176 | tf_op jit(solution)/shard_map/ppermute | solution.py:516
  46.5 1.2 shard_map.82.refs_2_
  47.7 0.0 collective-permute-done.2.refs_5_.refs_7_.refs_3_
  47.8 1.4 collective-permute-done.3.refs_6_.refs_8_.refs_4_
  49.1 2.4 %shard_map.83 = f32[384,128]{1,0:T(8,128)} custom-call(f32[24,128]{1,0:T(8,128)S(1)} %get-tuple-element.54.refs_0_, f32[120,128]{1,0:T(8,128)S(1)} %collective-permute-done.refs_1_.refs_3_, f32[32,128]{1,0:T(8,128)S(1)} %shard_map.82.refs_2_, f32[88,128]{1,0:T(8,128)S(1)} %collective-permute-done.2.refs_5_.refs_7_.refs_3_, ...), custom_call_target="tpu_custom_call" | custom-call | flops 100000000 | bytes 400000 | tf_op jit(solution)/shard_map/pallas_call | solution.py:491
  51.5 13.8 %all-to-all-start.1 = ((f32[16,24,128]{2,1,0:T(8,128)}), f32[16,24,128]{2,1,0:T(8,128)S(1)}, u32[]{:S(2)}, u32[]{:S(2)}) async-start(f32[16,24,128]{2,1,0:T(8,128)} %bitcast.7), calls=%async_computation.1 | async-start | bytes 393216 | tf_op jit(solution)/shard_map/all_to_all | solution.py:511
  65.4 3.1 %shard_map.81 = (f32[96,128]{1,0:T(8,128)S(1)}, f32[48,128]{1,0:T(8,128)S(1)}, f32[48,128]{1,0:T(8,128)S(1)}) custom-call(f32[1,128]{1,0:T(1,128)S(1)} %constant_dynamic-slice_fusion.refs_0_, f32[120,128]{1,0:T(8,128)S(1)} %collective-permute-done.refs_1_.refs_3_, f32[96,128]{1,0:T(8,128)S(1)} %get-tuple-element.47.refs_0_.refs_2_.refs_4_, ...), custom_call_target="tpu_custom_call" | custom-call | flops 200000000 | bytes 400000 | tf_op jit(solution)/shard_map/pallas_call | solution.py:491
  68.5 3.1 %collective-permute-start.4 = (f32[48,128]{1,0:T(8,128)S(1)}, f32[48,128]{1,0:T(8,128)S(1)}, u32[]{:S(2)}, u32[]{:S(2)}) collective-permute-start(f32[48,128]{1,0:T(8,128)S(1)} %get-tuple-element.56), channel_id=1, source_target_pairs={{460,488},{396,424},{332,360},{268,296},{204,232},{140,168},{76,10... | collective-permute-start | bytes 73736 | tf_op jit(solution)/shard_map/ppermute | solution.py:516
  71.6 1.8 all_gather.9.refs_5_
  73.4 0.2 collective-permute-done.4.refs_6_
  73.6 0.7 shard_map.84
  74.3 1.9 collective-permute-start.5
  76.2 3.4 %collective-permute-start.6 = (f32[48,128]{1,0:T(8,128)S(1)}, f32[48,128]{1,0:T(8,128)S(1)}, u32[]{:S(2)}, u32[]{:S(2)}) collective-permute-start(f32[48,128]{1,0:T(8,128)S(1)} %get-tuple-element.60), channel_id=1, source_target_pairs={{460,28},{396,460},{332,396},{268,332},{204,268},{140,204},{76,140... | collective-permute-start | bytes 73736 | tf_op jit(solution)/shard_map/ppermute | solution.py:516
  79.6 4.3 %shard_map.85.refs_4_ = f32[128,128]{1,0:T(8,128)S(1)} custom-call(f32[96,128]{1,0:T(8,128)S(1)} %get-tuple-element.57.refs_0_.refs_2_, f32[120,128]{1,0:T(8,128)S(1)} %collective-permute-done.refs_1_.refs_3_), custom_call_target="tpu_custom_call" | custom-call | flops 400000000 | bytes 400000 | tf_op jit(solution)/shard_map/pallas_call | solution.py:491
  83.9 0.0 collective-permute-done.5.refs_5_
  83.9 3.9 %shard_map.86 = (f32[96,128]{1,0:T(8,128)S(1)}, f32[96,128]{1,0:T(8,128)S(1)}, f32[48,128]{1,0:T(8,128)S(1)}, f32[48,128]{1,0:T(8,128)S(1)}, f32[24,128]{1,0:T(8...) custom-call(f32[1,128]{1,0:T(1,128)S(1)} %constant_dynamic-slice_fusion.refs_0_, ...), custom_call_target="tpu_custom_call" | custom-call | flops 200000000 | bytes 400000 | tf_op jit(solution)/shard_map/pallas_call | solution.py:491
  87.7 6.3 %all-to-all-start.2 = ((f32[16,24,128]{2,1,0:T(8,128)}), f32[16,24,128]{2,1,0:T(8,128)S(1)}, u32[]{:S(2)}, u32[]{:S(2)}) async-start(f32[16,24,128]{2,1,0:T(8,128)} %bitcast.9), calls=%async_computation.2 | async-start | bytes 393216 | tf_op jit(solution)/shard_map/all_to_all | solution.py:511
  94.0 4.3 %shard_map.87.refs_4_ = f32[128,128]{1,0:T(8,128)S(1)} custom-call(f32[96,128]{1,0:T(8,128)S(1)} %get-tuple-element.63.refs_0_.refs_2_, f32[120,128]{1,0:T(8,128)S(1)} %collective-permute-done.refs_1_.refs_3_), custom_call_target="tpu_custom_call" | custom-call | flops 400000000 | bytes 400000 | tf_op jit(solution)/shard_map/pallas_call | solution.py:491
  98.3 0.5 all-to-all-done.2
  98.8 2.9 %collective-permute-start.7 = (f32[72,128]{1,0:T(8,128)S(1)}, f32[72,128]{1,0:T(8,128)S(1)}, u32[]{:S(2)}, u32[]{:S(2)}) collective-permute-start(f32[72,128]{1,0:T(8,128)S(1)} %get-tuple-element.68), channel_id=1, source_target_pairs={{460,396},{396,332},{332,268},{268,204},{204,140},{140,76},{76,12}... | collective-permute-start | bytes 110600 | tf_op jit(solution)/shard_map/ppermute | solution.py:516
  101.7 2.4 %collective-permute-start.8 = (f32[72,128]{1,0:T(8,128)S(1)}, f32[72,128]{1,0:T(8,128)S(1)}, u32[]{:S(2)}, u32[]{:S(2)}) collective-permute-start(f32[72,128]{1,0:T(8,128)S(1)} %get-tuple-element.69), channel_id=1, source_target_pairs={{460,28},{396,460},{332,396},{268,332},{204,268},{140,204},{76,140... | collective-permute-start | bytes 110600 | tf_op jit(solution)/shard_map/ppermute | solution.py:516
  104.1 1.2 shard_map.90.refs_2_
  105.4 0.0 collective-permute-done.7.refs_5_.refs_3_
  105.4 2.2 %collective-permute-done.8.refs_6_.refs_4_ = f32[72,128]{1,0:T(8,128)S(1)} collective-permute-done((f32[72,128]{1,0:T(8,128)S(1)}, f32[72,128]{1,0:T(8,128)S(1)}, u32[]{:S(2)}, u32[]{:S(2)}) %collective-permute-start.8) | collective-permute-done | bytes 36896 | tf_op jit(solution)/shard_map/ppermute | solution.py:516
  107.6 2.4 %shard_map.91 = f32[384,128]{1,0:T(8,128)} custom-call(f32[24,128]{1,0:T(8,128)S(1)} %get-tuple-element.71.refs_0_, f32[120,128]{1,0:T(8,128)S(1)} %collective-permute-done.refs_1_.refs_3_, f32[32,128]{1,0:T(8,128)S(1)} %shard_map.90.refs_2_, f32[72,128]{1,0:T(8,128)S(1)} %collective-permute-done.7.refs_5_.refs_3_, ...), custom_call_target="tpu_custom_call" | custom-call | flops 100000000 | bytes 400000 | tf_op jit(solution)/shard_map/pallas_call | solution.py:491
  110.0 7.4 %all-to-all-start.3 = ((f32[16,24,128]{2,1,0:T(8,128)}), f32[16,24,128]{2,1,0:T(8,128)S(1)}, u32[]{:S(2)}, u32[]{:S(2)}) async-start(f32[16,24,128]{2,1,0:T(8,128)} %bitcast.11), calls=%async_computation.3 | async-start | bytes 393216 | tf_op jit(solution)/shard_map/all_to_all | solution.py:511
  117.4 3.1 %shard_map.89 = (f32[96,128]{1,0:T(8,128)S(1)}, f32[48,128]{1,0:T(8,128)S(1)}, f32[48,128]{1,0:T(8,128)S(1)}) custom-call(f32[1,128]{1,0:T(1,128)S(1)} %constant_dynamic-slice_fusion.refs_0_, f32[120,128]{1,0:T(8,128)S(1)} %collective-permute-done.refs_1_.refs_3_, f32[96,128]{1,0:T(8,128)S(1)} %get-tuple-element.63.refs_0_.refs_2_, ...), custom_call_target="tpu_custom_call" | custom-call | flops 200000000 | bytes 400000 | tf_op jit(solution)/shard_map/pallas_call | solution.py:491
  120.6 3.1 %collective-permute-start.9 = (f32[48,128]{1,0:T(8,128)S(1)}, f32[48,128]{1,0:T(8,128)S(1)}, u32[]{:S(2)}, u32[]{:S(2)}) collective-permute-start(f32[48,128]{1,0:T(8,128)S(1)} %get-tuple-element.73), channel_id=1, source_target_pairs={{460,488},{396,424},{332,360},{268,296},{204,232},{140,168},{76,10... | collective-permute-start | bytes 73736 | tf_op jit(solution)/shard_map/ppermute | solution.py:516
  123.6 1.8 all_gather.10.refs_5_
  125.5 0.2 collective-permute-done.9.refs_6_
  125.7 0.7 shard_map.92
  126.4 1.9 collective-permute-start.10
  128.3 3.4 %collective-permute-start.11 = (f32[48,128]{1,0:T(8,128)S(1)}, f32[48,128]{1,0:T(8,128)S(1)}, u32[]{:S(2)}, u32[]{:S(2)}) collective-permute-start(f32[48,128]{1,0:T(8,128)S(1)} %get-tuple-element.77), channel_id=1, source_target_pairs={{460,28},{396,460},{332,396},{268,332},{204,268},{140,204},{76,140... | collective-permute-start | bytes 73736 | tf_op jit(solution)/shard_map/ppermute | solution.py:516
  131.7 4.3 %shard_map.93.refs_4_ = f32[128,128]{1,0:T(8,128)S(1)} custom-call(f32[96,128]{1,0:T(8,128)S(1)} %get-tuple-element.74.refs_0_.refs_2_, f32[120,128]{1,0:T(8,128)S(1)} %collective-permute-done.refs_1_.refs_3_), custom_call_target="tpu_custom_call" | custom-call | flops 400000000 | bytes 400000 | tf_op jit(solution)/shard_map/pallas_call | solution.py:491
  135.9 0.0 collective-permute-done.10.refs_5_
  135.9 3.9 %shard_map.94 = (f32[96,128]{1,0:T(8,128)S(1)}, f32[96,128]{1,0:T(8,128)S(1)}, f32[48,128]{1,0:T(8,128)S(1)}, f32[48,128]{1,0:T(8,128)S(1)}, f32[24,128]{1,0:T(8...) custom-call(f32[1,128]{1,0:T(1,128)S(1)} %constant_dynamic-slice_fusion.refs_0_, ...), custom_call_target="tpu_custom_call" | custom-call | flops 200000000 | bytes 400000 | tf_op jit(solution)/shard_map/pallas_call | solution.py:491
  139.8 6.3 %all-to-all-start.4 = ((f32[16,24,128]{2,1,0:T(8,128)}), f32[16,24,128]{2,1,0:T(8,128)S(1)}, u32[]{:S(2)}, u32[]{:S(2)}) async-start(f32[16,24,128]{2,1,0:T(8,128)} %bitcast.13), calls=%async_computation.4 | async-start | bytes 393216 | tf_op jit(solution)/shard_map/all_to_all | solution.py:511
  146.1 4.3 %shard_map.95.refs_4_ = f32[128,128]{1,0:T(8,128)S(1)} custom-call(f32[96,128]{1,0:T(8,128)S(1)} %get-tuple-element.80.refs_0_.refs_2_.refs_3_, f32[120,128]{1,0:T(8,128)S(1)} %collective-permute-done.refs_1_.refs_3_), custom_call_target="tpu_custom_call" | custom-call | flops 400000000 | bytes 400000 | tf_op jit(solution)/shard_map/pallas_call | solution.py:491
  150.4 0.5 all-to-all-done.4
  150.9 2.9 %collective-permute-start.12 = (f32[72,128]{1,0:T(8,128)S(1)}, f32[72,128]{1,0:T(8,128)S(1)}, u32[]{:S(2)}, u32[]{:S(2)}) collective-permute-start(f32[72,128]{1,0:T(8,128)S(1)} %get-tuple-element.85), channel_id=1, source_target_pairs={{460,396},{396,332},{332,268},{268,204},{204,140},{140,76},{76,12}... | collective-permute-start | bytes 110600 | tf_op jit(solution)/shard_map/ppermute | solution.py:516
  153.8 2.7 %collective-permute-start.13 = (f32[72,128]{1,0:T(8,128)S(1)}, f32[72,128]{1,0:T(8,128)S(1)}, u32[]{:S(2)}, u32[]{:S(2)}) collective-permute-start(f32[72,128]{1,0:T(8,128)S(1)} %get-tuple-element.86), channel_id=1, source_target_pairs={{460,28},{396,460},{332,396},{268,332},{204,268},{140,204},{76,140... | collective-permute-start | bytes 110600 | tf_op jit(solution)/shard_map/ppermute | solution.py:516
  156.4 1.2 shard_map.98.refs_2_
  157.7 0.0 collective-permute-done.12.refs_5_.refs_3_
  157.7 2.0 collective-permute-done.13.refs_6_.refs_4_
  159.7 2.4 %shard_map.99 = (f32[384,128]{1,0:T(8,128)}, f32[24,128]{1,0:T(8,128)S(1)}) custom-call(f32[24,128]{1,0:T(8,128)S(1)} %get-tuple-element.87.refs_0_, f32[120,128]{1,0:T(8,128)S(1)} %collective-permute-done.refs_1_.refs_3_, f32[32,128]{1,0:T(8,128)S(1)} %shard_map.98.refs_2_, ...), custom_call_target="tpu_custom_call", output_to_operand_aliasing={{1}: (7, {})} | custom-call | flops 100000000 | bytes 400000 | tf_op jit(solution)/shard_map/pallas_call | solution.py:491
  162.1 7.4 %all-to-all-start.5 = ((f32[16,24,128]{2,1,0:T(8,128)}), f32[16,24,128]{2,1,0:T(8,128)S(1)}, u32[]{:S(2)}, u32[]{:S(2)}) async-start(f32[16,24,128]{2,1,0:T(8,128)} %bitcast.15), calls=%async_computation.5 | async-start | bytes 393216 | tf_op jit(solution)/shard_map/all_to_all | solution.py:511
  169.5 1.9 all_gather.11.refs_6_
  171.4 3.0 %collective-permute-start.14 = (f32[24,128]{1,0:T(8,128)S(1)}, f32[24,128]{1,0:T(8,128)S(1)}, u32[]{:S(2)}, u32[]{:S(2)}) collective-permute-start(f32[24,128]{1,0:T(8,128)S(1)} %get-tuple-element.91), channel_id=1, source_target_pairs={{460,488},{396,424},{332,360},{268,296},{204,232},{140,168},{76,10... | collective-permute-start | bytes 36872 | tf_op jit(solution)/shard_map/ppermute | solution.py:516
  174.4 3.1 %shard_map.97.refs_2_ = f32[96,128]{1,0:T(8,128)S(1)} custom-call(f32[1,128]{1,0:T(1,128)S(1)} %constant_dynamic-slice_fusion.refs_0_, f32[120,128]{1,0:T(8,128)S(1)} %collective-permute-done.refs_1_.refs_3_, f32[96,128]{1,0:T(8,128)S(1)} %get-tuple-element.80.refs_0_.refs_2_.refs_3_, f32[96,128]{1,0:T(8,128)S(1)} %get-tuple-element.81.refs_3_, ...), custom_call_target="tpu_custom_call" | custom-call | flops 200000000 | bytes 400000 | tf_op jit(solution)/shard_map/pallas_call | solution.py:491
  177.6 0.6 shard_map.100
  178.2 1.9 collective-permute-start.15
  180.1 20.6 %collective-permute-done.15 = f32[6,4,1024]{2,1,0:T(4,128)S(1)} collective-permute-done((f32[6,4,1024]{2,1,0:T(4,128)S(1)}, f32[6,4,1024]{2,1,0:T(4,128)S(1)}, u32[]{:S(2)}, u32[]{:S(2)}) %collective-permute-start.15) | collective-permute-done | bytes 98336 | tf_op jit(solution)/shard_map/ppermute | solution.py:619
  200.8 0.6 fusion
  (17 shorter events, 0.1 us)
Async XLA Ops:
  0.6 12.9 %collective-permute-start.1 = (f32[3,4,1024]{2,1,0:T(4,128)}, f32[3,4,1024]{2,1,0:T(4,128)S(1)}, u32[]{:S(2)}, u32[]{:S(2)}) collective-permute-start(f32[3,4,1024]{2,1,0:T(4,128)} %bitcast.29), channel_id=1, source_target_pairs={{0,460},{1,396},{2,332},{3,268},{4,204},{5,140},{6,76},{7,12},{8,0... | collective-permute-start | bytes 147464 | tf_op jit(solution)/shard_map/ppermute | solution.py:516
  14.8 8.5 %copy-start = (f32[4,3,1024]{2,0,1:T(4,128)S(1)}, f32[4,3,1024]{2,0,1:T(4,128)}, u32[]{:S(2)}) copy-start(f32[4,3,1024]{2,0,1:T(4,128)} %param.7) | copy-start | bytes 147460
  14.8 8.5 %copy-start.2 = (f32[1024]{0:T(1024)S(1)}, f32[1024]{0:T(1024)}, u32[]{:S(2)}) copy-start(f32[1024]{0:T(1024)} %param.9) | copy-start | bytes 12292
  14.8 8.5 %copy-start.3 = (f32[1024]{0:T(1024)S(1)}, f32[1024]{0:T(1024)}, u32[]{:S(2)}) copy-start(f32[1024]{0:T(1024)} %param.10) | copy-start | bytes 12292
  14.8 26.3 %all-to-all-start = ((f32[16,24,128]{2,1,0:T(8,128)}), f32[16,24,128]{2,1,0:T(8,128)S(1)}, u32[]{:S(2)}, u32[]{:S(2)}) async-start(f32[16,24,128]{2,1,0:T(8,128)} %bitcast.5), calls=%async_computation | async-start | bytes 393216 | tf_op jit(solution)/shard_map/all_to_all | solution.py:511
  23.3 0.7 copy-start.1
  24.0 12.9 %collective-permute-start = (f32[120,128]{1,0:T(8,128)S(1)}, f32[120,128]{1,0:T(8,128)S(1)}, u32[]{:S(2)}, u32[]{:S(2)}) collective-permute-start(f32[120,128]{1,0:T(8,128)S(1)} %shard_map.77), channel_id=1, source_target_pairs={{0,460},{1,396},{2,332},{3,268},{4,204},{5,140},{6,76},{7,12},{8,0... | collective-permute-start | bytes 184328 | tf_op jit(solution)/shard_map/ppermute | solution.py:516
  41.2 6.5 %collective-permute-start.2 = (f32[88,128]{1,0:T(8,128)S(1)}, f32[88,128]{1,0:T(8,128)S(1)}, u32[]{:S(2)}, u32[]{:S(2)}) collective-permute-start(f32[88,128]{1,0:T(8,128)S(1)} %get-tuple-element.51), channel_id=1, source_target_pairs={{460,396},{396,332},{332,268},{268,204},{204,140},{140,76},{76,12}... | collective-permute-start | bytes 135176 | tf_op jit(solution)/shard_map/ppermute | solution.py:516
  43.1 6.0 %collective-permute-start.3 = (f32[88,128]{1,0:T(8,128)S(1)}, f32[88,128]{1,0:T(8,128)S(1)}, u32[]{:S(2)}, u32[]{:S(2)}) collective-permute-start(f32[88,128]{1,0:T(8,128)S(1)} %get-tuple-element.52), channel_id=1, source_target_pairs={{460,28},{396,460},{332,396},{268,332},{204,268},{140,204},{76,140... | collective-permute-start | bytes 135176 | tf_op jit(solution)/shard_map/ppermute | solution.py:516
  51.5 22.1 %all-to-all-start.1 = ((f32[16,24,128]{2,1,0:T(8,128)}), f32[16,24,128]{2,1,0:T(8,128)S(1)}, u32[]{:S(2)}, u32[]{:S(2)}) async-start(f32[16,24,128]{2,1,0:T(8,128)} %bitcast.7), calls=%async_computation.1 | async-start | bytes 393216 | tf_op jit(solution)/shard_map/all_to_all | solution.py:511
  68.5 5.1 %collective-permute-start.4 = (f32[48,128]{1,0:T(8,128)S(1)}, f32[48,128]{1,0:T(8,128)S(1)}, u32[]{:S(2)}, u32[]{:S(2)}) collective-permute-start(f32[48,128]{1,0:T(8,128)S(1)} %get-tuple-element.56), channel_id=1, source_target_pairs={{460,488},{396,424},{332,360},{268,296},{204,232},{140,168},{76,10... | collective-permute-start | bytes 73736 | tf_op jit(solution)/shard_map/ppermute | solution.py:516
  74.3 9.6 %collective-permute-start.5 = (f32[48,128]{1,0:T(8,128)S(1)}, f32[48,128]{1,0:T(8,128)S(1)}, u32[]{:S(2)}, u32[]{:S(2)}) collective-permute-start(f32[48,128]{1,0:T(8,128)S(1)} %get-tuple-element.59), channel_id=1, source_target_pairs={{460,396},{396,332},{332,268},{268,204},{204,140},{140,76},{76,12}... | collective-permute-start | bytes 73736 | tf_op jit(solution)/shard_map/ppermute | solution.py:516
  76.2 7.6 %collective-permute-start.6 = (f32[48,128]{1,0:T(8,128)S(1)}, f32[48,128]{1,0:T(8,128)S(1)}, u32[]{:S(2)}, u32[]{:S(2)}) collective-permute-start(f32[48,128]{1,0:T(8,128)S(1)} %get-tuple-element.60), channel_id=1, source_target_pairs={{460,28},{396,460},{332,396},{268,332},{204,268},{140,204},{76,140... | collective-permute-start | bytes 73736 | tf_op jit(solution)/shard_map/ppermute | solution.py:516
  87.7 11.1 %all-to-all-start.2 = ((f32[16,24,128]{2,1,0:T(8,128)}), f32[16,24,128]{2,1,0:T(8,128)S(1)}, u32[]{:S(2)}, u32[]{:S(2)}) async-start(f32[16,24,128]{2,1,0:T(8,128)} %bitcast.9), calls=%async_computation.2 | async-start | bytes 393216 | tf_op jit(solution)/shard_map/all_to_all | solution.py:511
  98.8 6.5 %collective-permute-start.7 = (f32[72,128]{1,0:T(8,128)S(1)}, f32[72,128]{1,0:T(8,128)S(1)}, u32[]{:S(2)}, u32[]{:S(2)}) collective-permute-start(f32[72,128]{1,0:T(8,128)S(1)} %get-tuple-element.68), channel_id=1, source_target_pairs={{460,396},{396,332},{332,268},{268,204},{204,140},{140,76},{76,12}... | collective-permute-start | bytes 110600 | tf_op jit(solution)/shard_map/ppermute | solution.py:516
  101.7 5.9 %collective-permute-start.8 = (f32[72,128]{1,0:T(8,128)S(1)}, f32[72,128]{1,0:T(8,128)S(1)}, u32[]{:S(2)}, u32[]{:S(2)}) collective-permute-start(f32[72,128]{1,0:T(8,128)S(1)} %get-tuple-element.69), channel_id=1, source_target_pairs={{460,28},{396,460},{332,396},{268,332},{204,268},{140,204},{76,140... | collective-permute-start | bytes 110600 | tf_op jit(solution)/shard_map/ppermute | solution.py:516
  110.0 15.7 %all-to-all-start.3 = ((f32[16,24,128]{2,1,0:T(8,128)}), f32[16,24,128]{2,1,0:T(8,128)S(1)}, u32[]{:S(2)}, u32[]{:S(2)}) async-start(f32[16,24,128]{2,1,0:T(8,128)} %bitcast.11), calls=%async_computation.3 | async-start | bytes 393216 | tf_op jit(solution)/shard_map/all_to_all | solution.py:511
  120.6 5.1 %collective-permute-start.9 = (f32[48,128]{1,0:T(8,128)S(1)}, f32[48,128]{1,0:T(8,128)S(1)}, u32[]{:S(2)}, u32[]{:S(2)}) collective-permute-start(f32[48,128]{1,0:T(8,128)S(1)} %get-tuple-element.73), channel_id=1, source_target_pairs={{460,488},{396,424},{332,360},{268,296},{204,232},{140,168},{76,10... | collective-permute-start | bytes 73736 | tf_op jit(solution)/shard_map/ppermute | solution.py:516
  126.4 9.6 %collective-permute-start.10 = (f32[48,128]{1,0:T(8,128)S(1)}, f32[48,128]{1,0:T(8,128)S(1)}, u32[]{:S(2)}, u32[]{:S(2)}) collective-permute-start(f32[48,128]{1,0:T(8,128)S(1)} %get-tuple-element.76), channel_id=1, source_target_pairs={{460,396},{396,332},{332,268},{268,204},{204,140},{140,76},{76,12}... | collective-permute-start | bytes 73736 | tf_op jit(solution)/shard_map/ppermute | solution.py:516
  128.3 7.6 %collective-permute-start.11 = (f32[48,128]{1,0:T(8,128)S(1)}, f32[48,128]{1,0:T(8,128)S(1)}, u32[]{:S(2)}, u32[]{:S(2)}) collective-permute-start(f32[48,128]{1,0:T(8,128)S(1)} %get-tuple-element.77), channel_id=1, source_target_pairs={{460,28},{396,460},{332,396},{268,332},{204,268},{140,204},{76,140... | collective-permute-start | bytes 73736 | tf_op jit(solution)/shard_map/ppermute | solution.py:516
  139.8 11.1 %all-to-all-start.4 = ((f32[16,24,128]{2,1,0:T(8,128)}), f32[16,24,128]{2,1,0:T(8,128)S(1)}, u32[]{:S(2)}, u32[]{:S(2)}) async-start(f32[16,24,128]{2,1,0:T(8,128)} %bitcast.13), calls=%async_computation.4 | async-start | bytes 393216 | tf_op jit(solution)/shard_map/all_to_all | solution.py:511
  150.9 6.8 %collective-permute-start.12 = (f32[72,128]{1,0:T(8,128)S(1)}, f32[72,128]{1,0:T(8,128)S(1)}, u32[]{:S(2)}, u32[]{:S(2)}) collective-permute-start(f32[72,128]{1,0:T(8,128)S(1)} %get-tuple-element.85), channel_id=1, source_target_pairs={{460,396},{396,332},{332,268},{268,204},{204,140},{140,76},{76,12}... | collective-permute-start | bytes 110600 | tf_op jit(solution)/shard_map/ppermute | solution.py:516
  153.8 5.9 %collective-permute-start.13 = (f32[72,128]{1,0:T(8,128)S(1)}, f32[72,128]{1,0:T(8,128)S(1)}, u32[]{:S(2)}, u32[]{:S(2)}) collective-permute-start(f32[72,128]{1,0:T(8,128)S(1)} %get-tuple-element.86), channel_id=1, source_target_pairs={{460,28},{396,460},{332,396},{268,332},{204,268},{140,204},{76,140... | collective-permute-start | bytes 110600 | tf_op jit(solution)/shard_map/ppermute | solution.py:516
  162.1 15.4 %all-to-all-start.5 = ((f32[16,24,128]{2,1,0:T(8,128)}), f32[16,24,128]{2,1,0:T(8,128)S(1)}, u32[]{:S(2)}, u32[]{:S(2)}) async-start(f32[16,24,128]{2,1,0:T(8,128)} %bitcast.15), calls=%async_computation.5 | async-start | bytes 393216 | tf_op jit(solution)/shard_map/all_to_all | solution.py:511
  171.4 6.2 %collective-permute-start.14 = (f32[24,128]{1,0:T(8,128)S(1)}, f32[24,128]{1,0:T(8,128)S(1)}, u32[]{:S(2)}, u32[]{:S(2)}) collective-permute-start(f32[24,128]{1,0:T(8,128)S(1)} %get-tuple-element.91), channel_id=1, source_target_pairs={{460,488},{396,424},{332,360},{268,296},{204,232},{140,168},{76,10... | collective-permute-start | bytes 36872 | tf_op jit(solution)/shard_map/ppermute | solution.py:516
  178.2 22.6 %collective-permute-start.15 = (f32[6,4,1024]{2,1,0:T(4,128)S(1)}, f32[6,4,1024]{2,1,0:T(4,128)S(1)}, u32[]{:S(2)}, u32[]{:S(2)}) collective-permute-start(f32[6,4,1024]{2,1,0:T(4,128)S(1)} %shard_map.100), channel_id=1, source_target_pairs={{460,0},{396,1},{332,2},{268,3},{204,4},{140,5},{76,6},{12,7},{0,8... | collective-permute-start | bytes 294920 | tf_op jit(solution)/shard_map/ppermute | solution.py:619

commit v5 on v4

--- a/solution.py
+++ b/solution.py
@@ -35,18 +35,18 @@
 
 
 def _place():
-    ring = [(0, z) for z in range(16)] + [(1, z) for z in range(15, -1, -1)]
+    ring = [((0, 1, 1, 0)[s % 4], s // 2) for s in range(SLABS)]
     cycle = [(0, 0), (0, 1), (0, 2), (0, 3), (1, 3), (1, 2), (1, 1), (1, 0)]
     device = np.zeros((CBEADS, SLABS), np.int64)
     role = np.zeros((512, 2), np.int64)
     member = np.zeros((2, 16), np.int64)
     half_of = np.zeros(SLABS, np.int64)
     for s in range(SLABS):
-        half, z = ring[(s - 8) % SLABS]
+        half, z = ring[s]
         half_of[s] = half
         for b in range(CBEADS):
             q, core = divmod(b, 2)
-            xx, y = cycle[q]
+            xx, y = cycle[(q + 2) % 8]
             x = xx if half == 0 else 3 - xx
             d = ((z % 8) * 2 + core) * 32 + (z // 8) * 16 + x * 4 + y
             device[b, s] = d

time: 203 us -> 206 us (1.015)
  the two profiles are of different devices: /device:TPU:241 before, /device:TPU:253 now
where the time goes in v5:
time: 206 us; the launch traced here: 205 us
  starting transfers between devices  97.1 us (47%)
  Pallas kernels  52.6 us (26%)
  waiting for transfers between devices  46.3 us (22%)
  blocking collectives  6.3 us (3%)
    pallas_call x24, Pallas kernels, call(): pl.pallas_call(body, out_shape=shapes, in_specs=specs, out_specs=[pl.Bloc...  52.6 us
    ppermute x15, starting transfers between devices, send(): return lax.ppermute(x, AXES, moves)  50.3 us
    all_to_all x6, starting transfers between devices, exchange_team(): lax.all_to_all(x.reshape(TEAM_ROWS), TEAM, split_axis=0, concat_axis=0, t...  44.8 us
    ppermute x15, waiting for transfers between devices, send(): return lax.ppermute(x, AXES, moves)  23.2 us
    ppermute x1, waiting for transfers between devices, shards(): both = jnp.transpose(lax.ppermute(both, AXES, MOVE_OUT), (1, 0, 2))  20.9 us
    all_gather x3, blocking collectives, pair(): return lax.all_gather(x, 'core', axis=0, tiled=True)  6.3 us
  transfers between devices with their start and end apart: 22, of which 10 were waited for; matrix products, arithmetic and copies ran while one was open for 0% of the time, Pallas kernels for 17%

profile of v5, /device:TPU:253, one launch (start us, length us, event | category | flops | bytes accessed | tf_op | source)
XLA Modules:
  0.0 205.2 jit_solution(9071341414944597243)
XLA Ops:
  0.6 1.9 collective-permute-start.1
  2.6 0.7 constant_dynamic-slice_fusion.refs_0_
  3.3 9.0 %collective-permute-done.1.refs_1_ = f32[3,4,1024]{2,1,0:T(4,128)S(1)} collective-permute-done((f32[3,4,1024]{2,1,0:T(4,128)}, f32[3,4,1024]{2,1,0:T(4,128)S(1)}, u32[]{:S(2)}, u32[]{:S(2)}) %collective-permute-start.1) | collective-permute-done | bytes 49184 | tf_op jit(solution)/shard_map/ppermute | solution.py:516
  12.3 1.3 shard_map.78
  13.6 7.7 %all-to-all-start = ((f32[16,24,128]{2,1,0:T(8,128)}), f32[16,24,128]{2,1,0:T(8,128)S(1)}, u32[]{:S(2)}, u32[]{:S(2)}) async-start(f32[16,24,128]{2,1,0:T(8,128)} %bitcast.5), calls=%async_computation | async-start | bytes 393216 | tf_op jit(solution)/shard_map/all_to_all | solution.py:511
  21.3 0.6 copy-done.1
  22.0 2.2 %collective-permute-start = (f32[120,128]{1,0:T(8,128)S(1)}, f32[120,128]{1,0:T(8,128)S(1)}, u32[]{:S(2)}, u32[]{:S(2)}) collective-permute-start(f32[120,128]{1,0:T(8,128)S(1)} %shard_map.77), channel_id=1, source_target_pairs={{0,2},{1,14},{2,78},{3,66},{4,130},{5,142},{6,206},{7,194},{8,258}... | collective-permute-start | bytes 184328 | tf_op jit(solution)/shard_map/ppermute | solution.py:516
  24.2 9.4 %collective-permute-done.refs_1_.refs_3_ = f32[120,128]{1,0:T(8,128)S(1)} collective-permute-done((f32[120,128]{1,0:T(8,128)S(1)}, f32[120,128]{1,0:T(8,128)S(1)}, u32[]{:S(2)}, u32[]{:S(2)}) %collective-permute-start) | collective-permute-done | bytes 61472 | tf_op jit(solution)/shard_map/ppermute | solution.py:516
  33.5 4.3 %shard_map.79.refs_4_ = f32[128,128]{1,0:T(8,128)S(1)} custom-call(f32[96,128]{1,0:T(8,128)S(1)} %get-tuple-element.47.refs_0_.refs_2_.refs_4_, f32[120,128]{1,0:T(8,128)S(1)} %collective-permute-done.refs_1_.refs_3_), custom_call_target="tpu_custom_call" | custom-call | flops 400000000 | bytes 400000 | tf_op jit(solution)/shard_map/pallas_call | solution.py:491
  37.8 0.0 all-to-all-done
  37.8 9.0 %collective-permute-start.2 = (f32[88,128]{1,0:T(8,128)S(1)}, f32[88,128]{1,0:T(8,128)S(1)}, u32[]{:S(2)}, u32[]{:S(2)}) collective-permute-start(f32[88,128]{1,0:T(8,128)S(1)} %get-tuple-element.51), channel_id=1, source_target_pairs={{2,14},{14,78},{78,66},{66,130},{130,142},{142,206},{206,194},{194... | collective-permute-start | bytes 135176 | tf_op jit(solution)/shard_map/ppermute | solution.py:516
  46.8 1.9 collective-permute-start.3
  48.8 1.2 shard_map.82.refs_2_
  50.0 0.0 collective-permute-done.2.refs_5_.refs_7_.refs_3_
  50.0 1.6 collective-permute-done.3.refs_6_.refs_8_.refs_4_
  51.6 2.4 %shard_map.83 = f32[384,128]{1,0:T(8,128)} custom-call(f32[24,128]{1,0:T(8,128)S(1)} %get-tuple-element.54.refs_0_, f32[120,128]{1,0:T(8,128)S(1)} %collective-permute-done.refs_1_.refs_3_, f32[32,128]{1,0:T(8,128)S(1)} %shard_map.82.refs_2_, f32[88,128]{1,0:T(8,128)S(1)} %collective-permute-done.2.refs_5_.refs_7_.refs_3_, ...), custom_call_target="tpu_custom_call" | custom-call | flops 100000000 | bytes 400000 | tf_op jit(solution)/shard_map/pallas_call | solution.py:491
  54.0 8.3 %all-to-all-start.1 = ((f32[16,24,128]{2,1,0:T(8,128)}), f32[16,24,128]{2,1,0:T(8,128)S(1)}, u32[]{:S(2)}, u32[]{:S(2)}) async-start(f32[16,24,128]{2,1,0:T(8,128)} %bitcast.7), calls=%async_computation.1 | async-start | bytes 393216 | tf_op jit(solution)/shard_map/all_to_all | solution.py:511
  62.3 3.1 %shard_map.81 = (f32[96,128]{1,0:T(8,128)S(1)}, f32[48,128]{1,0:T(8,128)S(1)}, f32[48,128]{1,0:T(8,128)S(1)}) custom-call(f32[1,128]{1,0:T(1,128)S(1)} %constant_dynamic-slice_fusion.refs_0_, f32[120,128]{1,0:T(8,128)S(1)} %collective-permute-done.refs_1_.refs_3_, f32[96,128]{1,0:T(8,128)S(1)} %get-tuple-element.47.refs_0_.refs_2_.refs_4_, ...), custom_call_target="tpu_custom_call" | custom-call | flops 200000000 | bytes 400000 | tf_op jit(solution)/shard_map/pallas_call | solution.py:491
  65.4 2.8 %collective-permute-start.4 = (f32[48,128]{1,0:T(8,128)S(1)}, f32[48,128]{1,0:T(8,128)S(1)}, u32[]{:S(2)}, u32[]{:S(2)}) collective-permute-start(f32[48,128]{1,0:T(8,128)S(1)} %get-tuple-element.56), channel_id=1, source_target_pairs={{2,33},{14,45},{78,109},{66,97},{130,161},{142,173},{206,237},{194... | collective-permute-start | bytes 73736 | tf_op jit(solution)/shard_map/ppermute | solution.py:516
  68.2 2.2 %all_gather.9.refs_5_ = f32[96,128]{1,0:T(8,128)S(1)} all-gather(f32[48,128]{1,0:T(8,128)S(1)} %get-tuple-element.55), channel_id=1, replica_groups=mesh['z2'=2,'z1'=2,'z0'=2,'core'=2,'zh'=2,'x1'=2,'x0'=2,'y1'=2,'y0'=2] {..., dimensions={0}, use_global_device_ids=true | all-gather | bytes 73728 | tf_op jit(solution)/shard_map/all_gather | solution.py:520
  70.4 0.2 collective-permute-done.4.refs_6_
  70.6 0.7 shard_map.84
  71.3 6.8 %collective-permute-start.5 = (f32[48,128]{1,0:T(8,128)S(1)}, f32[48,128]{1,0:T(8,128)S(1)}, u32[]{:S(2)}, u32[]{:S(2)}) collective-permute-start(f32[48,128]{1,0:T(8,128)S(1)} %get-tuple-element.59), channel_id=1, source_target_pairs={{2,14},{14,78},{78,66},{66,130},{130,142},{142,206},{206,194},{194... | collective-permute-start | bytes 73736 | tf_op jit(solution)/shard_map/ppermute | solution.py:516
  78.1 1.9 collective-permute-start.6
  80.0 4.3 %shard_map.85.refs_4_ = f32[128,128]{1,0:T(8,128)S(1)} custom-call(f32[96,128]{1,0:T(8,128)S(1)} %get-tuple-element.57.refs_0_.refs_2_, f32[120,128]{1,0:T(8,128)S(1)} %collective-permute-done.refs_1_.refs_3_), custom_call_target="tpu_custom_call" | custom-call | flops 400000000 | bytes 400000 | tf_op jit(solution)/shard_map/pallas_call | solution.py:491
  84.2 0.0 collective-permute-done.5.refs_5_
  84.3 3.9 %shard_map.86 = (f32[96,128]{1,0:T(8,128)S(1)}, f32[96,128]{1,0:T(8,128)S(1)}, f32[48,128]{1,0:T(8,128)S(1)}, f32[48,128]{1,0:T(8,128)S(1)}, f32[24,128]{1,0:T(8...) custom-call(f32[1,128]{1,0:T(1,128)S(1)} %constant_dynamic-slice_fusion.refs_0_, ...), custom_call_target="tpu_custom_call" | custom-call | flops 200000000 | bytes 400000 | tf_op jit(solution)/shard_map/pallas_call | solution.py:491
  88.1 6.4 %all-to-all-start.2 = ((f32[16,24,128]{2,1,0:T(8,128)}), f32[16,24,128]{2,1,0:T(8,128)S(1)}, u32[]{:S(2)}, u32[]{:S(2)}) async-start(f32[16,24,128]{2,1,0:T(8,128)} %bitcast.9), calls=%async_computation.2 | async-start | bytes 393216 | tf_op jit(solution)/shard_map/all_to_all | solution.py:511
  94.5 4.3 %shard_map.87.refs_4_ = f32[128,128]{1,0:T(8,128)S(1)} custom-call(f32[96,128]{1,0:T(8,128)S(1)} %get-tuple-element.63.refs_0_.refs_2_, f32[120,128]{1,0:T(8,128)S(1)} %collective-permute-done.refs_1_.refs_3_), custom_call_target="tpu_custom_call" | custom-call | flops 400000000 | bytes 400000 | tf_op jit(solution)/shard_map/pallas_call | solution.py:491
  98.8 1.1 all-to-all-done.2
  99.9 4.2 %collective-permute-start.7 = (f32[72,128]{1,0:T(8,128)S(1)}, f32[72,128]{1,0:T(8,128)S(1)}, u32[]{:S(2)}, u32[]{:S(2)}) collective-permute-start(f32[72,128]{1,0:T(8,128)S(1)} %get-tuple-element.68), channel_id=1, source_target_pairs={{2,14},{14,78},{78,66},{66,130},{130,142},{142,206},{206,194},{194... | collective-permute-start | bytes 110600 | tf_op jit(solution)/shard_map/ppermute | solution.py:516
  104.2 1.9 collective-permute-start.8
  106.1 1.2 shard_map.90.refs_2_
  107.3 0.0 collective-permute-done.7.refs_5_.refs_3_
  107.3 2.3 %collective-permute-done.8.refs_6_.refs_4_ = f32[72,128]{1,0:T(8,128)S(1)} collective-permute-done((f32[72,128]{1,0:T(8,128)S(1)}, f32[72,128]{1,0:T(8,128)S(1)}, u32[]{:S(2)}, u32[]{:S(2)}) %collective-permute-start.8) | collective-permute-done | bytes 36896 | tf_op jit(solution)/shard_map/ppermute | solution.py:516
  109.6 2.4 %shard_map.91 = f32[384,128]{1,0:T(8,128)} custom-call(f32[24,128]{1,0:T(8,128)S(1)} %get-tuple-element.71.refs_0_, f32[120,128]{1,0:T(8,128)S(1)} %collective-permute-done.refs_1_.refs_3_, f32[32,128]{1,0:T(8,128)S(1)} %shard_map.90.refs_2_, f32[72,128]{1,0:T(8,128)S(1)} %collective-permute-done.7.refs_5_.refs_3_, ...), custom_call_target="tpu_custom_call" | custom-call | flops 100000000 | bytes 400000 | tf_op jit(solution)/shard_map/pallas_call | solution.py:491
  112.0 7.7 %all-to-all-start.3 = ((f32[16,24,128]{2,1,0:T(8,128)}), f32[16,24,128]{2,1,0:T(8,128)S(1)}, u32[]{:S(2)}, u32[]{:S(2)}) async-start(f32[16,24,128]{2,1,0:T(8,128)} %bitcast.11), calls=%async_computation.3 | async-start | bytes 393216 | tf_op jit(solution)/shard_map/all_to_all | solution.py:511
  119.7 3.1 %shard_map.89 = (f32[96,128]{1,0:T(8,128)S(1)}, f32[48,128]{1,0:T(8,128)S(1)}, f32[48,128]{1,0:T(8,128)S(1)}) custom-call(f32[1,128]{1,0:T(1,128)S(1)} %constant_dynamic-slice_fusion.refs_0_, f32[120,128]{1,0:T(8,128)S(1)} %collective-permute-done.refs_1_.refs_3_, f32[96,128]{1,0:T(8,128)S(1)} %get-tuple-element.63.refs_0_.refs_2_, ...), custom_call_target="tpu_custom_call" | custom-call | flops 200000000 | bytes 400000 | tf_op jit(solution)/shard_map/pallas_call | solution.py:491
  122.8 2.8 %collective-permute-start.9 = (f32[48,128]{1,0:T(8,128)S(1)}, f32[48,128]{1,0:T(8,128)S(1)}, u32[]{:S(2)}, u32[]{:S(2)}) collective-permute-start(f32[48,128]{1,0:T(8,128)S(1)} %get-tuple-element.73), channel_id=1, source_target_pairs={{2,33},{14,45},{78,109},{66,97},{130,161},{142,173},{206,237},{194... | collective-permute-start | bytes 73736 | tf_op jit(solution)/shard_map/ppermute | solution.py:516
  125.6 2.2 %all_gather.10.refs_5_ = f32[96,128]{1,0:T(8,128)S(1)} all-gather(f32[48,128]{1,0:T(8,128)S(1)} %get-tuple-element.72), channel_id=1, replica_groups=mesh['z2'=2,'z1'=2,'z0'=2,'core'=2,'zh'=2,'x1'=2,'x0'=2,'y1'=2,'y0'=2] {..., dimensions={0}, use_global_device_ids=true | all-gather | bytes 73728 | tf_op jit(solution)/shard_map/all_gather | solution.py:520
  127.8 0.2 collective-permute-done.9.refs_6_
  128.0 0.7 shard_map.92
  128.6 4.7 %collective-permute-start.10 = (f32[48,128]{1,0:T(8,128)S(1)}, f32[48,128]{1,0:T(8,128)S(1)}, u32[]{:S(2)}, u32[]{:S(2)}) collective-permute-start(f32[48,128]{1,0:T(8,128)S(1)} %get-tuple-element.76), channel_id=1, source_target_pairs={{2,14},{14,78},{78,66},{66,130},{130,142},{142,206},{206,194},{194... | collective-permute-start | bytes 73736 | tf_op jit(solution)/shard_map/ppermute | solution.py:516
  133.4 1.9 collective-permute-start.11
  135.3 4.3 %shard_map.93.refs_4_ = f32[128,128]{1,0:T(8,128)S(1)} custom-call(f32[96,128]{1,0:T(8,128)S(1)} %get-tuple-element.74.refs_0_.refs_2_, f32[120,128]{1,0:T(8,128)S(1)} %collective-permute-done.refs_1_.refs_3_), custom_call_target="tpu_custom_call" | custom-call | flops 400000000 | bytes 400000 | tf_op jit(solution)/shard_map/pallas_call | solution.py:491
  139.6 0.0 collective-permute-done.10.refs_5_
  139.6 3.9 %shard_map.94 = (f32[96,128]{1,0:T(8,128)S(1)}, f32[96,128]{1,0:T(8,128)S(1)}, f32[48,128]{1,0:T(8,128)S(1)}, f32[48,128]{1,0:T(8,128)S(1)}, f32[24,128]{1,0:T(8...) custom-call(f32[1,128]{1,0:T(1,128)S(1)} %constant_dynamic-slice_fusion.refs_0_, ...), custom_call_target="tpu_custom_call" | custom-call | flops 200000000 | bytes 400000 | tf_op jit(solution)/shard_map/pallas_call | solution.py:491
  143.4 6.3 %all-to-all-start.4 = ((f32[16,24,128]{2,1,0:T(8,128)}), f32[16,24,128]{2,1,0:T(8,128)S(1)}, u32[]{:S(2)}, u32[]{:S(2)}) async-start(f32[16,24,128]{2,1,0:T(8,128)} %bitcast.13), calls=%async_computation.4 | async-start | bytes 393216 | tf_op jit(solution)/shard_map/all_to_all | solution.py:511
  149.8 4.3 %shard_map.95.refs_4_ = f32[128,128]{1,0:T(8,128)S(1)} custom-call(f32[96,128]{1,0:T(8,128)S(1)} %get-tuple-element.80.refs_0_.refs_2_.refs_3_, f32[120,128]{1,0:T(8,128)S(1)} %collective-permute-done.refs_1_.refs_3_), custom_call_target="tpu_custom_call" | custom-call | flops 400000000 | bytes 400000 | tf_op jit(solution)/shard_map/pallas_call | solution.py:491
  154.0 1.1 all-to-all-done.4
  155.2 2.6 %collective-permute-start.12 = (f32[72,128]{1,0:T(8,128)S(1)}, f32[72,128]{1,0:T(8,128)S(1)}, u32[]{:S(2)}, u32[]{:S(2)}) collective-permute-start(f32[72,128]{1,0:T(8,128)S(1)} %get-tuple-element.85), channel_id=1, source_target_pairs={{2,14},{14,78},{78,66},{66,130},{130,142},{142,206},{206,194},{194... | collective-permute-start | bytes 110600 | tf_op jit(solution)/shard_map/ppermute | solution.py:516
  157.8 2.9 %collective-permute-start.13 = (f32[72,128]{1,0:T(8,128)S(1)}, f32[72,128]{1,0:T(8,128)S(1)}, u32[]{:S(2)}, u32[]{:S(2)}) collective-permute-start(f32[72,128]{1,0:T(8,128)S(1)} %get-tuple-element.86), channel_id=1, source_target_pairs={{2,466},{14,2},{78,14},{66,78},{130,66},{142,130},{206,142},{194,2... | collective-permute-start | bytes 110600 | tf_op jit(solution)/shard_map/ppermute | solution.py:516
  160.7 1.2 shard_map.98.refs_2_
  161.9 0.0 collective-permute-done.12.refs_5_.refs_3_
  161.9 0.6 collective-permute-done.13.refs_6_.refs_4_
  162.5 2.4 %shard_map.99 = (f32[384,128]{1,0:T(8,128)}, f32[24,128]{1,0:T(8,128)S(1)}) custom-call(f32[24,128]{1,0:T(8,128)S(1)} %get-tuple-element.87.refs_0_, f32[120,128]{1,0:T(8,128)S(1)} %collective-permute-done.refs_1_.refs_3_, f32[32,128]{1,0:T(8,128)S(1)} %shard_map.98.refs_2_, ...), custom_call_target="tpu_custom_call", output_to_operand_aliasing={{1}: (7, {})} | custom-call | flops 100000000 | bytes 400000 | tf_op jit(solution)/shard_map/pallas_call | solution.py:491
  164.9 8.4 %all-to-all-start.5 = ((f32[16,24,128]{2,1,0:T(8,128)}), f32[16,24,128]{2,1,0:T(8,128)S(1)}, u32[]{:S(2)}, u32[]{:S(2)}) async-start(f32[16,24,128]{2,1,0:T(8,128)} %bitcast.15), calls=%async_computation.5 | async-start | bytes 393216 | tf_op jit(solution)/shard_map/all_to_all | solution.py:511
  173.3 1.9 all_gather.11.refs_6_
  175.2 2.7 %collective-permute-start.14 = (f32[24,128]{1,0:T(8,128)S(1)}, f32[24,128]{1,0:T(8,128)S(1)}, u32[]{:S(2)}, u32[]{:S(2)}) collective-permute-start(f32[24,128]{1,0:T(8,128)S(1)} %get-tuple-element.91), channel_id=1, source_target_pairs={{2,33},{14,45},{78,109},{66,97},{130,161},{142,173},{206,237},{194... | collective-permute-start | bytes 36872 | tf_op jit(solution)/shard_map/ppermute | solution.py:516
  177.9 3.1 %shard_map.97.refs_2_ = f32[96,128]{1,0:T(8,128)S(1)} custom-call(f32[1,128]{1,0:T(1,128)S(1)} %constant_dynamic-slice_fusion.refs_0_, f32[120,128]{1,0:T(8,128)S(1)} %collective-permute-done.refs_1_.refs_3_, f32[96,128]{1,0:T(8,128)S(1)} %get-tuple-element.80.refs_0_.refs_2_.refs_3_, f32[96,128]{1,0:T(8,128)S(1)} %get-tuple-element.81.refs_3_, ...), custom_call_target="tpu_custom_call" | custom-call | flops 200000000 | bytes 400000 | tf_op jit(solution)/shard_map/pallas_call | solution.py:491
  181.0 0.6 shard_map.100
  181.7 1.9 collective-permute-start.15
  183.6 20.9 %collective-permute-done.15 = f32[6,4,1024]{2,1,0:T(4,128)S(1)} collective-permute-done((f32[6,4,1024]{2,1,0:T(4,128)S(1)}, f32[6,4,1024]{2,1,0:T(4,128)S(1)}, u32[]{:S(2)}, u32[]{:S(2)}) %collective-permute-start.15) | collective-permute-done | bytes 98336 | tf_op jit(solution)/shard_map/ppermute | solution.py:619
  204.5 0.6 fusion
  (17 shorter events, 0.1 us)
Async XLA Ops:
  0.6 11.7 %collective-permute-start.1 = (f32[3,4,1024]{2,1,0:T(4,128)}, f32[3,4,1024]{2,1,0:T(4,128)S(1)}, u32[]{:S(2)}, u32[]{:S(2)}) collective-permute-start(f32[3,4,1024]{2,1,0:T(4,128)} %bitcast.29), channel_id=1, source_target_pairs={{0,2},{1,14},{2,78},{3,66},{4,130},{5,142},{6,206},{7,194},{8,258}... | collective-permute-start | bytes 147464 | tf_op jit(solution)/shard_map/ppermute | solution.py:516
  13.6 7.7 %copy-start = (f32[4,3,1024]{2,0,1:T(4,128)S(1)}, f32[4,3,1024]{2,0,1:T(4,128)}, u32[]{:S(2)}) copy-start(f32[4,3,1024]{2,0,1:T(4,128)} %param.7) | copy-start | bytes 147460
  13.6 7.7 %copy-start.2 = (f32[1024]{0:T(1024)S(1)}, f32[1024]{0:T(1024)}, u32[]{:S(2)}) copy-start(f32[1024]{0:T(1024)} %param.9) | copy-start | bytes 12292
  13.6 7.7 %copy-start.3 = (f32[1024]{0:T(1024)S(1)}, f32[1024]{0:T(1024)}, u32[]{:S(2)}) copy-start(f32[1024]{0:T(1024)} %param.10) | copy-start | bytes 12292
  13.6 24.2 %all-to-all-start = ((f32[16,24,128]{2,1,0:T(8,128)}), f32[16,24,128]{2,1,0:T(8,128)S(1)}, u32[]{:S(2)}, u32[]{:S(2)}) async-start(f32[16,24,128]{2,1,0:T(8,128)} %bitcast.5), calls=%async_computation | async-start | bytes 393216 | tf_op jit(solution)/shard_map/all_to_all | solution.py:511
  21.3 0.7 copy-start.1
  22.0 11.6 %collective-permute-start = (f32[120,128]{1,0:T(8,128)S(1)}, f32[120,128]{1,0:T(8,128)S(1)}, u32[]{:S(2)}, u32[]{:S(2)}) collective-permute-start(f32[120,128]{1,0:T(8,128)S(1)} %shard_map.77), channel_id=1, source_target_pairs={{0,2},{1,14},{2,78},{3,66},{4,130},{5,142},{6,206},{7,194},{8,258}... | collective-permute-start | bytes 184328 | tf_op jit(solution)/shard_map/ppermute | solution.py:516
  37.8 12.2 %collective-permute-start.2 = (f32[88,128]{1,0:T(8,128)S(1)}, f32[88,128]{1,0:T(8,128)S(1)}, u32[]{:S(2)}, u32[]{:S(2)}) collective-permute-start(f32[88,128]{1,0:T(8,128)S(1)} %get-tuple-element.51), channel_id=1, source_target_pairs={{2,14},{14,78},{78,66},{66,130},{130,142},{142,206},{206,194},{194... | collective-permute-start | bytes 135176 | tf_op jit(solution)/shard_map/ppermute | solution.py:516
  46.8 4.8 %collective-permute-start.3 = (f32[88,128]{1,0:T(8,128)S(1)}, f32[88,128]{1,0:T(8,128)S(1)}, u32[]{:S(2)}, u32[]{:S(2)}) collective-permute-start(f32[88,128]{1,0:T(8,128)S(1)} %get-tuple-element.52), channel_id=1, source_target_pairs={{2,466},{14,2},{78,14},{66,78},{130,66},{142,130},{206,142},{194,2... | collective-permute-start | bytes 135176 | tf_op jit(solution)/shard_map/ppermute | solution.py:516
  54.0 16.6 %all-to-all-start.1 = ((f32[16,24,128]{2,1,0:T(8,128)}), f32[16,24,128]{2,1,0:T(8,128)S(1)}, u32[]{:S(2)}, u32[]{:S(2)}) async-start(f32[16,24,128]{2,1,0:T(8,128)} %bitcast.7), calls=%async_computation.1 | async-start | bytes 393216 | tf_op jit(solution)/shard_map/all_to_all | solution.py:511
  65.4 5.1 %collective-permute-start.4 = (f32[48,128]{1,0:T(8,128)S(1)}, f32[48,128]{1,0:T(8,128)S(1)}, u32[]{:S(2)}, u32[]{:S(2)}) collective-permute-start(f32[48,128]{1,0:T(8,128)S(1)} %get-tuple-element.56), channel_id=1, source_target_pairs={{2,33},{14,45},{78,109},{66,97},{130,161},{142,173},{206,237},{194... | collective-permute-start | bytes 73736 | tf_op jit(solution)/shard_map/ppermute | solution.py:516
  71.3 13.0 %collective-permute-start.5 = (f32[48,128]{1,0:T(8,128)S(1)}, f32[48,128]{1,0:T(8,128)S(1)}, u32[]{:S(2)}, u32[]{:S(2)}) collective-permute-start(f32[48,128]{1,0:T(8,128)S(1)} %get-tuple-element.59), channel_id=1, source_target_pairs={{2,14},{14,78},{78,66},{66,130},{130,142},{142,206},{206,194},{194... | collective-permute-start | bytes 73736 | tf_op jit(solution)/shard_map/ppermute | solution.py:516
  78.1 6.2 %collective-permute-start.6 = (f32[48,128]{1,0:T(8,128)S(1)}, f32[48,128]{1,0:T(8,128)S(1)}, u32[]{:S(2)}, u32[]{:S(2)}) collective-permute-start(f32[48,128]{1,0:T(8,128)S(1)} %get-tuple-element.60), channel_id=1, source_target_pairs={{2,466},{14,2},{78,14},{66,78},{130,66},{142,130},{206,142},{194,2... | collective-permute-start | bytes 73736 | tf_op jit(solution)/shard_map/ppermute | solution.py:516
  88.1 11.8 %all-to-all-start.2 = ((f32[16,24,128]{2,1,0:T(8,128)}), f32[16,24,128]{2,1,0:T(8,128)S(1)}, u32[]{:S(2)}, u32[]{:S(2)}) async-start(f32[16,24,128]{2,1,0:T(8,128)} %bitcast.9), calls=%async_computation.2 | async-start | bytes 393216 | tf_op jit(solution)/shard_map/all_to_all | solution.py:511
  99.9 7.4 %collective-permute-start.7 = (f32[72,128]{1,0:T(8,128)S(1)}, f32[72,128]{1,0:T(8,128)S(1)}, u32[]{:S(2)}, u32[]{:S(2)}) collective-permute-start(f32[72,128]{1,0:T(8,128)S(1)} %get-tuple-element.68), channel_id=1, source_target_pairs={{2,14},{14,78},{78,66},{66,130},{130,142},{142,206},{206,194},{194... | collective-permute-start | bytes 110600 | tf_op jit(solution)/shard_map/ppermute | solution.py:516
  104.2 5.5 %collective-permute-start.8 = (f32[72,128]{1,0:T(8,128)S(1)}, f32[72,128]{1,0:T(8,128)S(1)}, u32[]{:S(2)}, u32[]{:S(2)}) collective-permute-start(f32[72,128]{1,0:T(8,128)S(1)} %get-tuple-element.69), channel_id=1, source_target_pairs={{2,466},{14,2},{78,14},{66,78},{130,66},{142,130},{206,142},{194,2... | collective-permute-start | bytes 110600 | tf_op jit(solution)/shard_map/ppermute | solution.py:516
  112.0 15.9 %all-to-all-start.3 = ((f32[16,24,128]{2,1,0:T(8,128)}), f32[16,24,128]{2,1,0:T(8,128)S(1)}, u32[]{:S(2)}, u32[]{:S(2)}) async-start(f32[16,24,128]{2,1,0:T(8,128)} %bitcast.11), calls=%async_computation.3 | async-start | bytes 393216 | tf_op jit(solution)/shard_map/all_to_all | solution.py:511
  122.8 5.1 %collective-permute-start.9 = (f32[48,128]{1,0:T(8,128)S(1)}, f32[48,128]{1,0:T(8,128)S(1)}, u32[]{:S(2)}, u32[]{:S(2)}) collective-permute-start(f32[48,128]{1,0:T(8,128)S(1)} %get-tuple-element.73), channel_id=1, source_target_pairs={{2,33},{14,45},{78,109},{66,97},{130,161},{142,173},{206,237},{194... | collective-permute-start | bytes 73736 | tf_op jit(solution)/shard_map/ppermute | solution.py:516
  128.6 10.9 %collective-permute-start.10 = (f32[48,128]{1,0:T(8,128)S(1)}, f32[48,128]{1,0:T(8,128)S(1)}, u32[]{:S(2)}, u32[]{:S(2)}) collective-permute-start(f32[48,128]{1,0:T(8,128)S(1)} %get-tuple-element.76), channel_id=1, source_target_pairs={{2,14},{14,78},{78,66},{66,130},{130,142},{142,206},{206,194},{194... | collective-permute-start | bytes 73736 | tf_op jit(solution)/shard_map/ppermute | solution.py:516
  133.4 6.2 %collective-permute-start.11 = (f32[48,128]{1,0:T(8,128)S(1)}, f32[48,128]{1,0:T(8,128)S(1)}, u32[]{:S(2)}, u32[]{:S(2)}) collective-permute-start(f32[48,128]{1,0:T(8,128)S(1)} %get-tuple-element.77), channel_id=1, source_target_pairs={{2,466},{14,2},{78,14},{66,78},{130,66},{142,130},{206,142},{194,2... | collective-permute-start | bytes 73736 | tf_op jit(solution)/shard_map/ppermute | solution.py:516
  143.4 11.7 %all-to-all-start.4 = ((f32[16,24,128]{2,1,0:T(8,128)}), f32[16,24,128]{2,1,0:T(8,128)S(1)}, u32[]{:S(2)}, u32[]{:S(2)}) async-start(f32[16,24,128]{2,1,0:T(8,128)} %bitcast.13), calls=%async_computation.4 | async-start | bytes 393216 | tf_op jit(solution)/shard_map/all_to_all | solution.py:511
  155.2 6.8 %collective-permute-start.12 = (f32[72,128]{1,0:T(8,128)S(1)}, f32[72,128]{1,0:T(8,128)S(1)}, u32[]{:S(2)}, u32[]{:S(2)}) collective-permute-start(f32[72,128]{1,0:T(8,128)S(1)} %get-tuple-element.85), channel_id=1, source_target_pairs={{2,14},{14,78},{78,66},{66,130},{130,142},{142,206},{206,194},{194... | collective-permute-start | bytes 110600 | tf_op jit(solution)/shard_map/ppermute | solution.py:516
  157.8 4.7 %collective-permute-start.13 = (f32[72,128]{1,0:T(8,128)S(1)}, f32[72,128]{1,0:T(8,128)S(1)}, u32[]{:S(2)}, u32[]{:S(2)}) collective-permute-start(f32[72,128]{1,0:T(8,128)S(1)} %get-tuple-element.86), channel_id=1, source_target_pairs={{2,466},{14,2},{78,14},{66,78},{130,66},{142,130},{206,142},{194,2... | collective-permute-start | bytes 110600 | tf_op jit(solution)/shard_map/ppermute | solution.py:516
  164.9 16.1 %all-to-all-start.5 = ((f32[16,24,128]{2,1,0:T(8,128)}), f32[16,24,128]{2,1,0:T(8,128)S(1)}, u32[]{:S(2)}, u32[]{:S(2)}) async-start(f32[16,24,128]{2,1,0:T(8,128)} %bitcast.15), calls=%async_computation.5 | async-start | bytes 393216 | tf_op jit(solution)/shard_map/all_to_all | solution.py:511
  175.2 5.8 %collective-permute-start.14 = (f32[24,128]{1,0:T(8,128)S(1)}, f32[24,128]{1,0:T(8,128)S(1)}, u32[]{:S(2)}, u32[]{:S(2)}) collective-permute-start(f32[24,128]{1,0:T(8,128)S(1)} %get-tuple-element.91), channel_id=1, source_target_pairs={{2,33},{14,45},{78,109},{66,97},{130,161},{142,173},{206,237},{194... | collective-permute-start | bytes 36872 | tf_op jit(solution)/shard_map/ppermute | solution.py:516
  181.7 22.8 %collective-permute-start.15 = (f32[6,4,1024]{2,1,0:T(4,128)S(1)}, f32[6,4,1024]{2,1,0:T(4,128)S(1)}, u32[]{:S(2)}, u32[]{:S(2)}) collective-permute-start(f32[6,4,1024]{2,1,0:T(4,128)S(1)} %shard_map.100), channel_id=1, source_target_pairs={{2,0},{14,1},{78,2},{66,3},{130,4},{142,5},{206,6},{194,7},{258,8}... | collective-permute-start | bytes 294920 | tf_op jit(solution)/shard_map/ppermute | solution.py:619
